TPU v7x, 256 devices: a 8x8x2 block of a 8x8x16 slice. The times are simulated.
256 devices in a mesh: grp: 2 (over z), ma: 128 (over x, y, core).
Axes of the slice: x: 8, y: 8, z: 2, core: 2. Of those that a mesh axis runs over, the one named last changes fastest.
The devices are a block of a 8x8x16 slice.
Arguments:
- tbar_alm: bfloat16 [1024, 8, 2, 2049], P('ma', 'grp'), parts along dimension 1, may hold values from -6 to 6
- twf_alm: bfloat16 [1024, 8, 2, 2049], P('ma', 'grp'), parts along dimension 1, may hold values from -6 to 6
- legendre: bfloat16 [1024, 2049, 128], P('ma'), may hold values from -0.125 to 0.125
- m_slots: int32 [1024], replicated, may hold values from 0 to 1023, each once
- cycle_order: int32 [128], replicated, may hold values from 0 to 127, each once
- colatitude: float32 [128], replicated, may hold values from 0.35 to 2.79
- cycle_weight: float32 [128], replicated, may hold values from 0.25 to 1
- pixel_mask: int32 [128, 4096], P('ma'), may hold values from 0 to 3
Outputs:
- gradient: float32 [1024, 8, 2, 2049], P('ma', 'grp'), parts along dimension 1
- curl: float32 [1024, 8, 2, 2049], P('ma', 'grp'), parts along dimension 1
There are 2 independent parts, one for each index of `grp`. A program takes and returns all parts, laid end to end along the dimension named above; an argument that names none is the same for every part. Nothing has to cross between parts.
Inputs may be any that keep to these rules, and one draw needn't show every extreme that they name: Pair p holds the orders m_slots[p] and 2047 - m_slots[p]; each value appears once. Cycle slot i holds cycle cycle_order[i]; each value appears once.
All inputs are finite; a program needn't handle non-finite values.
Results may differ from a plain program's by a relative error of at most 0.017.
Values may be sent and summed in bfloat16 or wider, within the bound.
No kernel may reach another device: no remote copies, remote signals or barrier semaphores. Data moves between devices by JAX's collectives and lax.ppermute only.
A program may use at most 128 MiB of HBM per device.

v0:
```python
import math

import jax
import jax.numpy as jnp
from jax import lax
from jax.sharding import Mesh
from jax.sharding import PartitionSpec as P

MA = ("ma_0", "ma_1", "ma_2")


def cut_along(value, dim, length):
    before, after = (value.shape[:dim], value.shape[dim + 1 :])
    return jnp.moveaxis(value.reshape(*before, length, -1, *after), dim, 0)


def laid_out(pieces, dim):
    shape = list(pieces.shape[1:])
    shape[dim] *= pieces.shape[0]
    return jnp.moveaxis(pieces, 0, dim).reshape(shape)


def turned_blocks(pieces, axes, turns):
    inside = pieces.shape[1:]
    filled = pieces.reshape(*(lax.axis_size(a) for a in axes), *inside)
    for k in turns:
        filled = lax.all_to_all(filled, axes[k], k, k, tiled=True)
    return filled.reshape(-1, *inside)


def two_step_exchange(value, groups, turns, split_dim, concat_dim):
    length = lax.axis_size(groups[0]) * lax.axis_size(groups[1])
    pieces = cut_along(value, split_dim, length)
    return laid_out(turned_blocks(pieces, groups, turns), concat_dim)


def pair_layout(small_orders, mode_count):
    row_index = lax.broadcasted_iota(jnp.int32, (small_orders.shape[0], mode_count + 1), 1)
    smaller = small_orders[:, None]
    upper_half = row_index >= mode_count - smaller
    degree = jnp.where(upper_half, row_index - 1, smaller + row_index)
    orders = jnp.where(upper_half, mode_count - 1 - smaller, smaller + 0 * row_index)
    return (upper_half, degree.astype(jnp.float32), orders.astype(jnp.float32))


def raising(degree, orders):
    square = (
        (degree * degree - orders * orders)
        * (2.0 * degree + 1.0)
        / jnp.maximum(2.0 * degree - 1.0, 1.0)
    )
    return jnp.where(degree > orders, jnp.sqrt(jnp.where(degree > orders, square, 0.0)), 0.0)


def synthesis_sets(tbar_alm, twf_alm, degree, raising_factor, mode_count):
    wiener = twf_alm.astype(jnp.float32)
    scaled = (raising_factor / mode_count)[:, None, None, :] * wiener
    raised = jnp.concatenate([scaled[..., 1:], jnp.zeros_like(scaled[..., :1])], axis=-1)
    stacked = jnp.stack(
        [
            tbar_alm.astype(jnp.float32),
            wiener,
            (degree / mode_count)[:, None, None, :] * wiener,
            raised,
        ],
        axis=2,
    )
    return stacked.reshape(stacked.shape[0], stacked.shape[1], 8, stacked.shape[4]).astype(
        jnp.bfloat16
    )


def mode_columns(small_orders, mode_count):
    return jnp.stack([small_orders, mode_count - 1 - small_orders], axis=1).reshape(-1)


def fourier_table(orders_int, pixel_count):
    pixel_index = lax.broadcasted_iota(jnp.int32, (orders_int.shape[0], pixel_count), 1)
    turns = orders_int[:, None] * pixel_index % pixel_count
    radians = turns.astype(jnp.float32) * (2.0 * math.pi / pixel_count)
    return jnp.stack([jnp.cos(radians), -jnp.sin(radians)], axis=0).astype(jnp.bfloat16)


def combine_modes(legendre_sums, orders_int, cos_cycle, sin_cycle, mode_count):
    orders_real = orders_int.astype(jnp.float32)
    inv_sin = 1.0 / sin_cycle
    ratio = (orders_real / mode_count)[:, None]
    theta_real = (cos_cycle * legendre_sums[:, 4] - legendre_sums[:, 6]) * inv_sin
    theta_imag = (cos_cycle * legendre_sums[:, 5] - legendre_sums[:, 7]) * inv_sin
    phi_real = -ratio * legendre_sums[:, 3] * inv_sin
    phi_imag = ratio * legendre_sums[:, 2] * inv_sin
    weight = (jnp.where(orders_int == 0, 1.0, 2.0) * mode_count ** (-0.5))[:, None]
    stacked = jnp.stack(
        [legendre_sums[:, 0], legendre_sums[:, 1], theta_real, theta_imag, phi_real, phi_imag],
        axis=1,
    )
    return (stacked * weight).astype(jnp.bfloat16)


def analysis_sets(spectra, colatitude, cycle_weight):
    with_cos = cycle_weight * jnp.cos(colatitude) / jnp.sin(colatitude)
    with_sin = cycle_weight / jnp.sin(colatitude)
    stacked = jnp.stack(
        [
            spectra[:, 0] * with_cos,
            spectra[:, 0] * with_sin,
            spectra[:, 1] * with_cos,
            spectra[:, 1] * with_sin,
        ],
        axis=1,
    )
    return stacked.reshape(spectra.shape[0], 8, spectra.shape[3], spectra.shape[4]).astype(
        jnp.bfloat16
    )


def estimate(merged, degree, orders, raising_factor, mode_count, cycle_count):
    level = degree[:, None, :]
    azimuth = orders[:, None, :]
    factor = raising_factor[:, None, :]

    def previous(values):
        return jnp.concatenate([jnp.zeros_like(values[..., :1]), values[..., :-1]], axis=-1)

    grad_real = (
        level * merged[:, :, 0] - factor * previous(merged[:, :, 2]) + azimuth * merged[:, :, 7]
    )
    grad_imag = (
        level * merged[:, :, 1] - factor * previous(merged[:, :, 3]) - azimuth * merged[:, :, 6]
    )
    curl_real = (
        level * merged[:, :, 4] - factor * previous(merged[:, :, 6]) - azimuth * merged[:, :, 3]
    )
    curl_imag = (
        level * merged[:, :, 5] - factor * previous(merged[:, :, 7]) + azimuth * merged[:, :, 2]
    )
    scale = (mode_count / cycle_count) ** 0.5 / jnp.sqrt(jnp.maximum(level * (level + 1.0), 1.0))
    scale = scale[:, :, None, :]
    return (
        jnp.stack([grad_real, grad_imag], axis=2) * scale,
        jnp.stack([curl_real, curl_imag], axis=2) * scale,
    )


def shards(tbar_alm, twf_alm, legendre, m_slots, cycle_order, colatitude, cycle_weight, pixel_mask):
    pairs_dev = tbar_alm.shape[0]
    row_count = tbar_alm.shape[3]
    mode_count = row_count - 1
    cycle_count = legendre.shape[2]
    cycle_dev = pixel_mask.shape[0]
    pixel_count = pixel_mask.shape[1]
    device_slot = lax.axis_index(MA)
    local_small = lax.dynamic_slice_in_dim(m_slots, device_slot * pairs_dev, pairs_dev)
    upper_half, degree, orders = pair_layout(local_small, mode_count)
    raising_factor = raising(degree, orders)
    coeff_sets = synthesis_sets(tbar_alm, twf_alm, degree, raising_factor, mode_count)
    halves = jnp.stack([jnp.logical_not(upper_half), upper_half], axis=1)
    masked = coeff_sets[:, None] * halves.astype(jnp.bfloat16)[:, :, None, None, :]
    legendre_sums = jnp.einsum(
        "phsck,pkr->scphr", masked, legendre, preferred_element_type=jnp.float32
    )
    legendre_sums = jnp.take(legendre_sums, cycle_order, axis=4)
    legendre_sums = legendre_sums.reshape(legendre_sums.shape[0], 8, 2 * pairs_dev, cycle_count)
    all_orders = mode_columns(m_slots, mode_count)
    dft_table = fourier_table(all_orders, pixel_count)
    pixel_weights = pixel_mask.astype(jnp.float32)
    slot_theta = jnp.take(colatitude, cycle_order)
    local_orders = mode_columns(local_small, mode_count)
    outgoing = combine_modes(
        legendre_sums, local_orders, jnp.cos(slot_theta), jnp.sin(slot_theta), mode_count
    )
    fourier = lax.all_to_all(outgoing, MA, split_axis=3, concat_axis=2, tiled=True)
    fourier = fourier.reshape(fourier.shape[0], 3, 2, mode_count, cycle_dev)
    cycle_maps = jnp.einsum(
        "sqemr,emj->sqrj", fourier, dft_table, preferred_element_type=jnp.float32
    )
    products = (pixel_weights * cycle_maps[:, 0:1] * cycle_maps[:, 1:3]).astype(jnp.bfloat16)
    spectra = jnp.einsum("sqrj,emj->sqemr", products, dft_table, preferred_element_type=jnp.float32)
    received = (spectra * pixel_count ** (-0.5)).astype(jnp.bfloat16)
    returned = two_step_exchange(received, (("ma_0", "ma_1"), "ma_2"), (1, 0), 3, 4)
    inverse = (
        jnp.zeros((cycle_count,), jnp.int32).at[cycle_order].set(lax.iota(jnp.int32, cycle_count))
    )
    spectra = jnp.take(returned, inverse, axis=4).astype(jnp.float32)
    weighted = analysis_sets(spectra, colatitude, cycle_weight)
    weighted = weighted.reshape(weighted.shape[0], 8, pairs_dev, 2, cycle_count)
    projected = jnp.einsum(
        "scphr,pkr->phsck", weighted, legendre, preferred_element_type=jnp.float32
    )
    merged = jnp.sum(projected * halves.astype(jnp.float32)[:, :, None, None, :], axis=1)
    return estimate(merged, degree, orders, raising_factor, mode_count, cycle_count)


def solution(mesh):
    finer = Mesh(mesh.devices.reshape(mesh.shape["grp"], 8, 8, 2), ("grp", "ma_0", "ma_1", "ma_2"))
    in_specs = (
        P(MA, "grp", None, None),
        P(MA, "grp", None, None),
        P(MA, None, None),
        P(),
        P(),
        P(),
        P(),
        P(MA, None),
    )
    out_specs = (P(MA, "grp", None, None), P(MA, "grp", None, None))
    return jax.shard_map(
        shards, mesh=finer, in_specs=in_specs, out_specs=out_specs, check_vma=False
    )
```

profile of v0, /device:TPU:513, one launch (start us, length us, event | category | flops | bytes accessed | tf_op | source)
XLA Modules:
  0.0 266.2 jit_solution(7905125816305541250)
XLA Ops:
  0.7 0.8 fusion.79
  1.5 0.2 fusion.80
  1.7 0.2 sqrt_select_fusion
  1.9 1.0 copy_bitcast_fusion.8
  2.9 1.0 fusion.37
  4.0 0.2 fusion.36
  4.2 1.0 copy_bitcast_fusion.7
  5.2 0.2 pad_maximum_fusion.3
  5.3 0.1 copy.134
  5.5 0.2 fusion.82
  5.7 3.6 %fusion.29 = f32[4,8,8,2,128]{4,1,0,3,2:T(8,128)S(1)} fusion(bf16[8,2049,128,1,1]{2,0,1,4,3:T(8,128)(2,1)} %bitcast.149, bf16[8,2,2049]{2,1,0:T(2,128)(2,1)S(1)} %get-tuple-element.30, bf16[8,4,8,2049]{3,2,1,0:T(8,128)(2,1)S(1)} %copy.134), kind=kOutput, calls=%fused_computation.30 | convolution fusion | flops 269615616 | bytes 5573152 | tf_op jit(solution)/shard_map/phsck,pkr->scphr/dot_general | solution.py:159
  9.3 2.6 copy.136
  11.9 1.0 scatter_custom_fusion
  12.9 5.3 %gather_fusion = f32[128,4,8,8,2]{3,2,4,1,0:T(8,128)} fusion(f32[4,8,8,2,128]{2,1,4,3,0:T(8,128)} %copy.136, s32[1024]{0:T(1024)S(1)} %get-tuple-element.59), kind=kCustom, calls=%fused_computation | custom fusion | bytes 524800 | tf_op jit(solution)/shard_map/jit(_take)/gather | solution.py:162
  18.2 3.8 %copy.137 = f32[4,8,8,2,128]{4,1,3,2,0:T(8,128)S(1)} copy(f32[4,8,8,2,128]{2,1,3,0,4:T(8,128)} %bitcast.147) | data formatting | bytes 524288 | tf_op jit(solution)/shard_map/jit(_take)/gather | solution.py:162
  22.0 1.2 gather_fusion.1
  24.0 0.1 multiply_convert_fusion.1
  24.1 0.6 copy.141
  24.7 1.4 reshape.640
  26.1 27.5 %all-to-all-start = ((bf16[128,2,192]{2,1,0:T(2,128)(2,1)}), bf16[128,2,192]{2,1,0:T(2,128)(2,1)S(1)}, u32[]{:S(2)}, u32[]{:S(2)}) async-start(bf16[128,2,192]{2,1,0:T(2,128)(2,1)} %reshape.640), calls=%async_computation | async-start | bytes 262144 | tf_op jit(solution)/shard_map/all_to_all | solution.py:172
  53.7 0.2 copy.129
  53.9 0.3 mul.380
  54.2 139.1 %cosine_convert_fusion = (bf16[1,2048,4096]{2,1,0:T(8,128)(2,1)}, bf16[1,2048,4096]{2,1,0:T(8,128)(2,1)}) fusion(s32[2048]{0:T(1024)S(1)} %mul.380), kind=kLoop, calls=%fused_computation.16 | loop fusion | flops 142606336 | bytes 33562624 | tf_op jit(solution)/shard_map/convert.15
  193.4 0.6 reshape.641
  194.0 0.3 bitcast_bitcast_fusion
  194.2 0.2 copy.168
  194.4 0.8 reshape.637
  195.2 12.5 %fusion.10 = f32[4,3,1,4096]{3,0,1,2:T(4,128)S(1)} fusion(bf16[4,3,2,2048]{3,0,2,1:T(4,128)(2,1)S(1)} %reshape.637, bf16[1,2048,4096]{2,1,0:T(8,128)(2,1)} %get-tuple-element.45, bf16[1,2048,4096]{2,1,0:T(8,128)(2,1)} %get-tuple-element.44), kind=kOutput, calls=%fused_computation.21 | convolution fusion | flops 419430400 | bytes 33849344 | tf_op jit(solution)/shard_map/sqemr,emj->sqrj/dot_general | solution.py:174
  207.7 14.1 %fusion.23 = bf16[4,2,2,2048,1]{3,0,1,2,4:T(4,128)(2,1)S(1)} fusion(bf16[1,2048,4096]{2,1,0:T(8,128)(2,1)} %get-tuple-element.45, bf16[1,2048,4096]{2,1,0:T(8,128)(2,1)} %get-tuple-element.44, f32[4,3,1,4096]{3,0,1,2:T(4,128)S(1)} %fusion.10, f32[4,4096]{1,0:T(4,128)S(1)} %fusion.63), kind=kOutput, calls=%fused_computation.28 | convolution fusion | flops 335675392 | bytes 33816576 | tf_op jit(solution)/shard_map/sqrj,emj->sqemr/dot_general | solution.py:178
  222.0 0.4 reshape.592
  222.3 0.4 copy.145
  222.7 0.2 reshape.642
  222.9 6.5 %all_to_all.25 = bf16[2,2,8192]{2,1,0:T(2,128)(2,1)S(1)} all-to-all(bf16[2,2,8192]{2,1,0:T(2,128)(2,1)S(1)} %reshape.642), channel_id=1, replica_groups=mesh['grp'=2,'ma_0'=8,'ma_1'=8,'ma_2'=2] {'ma_2'}, dimensions={0} | all-to-all | bytes 131072 | tf_op jit(solution)/shard_map/all_to_all | solution.py:27
  229.4 0.1 reshape.643
  229.6 0.8 copy.146
  230.4 1.1 reshape.644
  231.4 12.9 %all-to-all-start.2 = ((bf16[64,2,256]{2,1,0:T(2,128)(2,1)}), bf16[64,2,256]{2,1,0:T(2,128)(2,1)S(1)}, u32[]{:S(2)}, u32[]{:S(2)}) async-start(bf16[64,2,256]{2,1,0:T(2,128)(2,1)} %reshape.644), calls=%async_computation.2 | async-start | bytes 131072 | tf_op jit(solution)/shard_map/all_to_all | solution.py:27
  244.4 9.7 %all-to-all-done.2 = bf16[64,2,256]{2,1,0:T(2,128)(2,1)S(1)} async-done(((bf16[64,2,256]{2,1,0:T(2,128)(2,1)}), bf16[64,2,256]{2,1,0:T(2,128)(2,1)S(1)}, u32[]{:S(2)}, u32[]{:S(2)}) %all-to-all-start.2) | async-done | bytes 65568 | tf_op jit(solution)/shard_map/all_to_all | solution.py:27
  254.1 0.4 reshape.645
  254.5 0.2 copy.147
  254.6 1.2 gather_fusion.2
  255.8 0.4 copy.148
  256.4 3.8 %fusion.26 = f32[8,4,8,2049]{3,2,1,0:T(8,128)S(1)} fusion(f32[8,2,2049]{2,1,0:T(2,128)S(1)} %get-tuple-element.31, bf16[8,2049,128,1,1]{2,0,1,4,3:T(8,128)(2,1)} %bitcast.150, bf16[4,8,8,2,128]{4,3,2,1,0:T(2,128)(2,1)S(1)} %bitcast.161), kind=kOutput, calls=%fused_computation.29 | convolution fusion | flops 270140160 | bytes 6556736 | tf_op jit(solution)/shard_map/scphr,pkr->phsck/dot_general | solution.py:187
  260.2 1.5 fusion.83
  262.1 1.2 fusion.41
  263.4 0.3 maximum_multiply_fusion.1
  263.7 1.2 copy.160
  264.9 1.2 copy.161
  (51 shorter events, 1.5 us)
Async XLA Ops:
  0.6 52.9 %copy-start.1 = (s32[1024]{0:T(1024)S(1)}, s32[1024]{0:T(1024)}, u32[]{:S(2)}) copy-start(s32[1024]{0:T(1024)} %param.11) | copy-start | bytes 12292
  0.6 11.3 %copy-start.3 = (s32[128]{0:T(128)S(1)}, s32[128]{0:T(128)}, u32[]{:S(2)}) copy-start(s32[128]{0:T(128)} %param.12) | copy-start | bytes 1540
  0.7 21.4 %copy-start = (f32[128]{0:T(128)S(1)}, f32[128]{0:T(128)}, u32[]{:S(2)}) copy-start(f32[128]{0:T(128)} %param.13) | copy-start | bytes 1540
  26.1 167.3 %all-to-all-start = ((bf16[128,2,192]{2,1,0:T(2,128)(2,1)}), bf16[128,2,192]{2,1,0:T(2,128)(2,1)S(1)}, u32[]{:S(2)}, u32[]{:S(2)}) async-start(bf16[128,2,192]{2,1,0:T(2,128)(2,1)} %reshape.640), calls=%async_computation | async-start | bytes 262144 | tf_op jit(solution)/shard_map/all_to_all | solution.py:172
  54.2 139.1 %copy-start.2 = (s32[1,4096]{1,0:T(1,128)S(1)}, s32[1,4096]{1,0:T(1,128)}, u32[]{:S(2)}) copy-start(s32[1,4096]{1,0:T(1,128)} %param.15) | copy-start | bytes 49156
  54.2 139.2 %copy-start.4 = (f32[128]{0:T(128)S(1)}, f32[128]{0:T(128)}, u32[]{:S(2)}) copy-start(f32[128]{0:T(128)} %param.14) | copy-start | bytes 1540
  231.4 22.6 %all-to-all-start.2 = ((bf16[64,2,256]{2,1,0:T(2,128)(2,1)}), bf16[64,2,256]{2,1,0:T(2,128)(2,1)S(1)}, u32[]{:S(2)}, u32[]{:S(2)}) async-start(bf16[64,2,256]{2,1,0:T(2,128)(2,1)} %reshape.644), calls=%async_computation.2 | async-start | bytes 131072 | tf_op jit(solution)/shard_map/all_to_all | solution.py:27
where the time goes:
time: 267 us; the launch traced here: 266 us
  other arithmetic  145 us (54%)
  starting transfers between devices  40.4 us (15%)
  matrix products  34.1 us (13%)
  local copies, waits for them, and re-layouts  29.2 us (11%)
  waiting for transfers between devices  9.67 us (4%)
  blocking collectives  6.52 us (2%)
    another operation x3, other arithmetic  139 us
    all_to_all x1, starting transfers between devices, shards(): lax.all_to_all(outgoing, MA, split_axis=3, concat_axis=2, tiled=True)  27.5 us
    dot_general x1, matrix products, shards(): jnp.einsum('sqrj,emj->sqemr', products, dft_table, preferred_element_type...  14.1 us
    all_to_all x1, starting transfers between devices, turned_blocks(): filled = lax.all_to_all(filled, axes[k], k, k, tiled=True)  12.9 us
    dot_general x1, matrix products, shards(): jnp.einsum('sqemr,emj->sqrj', fourier, dft_table, preferred_element_type=...  12.5 us
    all_to_all x1, waiting for transfers between devices, turned_blocks(): filled = lax.all_to_all(filled, axes[k], k, k, tiled=True)  9.67 us
    gather x2, local copies, waits for them, and re-layouts, shards(): legendre_sums = jnp.take(legendre_sums, cycle_order, axis=4)  9.09 us
    all_to_all x1, blocking collectives, turned_blocks(): filled = lax.all_to_all(filled, axes[k], k, k, tiled=True)  6.52 us
  transfers between devices with their start and end apart: 2, of which 1 were waited for; matrix products, arithmetic and copies ran while one was open for 53% of the time, Pallas kernels for 0%

commit v1 on v0

--- a/solution.py
+++ b/solution.py
@@ -7,31 +7,6 @@
 from jax.sharding import PartitionSpec as P
 
 MA = ("ma_0", "ma_1", "ma_2")
-
-
-def cut_along(value, dim, length):
-    before, after = (value.shape[:dim], value.shape[dim + 1 :])
-    return jnp.moveaxis(value.reshape(*before, length, -1, *after), dim, 0)
-
-
-def laid_out(pieces, dim):
-    shape = list(pieces.shape[1:])
-    shape[dim] *= pieces.shape[0]
-    return jnp.moveaxis(pieces, 0, dim).reshape(shape)
-
-
-def turned_blocks(pieces, axes, turns):
-    inside = pieces.shape[1:]
-    filled = pieces.reshape(*(lax.axis_size(a) for a in axes), *inside)
-    for k in turns:
-        filled = lax.all_to_all(filled, axes[k], k, k, tiled=True)
-    return filled.reshape(-1, *inside)
-
-
-def two_step_exchange(value, groups, turns, split_dim, concat_dim):
-    length = lax.axis_size(groups[0]) * lax.axis_size(groups[1])
-    pieces = cut_along(value, split_dim, length)
-    return laid_out(turned_blocks(pieces, groups, turns), concat_dim)
 
 
 def pair_layout(small_orders, mode_count):
@@ -74,11 +49,47 @@
     return jnp.stack([small_orders, mode_count - 1 - small_orders], axis=1).reshape(-1)
 
 
-def fourier_table(orders_int, pixel_count):
-    pixel_index = lax.broadcasted_iota(jnp.int32, (orders_int.shape[0], pixel_count), 1)
-    turns = orders_int[:, None] * pixel_index % pixel_count
-    radians = turns.astype(jnp.float32) * (2.0 * math.pi / pixel_count)
-    return jnp.stack([jnp.cos(radians), -jnp.sin(radians)], axis=0).astype(jnp.bfloat16)
+def phases(rows, columns, period):
+    turns = lax.broadcasted_iota(jnp.int32, (rows, columns), 0) * lax.broadcasted_iota(
+        jnp.int32, (rows, columns), 1
+    )
+    radians = (turns % period).astype(jnp.float32) * (2.0 * math.pi / period)
+    return jnp.cos(radians), jnp.sin(radians)
+
+
+def bf(x):
+    return x.astype(jnp.bfloat16)
+
+
+def dot(spec, a, b):
+    return jnp.einsum(spec, bf(a), bf(b), preferred_element_type=jnp.float32)
+
+
+def to_pixels(values, pixel_count):
+    s, q, _, mode_count = values.shape
+    v = values.reshape(s, q, 2, mode_count // 64, 64)
+    c, d = phases(mode_count // 64, 64, 64)
+    re = dot("sqak,aj->sqkj", v[:, :, 0], c) - dot("sqak,aj->sqkj", v[:, :, 1], d)
+    im = dot("sqak,aj->sqkj", v[:, :, 0], d) + dot("sqak,aj->sqkj", v[:, :, 1], c)
+    tc, td = phases(64, 64, pixel_count)
+    hr = re * tc - im * td
+    hi = re * td + im * tc
+    c, d = phases(64, pixel_count // 64, 64)
+    return dot("sqkj,kl->sqjl", hr, c) - dot("sqkj,kl->sqjl", hi, d)
+
+
+def to_modes(values, mode_count):
+    s, q, j2, j1 = values.shape
+    c, d = phases(64, j1, 64)
+    re = dot("sqjl,kl->sqjk", values, c)
+    im = -dot("sqjl,kl->sqjk", values, d)
+    tc, td = phases(64, 64, j1 * j2)
+    rr = re * tc + im * td
+    ri = im * tc - re * td
+    c, d = phases(mode_count // 64, 64, 64)
+    zr = dot("sqjk,aj->sqak", rr, c) + dot("sqjk,aj->sqak", ri, d)
+    zi = dot("sqjk,aj->sqak", ri, c) - dot("sqjk,aj->sqak", rr, d)
+    return jnp.stack([zr, zi], axis=2).reshape(s, q, 2, mode_count)
 
 
 def combine_modes(legendre_sums, orders_int, cos_cycle, sin_cycle, mode_count):
@@ -162,22 +173,23 @@
     legendre_sums = jnp.take(legendre_sums, cycle_order, axis=4)
     legendre_sums = legendre_sums.reshape(legendre_sums.shape[0], 8, 2 * pairs_dev, cycle_count)
     all_orders = mode_columns(m_slots, mode_count)
-    dft_table = fourier_table(all_orders, pixel_count)
-    pixel_weights = pixel_mask.astype(jnp.float32)
+    pixel_weights = pixel_mask.astype(jnp.float32).reshape(pixel_count // 64, 64).T
     slot_theta = jnp.take(colatitude, cycle_order)
     local_orders = mode_columns(local_small, mode_count)
     outgoing = combine_modes(
         legendre_sums, local_orders, jnp.cos(slot_theta), jnp.sin(slot_theta), mode_count
     )
     fourier = lax.all_to_all(outgoing, MA, split_axis=3, concat_axis=2, tiled=True)
-    fourier = fourier.reshape(fourier.shape[0], 3, 2, mode_count, cycle_dev)
-    cycle_maps = jnp.einsum(
-        "sqemr,emj->sqrj", fourier, dft_table, preferred_element_type=jnp.float32
-    )
+    fourier = fourier.reshape(fourier.shape[0], 3, 2, mode_count)
+    place = (
+        jnp.zeros((mode_count,), jnp.int32).at[all_orders].set(lax.iota(jnp.int32, mode_count))
+    )
+    cycle_maps = to_pixels(jnp.take(fourier, place, axis=3), pixel_count)
     products = (pixel_weights * cycle_maps[:, 0:1] * cycle_maps[:, 1:3]).astype(jnp.bfloat16)
-    spectra = jnp.einsum("sqrj,emj->sqemr", products, dft_table, preferred_element_type=jnp.float32)
+    spectra = to_modes(products, mode_count)
     received = (spectra * pixel_count ** (-0.5)).astype(jnp.bfloat16)
-    returned = two_step_exchange(received, (("ma_0", "ma_1"), "ma_2"), (1, 0), 3, 4)
+    received = jnp.take(received, all_orders, axis=3)[..., None]
+    returned = lax.all_to_all(received, MA, split_axis=3, concat_axis=4, tiled=True)
     inverse = (
         jnp.zeros((cycle_count,), jnp.int32).at[cycle_order].set(lax.iota(jnp.int32, cycle_count))
     )

time: 267 us -> 186 us (0.70)
  other arithmetic: 145 us -> 19.1 us
  local copies, waits for them, and re-layouts: 29.2 us -> 99.8 us
  matrix products: 34.1 us -> 8.63 us
  blocking collectives: 6.52 us -> 0 us
  starting transfers between devices: 40.4 us -> 43.5 us
  waiting for transfers between devices: 9.67 us -> 12.4 us
    another operation x3 -> x2, other arithmetic: 139 us -> 0.23 us
    gather x0 -> x3, local copies, waits for them, and re-layouts: none -> 44.6 us  [the longest x2 27.8 us: shards(): cycle_maps = to_pixels(jnp.take(fourier, place, axis=3), pixel_count)]
    dot_general x2 -> x12, matrix products: 26.6 us -> 3.34 us  [dot(): return jnp.einsum(spec, bf(a), bf(b), preferred_element_type=jnp.float32)]
    unnamed x23 -> x43, local copies, waits for them, and re-layouts: 6.47 us -> 16.4 us
    unnamed x3 -> x4, other arithmetic: 0.1 us -> 9.3 us
    scatter x0 -> x1, local copies, waits for them, and re-layouts: none -> 8.05 us  [shards(): jnp.zeros((mode_count,), jnp.int32).at[all_orders]]
    all_to_all x1 -> x0, blocking collectives: 6.52 us -> none  [turned_blocks(): filled = lax.all_to_all(filled, axes[k], k, k, tiled=True)]
    all_to_all x2 -> x1, local copies, waits for them, and re-layouts: 0.97 us -> 5.16 us  [shards(): lax.all_to_all(received, MA, split_axis=3, concat_axis=4, tiled=True)]
  transfers between devices with their start and end apart: 2 -> 2, of which waited for: 1 -> 2; matrix products, arithmetic and copies ran while one was open for 53% -> 6% of each run, Pallas kernels for 0% -> 0%
where the time goes in v1:
time: 186 us; the launch traced here: 185 us
  local copies, waits for them, and re-layouts  99.8 us (54%)
  starting transfers between devices  43.5 us (23%)
  other arithmetic  19.1 us (10%)
  waiting for transfers between devices  12.4 us (7%)
  matrix products  8.63 us (5%)
    gather x2, local copies, waits for them, and re-layouts, shards(): cycle_maps = to_pixels(jnp.take(fourier, place, axis=3), pixel_count)  27.8 us
    all_to_all x1, starting transfers between devices, shards(): lax.all_to_all(outgoing, MA, split_axis=3, concat_axis=2, tiled=True)  27.5 us
    gather x1, local copies, waits for them, and re-layouts, shards(): received = jnp.take(received, all_orders, axis=3)[..., None]  16.8 us
    unnamed x43, local copies, waits for them, and re-layouts  16.4 us
    all_to_all x1, starting transfers between devices, shards(): lax.all_to_all(received, MA, split_axis=3, concat_axis=4, tiled=True)  16.1 us
    all_to_all x1, waiting for transfers between devices, shards(): lax.all_to_all(received, MA, split_axis=3, concat_axis=4, tiled=True)  11.9 us
    unnamed x4, other arithmetic  9.3 us
    gather x2, local copies, waits for them, and re-layouts, shards(): legendre_sums = jnp.take(legendre_sums, cycle_order, axis=4)  9.13 us
  transfers between devices with their start and end apart: 2, of which 2 were waited for; matrix products, arithmetic and copies ran while one was open for 6% of the time, Pallas kernels for 0%

profile of v1, /device:TPU:513, one launch (start us, length us, event | category | flops | bytes accessed | tf_op | source)
XLA Modules:
  0.0 184.8 jit_solution(17915096745473238373)
XLA Ops:
  0.7 0.8 fusion.152
  1.7 1.0 copy_bitcast_fusion.8
  2.7 0.8 sqrt_select_fusion
  3.6 1.0 fusion.18
  5.3 1.7 copy-done.1
  7.0 1.5 fusion.8
  8.5 2.6 %copy.174 = f32[4,8,8,2,128]{2,1,4,3,0:T(8,128)} copy(f32[4,8,8,2,128]{4,1,0,3,2:T(8,128)S(1)} %fusion.8) | data formatting | bytes 524288 | tf_op jit(solution)/shard_map/phsck,pkr->scphr/transpose | solution.py:170
  11.1 1.0 scatter_custom_fusion
  12.1 0.5 copy-done.14
  12.6 0.6 pad_clamp_fusion
  13.2 5.3 %gather_fusion = f32[128,4,8,8,2]{3,2,4,1,0:T(8,128)} fusion(f32[4,8,8,2,128]{2,1,4,3,0:T(8,128)} %copy.174, s32[1024]{0:T(1024)S(1)} %get-tuple-element.61), kind=kCustom, calls=%fused_computation | custom fusion | bytes 524800 | tf_op jit(solution)/shard_map/jit(_take)/gather | solution.py:173
  18.5 3.8 %copy.175 = f32[4,8,8,2,128]{4,1,3,2,0:T(8,128)S(1)} copy(f32[4,8,8,2,128]{2,1,3,0,4:T(8,128)} %bitcast.179) | data formatting | bytes 524288 | tf_op jit(solution)/shard_map/jit(_take)/gather | solution.py:173
  22.4 1.2 gather_fusion.1
  24.4 0.6 copy.179
  25.1 1.4 reshape.624
  26.4 27.5 %all-to-all-start = ((bf16[128,2,192]{2,1,0:T(2,128)(2,1)}), bf16[128,2,192]{2,1,0:T(2,128)(2,1)S(1)}, u32[]{:S(2)}, u32[]{:S(2)}) async-start(bf16[128,2,192]{2,1,0:T(2,128)(2,1)} %reshape.624), calls=%async_computation | async-start | bytes 262144 | tf_op jit(solution)/shard_map/all_to_all | solution.py:182
  54.1 0.3 reshape.544
  54.5 8.0 %scatter_custom_fusion.1 = s32[2048]{0:T(1024)S(1)} fusion(s32[2048]{0:T(1024)S(1)} %bitcast.193, s32[2048]{0:T(1024)S(1)} %iota.189, s32[]{:T(128)} %constant.152.clone.1), kind=kCustom, calls=%fused_computation.169 | custom fusion | bytes 8196 | tf_op jit(solution)/shard_map/scatter | solution.py:185
  62.6 0.6 fusion.97
  63.6 0.7 select_convert_fusion.1
  64.6 0.6 compare_and_fusion.1
  65.2 0.6 multiply_divide_fusion
  65.8 0.5 all-to-all-done
  66.3 0.6 reshape.625
  67.3 0.8 reshape.545
  68.1 2.7 %copy.181 = bf16[4,3,2,2048]{0,2,3,1:T(2,128)(2,1)S(1)} copy(bf16[4,3,2,2048]{3,2,1,0:T(2,128)(2,1)S(1)} %reshape.545) | data formatting | bytes 196608 | tf_op jit(solution)/shard_map/reshape | solution.py:183
  70.9 20.3 %gather_fusion.2 = bf16[2048,4,3,2]{1,3,2,0:T(2,128)(2,1)} fusion(bf16[4,3,2,2048]{0,2,3,1:T(2,128)(2,1)S(1)} %copy.181, s32[2048]{0:T(1024)} %get-tuple-element.58), kind=kCustom, calls=%fused_computation.2 | custom fusion | bytes 204800 | tf_op jit(solution)/shard_map/jit(_take)/gather | solution.py:187
  91.2 7.5 %copy.183 = bf16[4,3,2,32,64]{4,3,1,0,2:T(8,128)(2,1)S(1)} copy(bf16[4,3,2,32,64]{0,2,1,4,3:T(2,128)(2,1)} %bitcast.183) | data formatting | bytes 196608 | tf_op jit(solution)/shard_map/jit(_take)/gather | solution.py:187
  99.9 0.4 fusion.35
  100.2 0.4 convolution_subtract_fusion
  100.6 0.3 fusion.79
  101.0 0.3 add_convert_fusion.1
  102.6 1.8 copy.188
  104.4 16.8 %gather_fusion.3 = bf16[2048,4,2,2]{1,3,2,0:T(2,128)(2,1)} fusion(bf16[4,2,2,2048]{0,2,3,1:T(2,128)(2,1)S(1)} %copy.188, s32[2048]{0:T(1024)S(1)} %copy-done.6), kind=kCustom, calls=%fused_computation.3 | custom fusion | bytes 139264 | tf_op jit(solution)/shard_map/jit(_take)/gather | solution.py:191
  121.2 9.2 %fusion.159 = bf16[2048,1,2,2,4]{4,3,2,1,0:T(2,128)(2,1)S(1)} fusion(bf16[2048,4,2,2]{1,3,2,0:T(2,128)(2,1)} %gather_fusion.3, pred[2048]{0:T(1024)(128)(4,1)S(1)} %copy-done.9), kind=kLoop, calls=%fused_computation.241 | loop fusion | flops 32768 | bytes 133120
  130.4 4.5 %reshape.626 = bf16[128,2,128]{2,1,0:T(2,128)(2,1)} reshape(bf16[2048,1,2,2,4]{4,3,2,1,0:T(2,128)(2,1)S(1)} %fusion.159) | data formatting | bytes 131072
  134.9 16.1 %all-to-all-start.1 = ((bf16[128,2,128]{2,1,0:T(2,128)(2,1)}), bf16[128,2,128]{2,1,0:T(2,128)(2,1)S(1)}, u32[]{:S(2)}, u32[]{:S(2)}) async-start(bf16[128,2,128]{2,1,0:T(2,128)(2,1)} %reshape.626), calls=%async_computation.1 | async-start | bytes 131072 | tf_op jit(solution)/shard_map/all_to_all | solution.py:192
  151.0 11.9 %all-to-all-done.1 = bf16[128,2,128]{2,1,0:T(2,128)(2,1)S(1)} async-done(((bf16[128,2,128]{2,1,0:T(2,128)(2,1)}), bf16[128,2,128]{2,1,0:T(2,128)(2,1)S(1)}, u32[]{:S(2)}, u32[]{:S(2)}) %all-to-all-start.1) | async-done | bytes 65568 | tf_op jit(solution)/shard_map/all_to_all | solution.py:192
  162.9 4.5 %reshape.627 = bf16[2048,1,2,2,4]{4,3,2,1,0:T(2,128)(2,1)S(1)} reshape(bf16[128,2,128]{2,1,0:T(2,128)(2,1)S(1)} %all-to-all-done.1) | data formatting | bytes 131072
  167.4 5.2 %copy.191 = bf16[4,2,2,128,16,1]{4,0,3,2,1,5:T(4,128)(2,1)S(1)} copy(bf16[4,2,2,128,16,1]{0,2,1,4,3,5:T(2,128)(2,1)S(1)} %bitcast.178) | data formatting | bytes 131072 | tf_op jit(solution)/shard_map/all_to_all | solution.py:192
  172.6 1.3 gather_fusion.4
  173.9 0.4 copy.192
  174.5 3.8 %fusion.5 = f32[8,4,8,2049]{3,2,1,0:T(8,128)S(1)} fusion(f32[8,2,2049]{2,1,0:T(2,128)S(1)} %get-tuple-element.33, bf16[8,2049,128,1,1]{2,0,1,4,3:T(8,128)(2,1)} %bitcast.181, bf16[4,8,8,2,128]{4,3,2,1,0:T(2,128)(2,1)S(1)} %bitcast.191), kind=kOutput, calls=%fused_computation.14 | convolution fusion | flops 270140160 | bytes 6556736 | tf_op jit(solution)/shard_map/scphr,pkr->phsck/dot_general | solution.py:199
  178.3 1.5 fusion.158
  180.3 0.4 copy-done.3
  180.8 1.2 fusion.22
  182.3 1.2 copy.204
  183.6 1.2 copy.205
  (98 shorter events, 6.4 us)
Async XLA Ops:
  0.6 4.2 %copy-start.2 = (bf16[8,4,2,2049]{3,2,1,0:T(2,128)(2,1)S(1)}, bf16[8,4,2,2049]{3,2,1,0:T(2,128)(2,1)}, u32[]{:S(2)}) copy-start(bf16[8,4,2,2049]{3,2,1,0:T(2,128)(2,1)} %param.8) | copy-start | bytes 786820
  4.8 2.2 %copy-start.1 = (bf16[8,2049,128]{2,0,1:T(8,128)(2,1)S(1)}, bf16[8,2049,128]{2,0,1:T(8,128)(2,1)}, u32[]{:S(2)}) copy-start(bf16[8,2049,128]{2,0,1:T(8,128)(2,1)} %param.10) | copy-start | bytes 12589060
  8.5 2.6 %copy-start.12 = (s32[128]{0:T(128)S(1)}, s32[128]{0:T(128)}, u32[]{:S(2)}) copy-start(s32[128]{0:T(128)} %param.12) | copy-start | bytes 1540
  12.1 0.5 copy-start.14
  18.5 3.8 %copy-start = (f32[128]{0:T(128)S(1)}, f32[128]{0:T(128)}, u32[]{:S(2)}) copy-start(f32[128]{0:T(128)} %param.13) | copy-start | bytes 1540
  22.3 31.5 %copy-start.7 = (s32[1024]{0:T(1024)S(1)}, s32[1024]{0:T(1024)}, u32[]{:S(2)}) copy-start(s32[1024]{0:T(1024)} %param.11) | copy-start | bytes 12292
  23.8 40.6 %copy-start.8 = (s32[1,4096]{1,0:T(1,128)S(1)}, s32[1,4096]{1,0:T(1,128)}, u32[]{:S(2)}) copy-start(s32[1,4096]{1,0:T(1,128)} %param.15) | copy-start | bytes 49156
  24.2 41.0 %copy-start.13 = (f32[128]{0:T(128)S(1)}, f32[128]{0:T(128)}, u32[]{:S(2)}) copy-start(f32[128]{0:T(128)} %param.14) | copy-start | bytes 1540
  26.4 39.9 %all-to-all-start = ((bf16[128,2,192]{2,1,0:T(2,128)(2,1)}), bf16[128,2,192]{2,1,0:T(2,128)(2,1)S(1)}, u32[]{:S(2)}, u32[]{:S(2)}) async-start(bf16[128,2,192]{2,1,0:T(2,128)(2,1)} %reshape.624), calls=%async_computation | async-start | bytes 262144 | tf_op jit(solution)/shard_map/all_to_all | solution.py:182
  101.3 3.1 %copy-start.6 = (s32[2048]{0:T(1024)S(1)}, s32[2048]{0:T(1024)}, u32[]{:S(2)}) copy-start(s32[2048]{0:T(1024)} %get-tuple-element.59) | copy-start | bytes 24580
  101.3 19.9 %copy-start.9 = (pred[2048]{0:T(1024)(128)(4,1)S(1)}, pred[2048]{0:T(1024)(128)(4,1)}, u32[]{:S(2)}) copy-start(pred[2048]{0:T(1024)(128)(4,1)} %compare_and_fusion.1) | copy-start | bytes 6148
  121.2 29.8 %copy-start.15 = (s32[128]{0:T(128)S(1)}, s32[128]{0:T(128)}, u32[]{:S(2)}) copy-start(s32[128]{0:T(128)} %copy-done.14) | copy-start | bytes 1540
  134.9 28.0 %all-to-all-start.1 = ((bf16[128,2,128]{2,1,0:T(2,128)(2,1)}), bf16[128,2,128]{2,1,0:T(2,128)(2,1)S(1)}, u32[]{:S(2)}, u32[]{:S(2)}) async-start(bf16[128,2,128]{2,1,0:T(2,128)(2,1)} %reshape.626), calls=%async_computation.1 | async-start | bytes 131072 | tf_op jit(solution)/shard_map/all_to_all | solution.py:192
  167.4 7.0 %copy-start.10 = (f32[128]{0:T(128)S(1)}, f32[128]{0:T(128)}, u32[]{:S(2)}) copy-start(f32[128]{0:T(128)} %get-tuple-element.48) | copy-start | bytes 1540
  167.4 7.0 %copy-start.11 = (f32[128]{0:T(128)S(1)}, f32[128]{0:T(128)}, u32[]{:S(2)}) copy-start(f32[128]{0:T(128)} %get-tuple-element.49) | copy-start | bytes 1540
  179.8 0.9 copy-start.3
  179.8 0.9 copy-start.4
  179.8 0.9 copy-start.5

commit v2 on v0

v2 whole, which is shorter than its diff:
```python
import functools
import math

import jax
import jax.numpy as jnp
import numpy as np
from jax import lax
from jax.experimental import pallas as pl
from jax.experimental.pallas import tpu as pltpu
from jax.sharding import PartitionSpec as P

F32 = jnp.float32
BF16 = jnp.bfloat16
FOLD = 64
NT = (((1,), (1,)), ((), ()))
NN = (((1,), (0,)), ((), ()))


def dot(a, b, dims=NN):
    return lax.dot_general(a, b, dims, preferred_element_type=F32)


def iota(shape, dim):
    return lax.broadcasted_iota(jnp.int32, shape, dim)


def small_column(m_ref, first, pairs):
    row = iota((pairs, 1), 0)
    column = jnp.zeros((pairs, 1), jnp.int32)
    for p in range(pairs):
        column = jnp.where(row == p, m_ref[first + p], column)
    return column


def layout_rows(small, modes):
    k = iota((small.shape[0], modes), 1)
    upper = k >= modes - small
    degree = jnp.where(upper, k - 1, small + k).astype(F32)
    orders = jnp.where(upper, modes - 1 - small, small).astype(F32)
    last_degree = jnp.full(small.shape, modes - 1, F32)
    last_orders = (modes - 1 - small).astype(F32)
    return (
        (degree, orders, raising(degree, orders)),
        (last_degree, last_orders, raising(last_degree, last_orders)),
    )


def raising(degree, orders):
    square = (
        (degree * degree - orders * orders)
        * (2.0 * degree + 1.0)
        / jnp.maximum(2.0 * degree - 1.0, 1.0)
    )
    return jnp.where(degree > orders, jnp.sqrt(jnp.where(degree > orders, square, 0.0)), 0.0)


def slot_of_cycle(order_ref):
    n = order_ref.shape[1]
    return jnp.where(iota((n, n), 0) == order_ref[...], 1.0, 0.0)


def turn(values):
    rows = values.shape[0]
    real = iota(values.shape, 0) % 2 == 0
    return jnp.where(real, -pltpu.roll(values, rows - 1, 0), pltpu.roll(values, 1, 0))


def rows_of(ref, p):
    return jnp.concatenate([ref[p, s].astype(F32) for s in range(ref.shape[1])], axis=0)


def synth_kernel(
    axis, m_ref, order_ref, colat_ref, t_ref, w_ref, l_ref, tail_ref, out_ref, lr_ref, ltail_ref,
    c_ref, s_ref, f_ref, deg_ref, eps_ref,
):
    step = pl.program_id(0)
    pairs, sims = t_ref.shape[0], t_ref.shape[1]
    modes = t_ref.shape[3] - 1
    lines = 2 * sims
    chunk = l_ref.shape[0]
    first = lax.axis_index(axis) * pairs
    wide = out_ref.shape[1] // pairs

    @pl.when(step == 0)
    def _():
        small = small_column(m_ref, first, pairs)
        (degree, _, eps), (_, _, last_eps) = layout_rows(small, modes)
        deg_ref[...] = degree * (1.0 / modes)
        eps_ref[...] = eps * (1.0 / modes)
        k = iota((lines, modes), 1)
        tail_rows = tail_ref[0].astype(F32)
        for p in range(pairs):
            tbar, wiener = rows_of(t_ref, p), rows_of(w_ref, p)
            main, last = wiener[:, :modes], wiener[:, modes:]
            scaled = eps_ref[p : p + 1, :] * main
            raised = pltpu.roll(scaled, modes - 1, 1)
            last_scaled = (last_eps[p : p + 1, :] * (1.0 / modes)) * last
            raised = jnp.where(k == modes - 1, last_scaled, raised)
            sets = (tbar[:, :modes], main, deg_ref[p : p + 1, :] * main, raised)
            upper = k >= modes - m_ref[first + p]
            for q, values in enumerate(sets):
                c_ref[p, q * lines : (q + 1) * lines, :] = jnp.where(upper, 0.0, values).astype(BF16)
                c_ref[p, (4 + q) * lines : (5 + q) * lines, :] = jnp.where(upper, values, 0.0).astype(BF16)
            lasts = (tbar[:, modes:], last, ((modes - 1.0) / modes) * last)
            s_ref[p] = jnp.zeros(s_ref.shape[1:], F32)
            for q, values in enumerate(lasts):
                s_ref[p, (4 + q) * lines : (5 + q) * lines, :] = (
                    values.astype(BF16).astype(F32) * tail_rows[p : p + 1, :]
                )
        ltail_ref[...] = tail_rows

    f_ref[...] = l_ref[...].astype(F32).reshape(chunk * pairs, l_ref.shape[2])
    for p in range(pairs):
        table = f_ref[pl.ds(p, chunk, stride=pairs), :].astype(BF16)
        lr_ref[p] = table
        at = pl.multiple_of(step * chunk, chunk)
        s_ref[p] += dot(c_ref[p, :, pl.ds(at, chunk)], table)

    @pl.when(step == pl.num_programs(0) - 1)
    def _():
        theta = colat_ref[...]
        cos, inv_sin = jnp.cos(theta), 1.0 / jnp.sin(theta)
        blocks = []
        for p in range(pairs):
            small = m_ref[first + p]
            for half, order in enumerate((small, modes - 1 - small)):
                at = 4 * lines * half
                s0, s1, s2, s3 = (s_ref[p, at + q * lines : at + (q + 1) * lines, :] for q in range(4))
                weight = jnp.where(order == 0, 1.0, 2.0) * modes ** (-0.5)
                ratio = order.astype(F32) * (1.0 / modes)
                blocks.append(s0 * weight)
                blocks.append((cos * s2 - s3) * inv_sin * weight)
                blocks.append(turn(s1) * ratio * inv_sin * weight)
            row = iota((wide - 6 * lines, s_ref.shape[2]), 0)
            low, high = (small % FOLD).astype(F32), (small // FOLD).astype(F32)
            blocks.append(jnp.where(row == 0, low, jnp.where(row == 1, high, 0.0)))
        fourier = jnp.concatenate(blocks, axis=0).astype(BF16)
        cycle_of_slot = slot_of_cycle(order_ref).T.astype(BF16)
        out_ref[...] = dot(cycle_of_slot, fourier, NT).astype(BF16)


def synth(tbar_alm, twf_alm, table, m_slots, cycle_order, colatitude, axis):
    pairs, sims, _, rows = tbar_alm.shape
    modes = rows - 1
    cycles = table.shape[2]
    steps = 8
    chunk = modes // steps
    lines = 2 * sims
    wide = 8 * lines
    vmem = pl.BlockSpec(memory_space=pltpu.VMEM)
    return pl.pallas_call(
        functools.partial(synth_kernel, axis),
        grid=(steps,),
        in_specs=[
            pl.BlockSpec(memory_space=pltpu.SMEM), vmem, vmem, vmem, vmem,
            pl.BlockSpec((chunk, pairs, cycles), lambda j: (j, 0, 0)),
            pl.BlockSpec((1, pairs, cycles), lambda j: (modes, 0, 0)),
        ],
        out_specs=[
            pl.BlockSpec((cycles, pairs * wide), lambda j: (0, 0)),
            pl.BlockSpec((pairs, chunk, cycles), lambda j: (0, j, 0)),
            pl.BlockSpec((pairs, cycles), lambda j: (0, 0)),
        ],
        out_shape=[
            jax.ShapeDtypeStruct((cycles, pairs * wide), BF16),
            jax.ShapeDtypeStruct((pairs, modes, cycles), BF16),
            jax.ShapeDtypeStruct((pairs, cycles), F32),
        ],
        scratch_shapes=[
            pltpu.VMEM((pairs, 8 * lines, modes), BF16),
            pltpu.VMEM((pairs, 8 * lines, cycles), F32),
            pltpu.VMEM((chunk * pairs, cycles), F32),
            pltpu.VMEM((pairs, modes), F32),
            pltpu.VMEM((pairs, modes), F32),
        ],
        name="synth",
    )(m_slots, cycle_order.reshape(1, -1), colatitude.reshape(1, -1), tbar_alm, twf_alm, table, table)


def angles(left, right, period):
    return 2.0 * np.pi * (np.outer(left, right) % period) / period


def split(table):
    high = table.astype(np.float32).astype(jnp.bfloat16)
    return high, (table - high.astype(np.float64)).astype(np.float32).astype(jnp.bfloat16)


def sky_tables(modes, pixels):
    m1, j2, m2 = np.arange(FOLD), np.arange(FOLD), np.arange(modes // FOLD)
    j1 = np.arange(pixels // FOLD).reshape(-1, 2).T.reshape(-1)
    th = angles(j2, m2, FOLD).reshape(FOLD, 2, -1)
    c, s = np.cos(th), np.sin(th)
    first = np.stack([np.stack([c, -s], 2), np.stack([s, c], 2)], 0).reshape(2 * FOLD, -1)
    th = angles(j2, m1, pixels)
    twist = np.stack([np.tile(np.cos(th), (1, 2)), np.tile(np.sin(th), (1, 2))])
    th = angles(m1, j1, FOLD)
    two = np.eye(2)
    second = np.concatenate([np.kron(two, np.cos(th)), np.kron(two, -np.sin(th))], 0)
    third = np.concatenate([np.kron(two, np.cos(th.T)), np.kron(two, -np.sin(th.T))], 1)
    th = angles(m2, j2, FOLD).reshape(2, -1, FOLD)
    c, s = np.cos(th), np.sin(th)
    fourth = np.stack([np.concatenate([c, s], 2), np.concatenate([-s, c], 2)], 1)
    fourth = fourth.reshape(2 * modes // FOLD, -1)
    return (
        np.concatenate(split(first), 1), twist.astype(np.float32), np.concatenate(split(second), 0),
        np.concatenate(split(third), 0), np.concatenate(split(fourth), 1),
    )


def sky_kernel(
    pairs, sims, x_ref, mask_ref, first_ref, twist_ref, second_ref, third_ref, fourth_ref, out_ref,
    xt_ref, lhs_ref, hot_ref,
):
    devices, width = x_ref.shape
    wide = width // pairs
    lines = 2 * sims
    half_sims = sims // 2
    fold2 = 2 * FOLD
    tall = fourth_ref.shape[0] // 4
    xt_ref[...] = x_ref[...].astype(F32).T
    groups = [(q, a) for q in range(3) for a in range(half_sims)]

    def key(p, half):
        low = xt_ref[p * wide + 6 * lines : p * wide + 6 * lines + 1, :].astype(jnp.int32)
        high = xt_ref[p * wide + 6 * lines + 1 : p * wide + 6 * lines + 2, :].astype(jnp.int32)
        return (FOLD - 1 - low, tall - 1 - high) if half else (low, high)

    sorted_halves, places = [], []
    for half in range(2):
        place = []
        for p in range(pairs):
            low, high = key(p, half)
            place.append(iota((tall, devices), 0) == high)
            for e in range(2):
                at = (e * pairs + p) * devices
                hot_ref[half, :, at : at + devices] = jnp.where(
                    iota((fold2, devices), 0) == low + e * FOLD, 1.0, 0.0
                ).astype(BF16)
                parts = []
                for q, a in groups:
                    for c in range(2):
                        row = p * wide + (half * 3 + q) * lines + (e * half_sims + a) * 2 + c
                        parts.append(jnp.where(place[p], xt_ref[row : row + 1, :], 0.0))
                lhs_ref[:, at : at + devices] = jnp.concatenate(parts, axis=0).astype(BF16)
        places.append(place)
        sorted_halves.append(dot(lhs_ref[...], hot_ref[half], NT).astype(BF16))

    n = 2 * tall
    spread = jnp.concatenate(
        [
            jnp.concatenate([s[g * n : (g + 1) * n] for s in sorted_halves], axis=0)
            for g in range(len(groups))
        ],
        axis=1,
    )
    stage = dot(first_ref[...], jnp.concatenate([spread, spread], axis=0))
    cos, sin = twist_ref[0], twist_ref[1]
    twisted = []
    for g in range(len(groups)):
        re, im = (stage[i * FOLD : (i + 1) * FOLD, g * fold2 : (g + 1) * fold2] for i in range(2))
        twisted.append(jnp.concatenate([re * cos - im * sin, re * sin + im * cos], axis=1))
    twisted = jnp.concatenate(twisted, axis=0).astype(BF16)
    maps = dot(twisted, second_ref[: 2 * fold2]) + dot(twisted, second_ref[2 * fold2 :])

    mask = mask_ref[...].astype(F32).T
    mask = jnp.concatenate([mask[:FOLD], mask[FOLD:]] * 2, axis=1)
    products = []
    for q in range(1, 3):
        for a in range(half_sims):
            one = maps[a * FOLD : (a + 1) * FOLD]
            at = (q * half_sims + a) * FOLD
            products.append(mask * one * maps[at : at + FOLD])
    products = jnp.concatenate(products, axis=0).astype(BF16)
    stage = dot(products, third_ref[:fold2]) + dot(products, third_ref[fold2:])
    twisted = []
    for g in range(2 * half_sims):
        re, im = (stage[g * FOLD : (g + 1) * FOLD, i * fold2 : (i + 1) * fold2] for i in range(2))
        twisted.append(jnp.concatenate([re * cos + im * sin, im * cos - re * sin], axis=0))
    twisted = jnp.concatenate(twisted, axis=1).astype(BF16)
    pixels = mask_ref.shape[0] * mask_ref.shape[1]
    spectra = dot(fourth_ref[...], jnp.concatenate([twisted, twisted], axis=0)) * pixels ** (-0.5)
    spectra = spectra.astype(BF16)

    groups = 2 * half_sims
    add = jnp.where(
        iota((2 * groups, 2 * groups * tall), 1) // tall == iota((2 * groups, 2 * groups * tall), 0), 1.0, 0.0
    ).astype(BF16)
    found = []
    for half in range(2):
        rows = jnp.concatenate(
            [spectra[half * n : (half + 1) * n, g * fold2 : (g + 1) * fold2] for g in range(groups)], axis=0
        )
        for e in range(2):
            for p in range(pairs):
                at = (e * pairs + p) * devices
                values = dot(rows, hot_ref[half, :, at : at + devices])
                keep = jnp.concatenate([places[half][p]] * (2 * groups), axis=0)
                lhs_ref[: values.shape[0], at : at + devices] = jnp.where(keep, values, 0.0).astype(BF16)
        found.append(dot(add, lhs_ref[: 2 * groups * tall, :]))
    blocks = []
    upper = iota((lines, devices), 0) >= lines // 2
    for p in range(pairs):
        for half in range(2):
            a, b = (
                found[half][:, (e * pairs + p) * devices : (e * pairs + p + 1) * devices] for e in range(2)
            )
            blocks.append(jnp.where(upper, pltpu.roll(b, lines // 2, 0), a))
            blocks.append(jnp.where(upper, b, pltpu.roll(a, lines // 2, 0)))
    out_ref[...] = jnp.concatenate(blocks, axis=0).T.astype(BF16)


def sky(received, pixel_mask, pairs, sims, modes):
    devices = received.shape[0]
    pixels = pixel_mask.shape[1]
    tables = sky_tables(modes, pixels)
    vmem = pl.BlockSpec(memory_space=pltpu.VMEM)
    tall = modes // FOLD // 2
    return pl.pallas_call(
        functools.partial(sky_kernel, pairs, sims),
        in_specs=[vmem] * 7,
        out_specs=vmem,
        out_shape=jax.ShapeDtypeStruct((devices, pairs * 8 * sims), BF16),
        scratch_shapes=[
            pltpu.VMEM(received.shape[::-1], F32),
            pltpu.VMEM((3 * sims * tall, 2 * pairs * devices), BF16),
            pltpu.VMEM((2, 2 * FOLD, 2 * pairs * devices), BF16),
        ],
        name="sky",
    )(received, pixel_mask.reshape(-1, 2 * FOLD), *(jnp.asarray(t) for t in tables))


def analyse_kernel(
    axis, m_ref, order_ref, colat_ref, weight_ref, r_ref, l_ref, tail_ref, grad_ref, curl_ref,
    w_ref, deg_ref, eps_ref, ord_ref,
):
    p = pl.program_id(0)
    pairs, lines2, cycles = w_ref.shape
    lines = lines2 // 8
    modes = l_ref.shape[1]
    first = lax.axis_index(axis) * pairs
    factor = (modes / cycles) ** 0.5

    def scale_of(degree):
        return factor / jnp.sqrt(jnp.maximum(degree * (degree + 1.0), 1.0))

    @pl.when(p == 0)
    def _():
        small = small_column(m_ref, first, pairs)
        (degree, orders, eps), _ = layout_rows(small, modes)
        scale = scale_of(degree)
        deg_ref[...] = degree * scale
        eps_ref[...] = eps * scale
        ord_ref[...] = orders * scale
        spectra = dot(r_ref[...].astype(F32).T.astype(BF16), slot_of_cycle(order_ref).astype(BF16), NT)
        theta, weight = colat_ref[...], weight_ref[...]
        with_cos = weight * jnp.cos(theta) / jnp.sin(theta)
        with_sin = weight / jnp.sin(theta)
        for i in range(pairs):
            for half in range(2):
                for q in range(2):
                    at = ((i * 2 + half) * 2 + q) * lines
                    values = spectra[at : at + lines]
                    at = (half * 4 + q * 2) * lines
                    w_ref[i, at : at + lines] = (values * with_cos).astype(BF16)
                    w_ref[i, at + lines : at + 2 * lines] = (values * with_sin).astype(BF16)

    small = m_ref[first + p]
    level, raised, azimuth = (ref[pl.ds(p, 1), :] for ref in (deg_ref, eps_ref, ord_ref))
    weighted = w_ref[p]
    sums = dot(weighted, l_ref[0], NT)
    k = iota((lines, modes), 1)
    upper = k >= modes - small
    a0, a1, a2, a3 = (
        jnp.where(upper, sums[(4 + q) * lines : (5 + q) * lines], sums[q * lines : (q + 1) * lines])
        for q in range(4)
    )

    def previous(values):
        return jnp.where(k == 0, 0.0, pltpu.roll(values, 1, 1))

    grad = level * a0 - raised * previous(a1) - azimuth * turn(a3)
    curl = level * a2 - raised * previous(a3) + azimuth * turn(a1)
    last = jnp.sum(
        weighted[4 * lines :].astype(F32) * tail_ref[pl.ds(p, 1), :], axis=1, keepdims=True
    )
    degree = jnp.full((1, 1), modes - 1, F32)
    order = jnp.full((1, 1), modes - 1 - small, jnp.int32).astype(F32)
    scale = scale_of(degree)
    level, raised, azimuth = degree * scale, raising(degree, order) * scale, order * scale
    b0, b1, b2, b3 = (last[q * lines : (q + 1) * lines] for q in range(4))
    last_grad = level * b0 - raised * a1[:, modes - 1 :] - azimuth * turn(b3)
    last_curl = level * b2 - raised * a3[:, modes - 1 :] + azimuth * turn(b1)
    for s in range(lines // 2):
        rows = slice(2 * s, 2 * s + 2)
        grad_ref[0, s, :, :modes] = grad[rows]
        grad_ref[0, s, :, modes:] = last_grad[rows]
        curl_ref[0, s, :, :modes] = curl[rows]
        curl_ref[0, s, :, modes:] = last_curl[rows]


def analyse(returned, table, tail, m_slots, cycle_order, colatitude, cycle_weight, sims, axis):
    pairs, modes, cycles = table.shape
    vmem = pl.BlockSpec(memory_space=pltpu.VMEM)
    out = jax.ShapeDtypeStruct((pairs, sims, 2, modes + 1), F32)
    out_spec = pl.BlockSpec((1, sims, 2, modes + 1), lambda p: (p, 0, 0, 0))
    return pl.pallas_call(
        functools.partial(analyse_kernel, axis),
        grid=(pairs,),
        in_specs=[
            pl.BlockSpec(memory_space=pltpu.SMEM), vmem, vmem, vmem, vmem,
            pl.BlockSpec((1, modes, cycles), lambda p: (p, 0, 0)), vmem,
        ],
        out_specs=[out_spec, out_spec],
        out_shape=[out, out],
        scratch_shapes=[
            pltpu.VMEM((pairs, 16 * sims, cycles), BF16),
            pltpu.VMEM((pairs, modes), F32),
            pltpu.VMEM((pairs, modes), F32),
            pltpu.VMEM((pairs, modes), F32),
        ],
        name="analyse",
    )(m_slots, cycle_order.reshape(1, -1), colatitude.reshape(1, -1), cycle_weight.reshape(1, -1), returned, table, tail)


def shards(axis, tbar_alm, twf_alm, legendre, m_slots, cycle_order, colatitude, cycle_weight, pixel_mask):
    pairs, sims, _, rows = tbar_alm.shape
    by_row = jnp.transpose(legendre, (1, 0, 2))
    outgoing, table, tail = synth(tbar_alm, twf_alm, by_row, m_slots, cycle_order, colatitude, axis)
    received = lax.all_to_all(outgoing, axis, 0, 0, tiled=True)
    spectra = sky(received, pixel_mask, pairs, sims, rows - 1)
    returned = lax.all_to_all(spectra, axis, 0, 0, tiled=True)
    return analyse(returned, table, tail, m_slots, cycle_order, colatitude, cycle_weight, sims, axis)


def solution(mesh):
    coefficients = P("ma", "grp", None, None)
    return jax.shard_map(
        functools.partial(shards, "ma"),
        mesh=mesh,
        in_specs=(coefficients, coefficients, P("ma", None, None), P(), P(), P(), P(), P("ma", None)),
        out_specs=(coefficients, coefficients),
        check_vma=False,
    )
```

time: 267 us -> 86.3 us (0.32)
  other arithmetic: 145 us -> 3.02 us
  blocking collectives: 6.52 us -> 58.5 us
  starting transfers between devices: 40.4 us -> 0 us
  matrix products: 34.1 us -> 0 us
  local copies, waits for them, and re-layouts: 29.2 us -> 2.03 us
  Pallas kernels: 0 us -> 21.5 us
  waiting for transfers between devices: 9.67 us -> 0 us
    another operation x11 -> x0, other arithmetic: 144 us -> none
    all_to_all x1 -> x2, blocking collectives: 6.52 us -> 58.5 us  [the longest x1 39.3 us: shards(): received = lax.all_to_all(outgoing, axis, 0, 0, tiled=True)]
    all_to_all x2 -> x0, starting transfers between devices: 40.4 us -> none  [the longest x1 27.5 us: shards(): lax.all_to_all(outgoing, MA, split_axis=3, concat_axis=2, tiled=True)]
    dot_general x4 -> x0, matrix products: 34.1 us -> none  [the longest x1 14.1 us: shards(): jnp.einsum('sqrj,emj->sqemr', products, dft_table, preferred_element_type...]
    pallas_call x0 -> x3, Pallas kernels: none -> 21.5 us  [the longest x1 9.34 us: synth(): pl.pallas_call(functools.partial(synth_kernel, axis), grid=(steps,), in_s...]
    gather x5 -> x0, local copies, waits for them, and re-layouts: 11.9 us -> none  [the longest x2 9.09 us: shards(): legendre_sums = jnp.take(legendre_sums, cycle_order, axis=4)]
    all_to_all x2 -> x0, waiting for transfers between devices: 9.67 us -> none  [the longest x1 9.67 us: turned_blocks(): filled = lax.all_to_all(filled, axes[k], k, k, tiled=True)]
    unnamed x23 -> x6, local copies, waits for them, and re-layouts: 6.47 us -> 1.51 us
  transfers between devices with their start and end apart: 2 -> 0, of which waited for: 1 -> 0; matrix products, arithmetic and copies ran while one was open for 53% -> 0% of each run, Pallas kernels for 0% -> 0%
where the time goes in v2:
time: 86.3 us; the launch traced here: 85.7 us
  blocking collectives  58.5 us (68%)
  Pallas kernels  21.5 us (25%)
  other arithmetic  3.02 us (3%)
  local copies, waits for them, and re-layouts  2.03 us (2%)
    all_to_all x1, blocking collectives, shards(): received = lax.all_to_all(outgoing, axis, 0, 0, tiled=True)  39.3 us
    all_to_all x1, blocking collectives, shards(): returned = lax.all_to_all(spectra, axis, 0, 0, tiled=True)  19.2 us
    pallas_call x1, Pallas kernels, synth(): pl.pallas_call(functools.partial(synth_kernel, axis), grid=(steps,), in_s...  9.34 us
    pallas_call x1, Pallas kernels, analyse(): pl.pallas_call(functools.partial(analyse_kernel, axis), grid=(pairs,), in...  7.6 us
    pallas_call x1, Pallas kernels, sky(): pl.pallas_call(functools.partial(sky_kernel, pairs, sims), in_specs=[vmem...  4.56 us

profile of v2, /device:TPU:513, one launch (start us, length us, event | category | flops | bytes accessed | tf_op | source)
XLA Modules:
  0.0 85.7 jit_solution(13889324906350751720)
XLA Ops:
  0.6 9.3 %synth.1 = (bf16[128,512]{1,0:T(8,128)(2,1)}, bf16[8,2048,128]{2,1,0:T(8,128)(2,1)}, f32[8,128]{1,0:T(8,128)}) custom-call(s32[1024]{0:T(1024)} %m_ref.3, s32[1,128]{1,0:T(1,128)} %bitcast.20, f32[1,128]{1,0:T(1,128)} %bitcast.22, bf16[8,4,2,2049]{3,2,1,0:T(2,128)(2,1)} %t_ref.1, bf16[8,4,2,2049]{3,2,1,0:T(2,128)(2,1)} %w_ref.1, ...), custom_call_target="tpu_custom_call" | custom-call | tf_op jit(solution)/shard_map/synth/pallas_call | solution.py:151
  10.0 0.5 broadcast
  10.5 1.6 %reduce = bf16[128,512]{1,0:T(8,128)(2,1)S(1)} reduce(bf16[128,1,512]{2,0,1:T(8,128)(2,1)} %bitcast.18, bf16[]{:T(256)} %broadcast), dimensions={1}, to_apply=%copy.17.reduce_sub_computation | reduce | bytes 262146 | tf_op jit(solution)/shard_map/all_to_all | solution.py:430
  12.1 39.3 %all_to_all.22 = bf16[128,2,256]{2,1,0:T(2,128)(2,1)S(1)} all-to-all(bf16[128,2,256]{2,1,0:T(2,128)(2,1)S(1)} %reshape.26), channel_id=1, replica_groups=mesh['grp'=2,'ma'=128] {'ma'}, dimensions={0} | all-to-all | bytes 262144 | tf_op jit(solution)/shard_map/all_to_all | solution.py:430
  51.3 0.1 reshape.27
  51.4 0.7 copy.23
  52.1 4.6 %sky.1 = bf16[128,256]{1,0:T(8,128)(2,1)} custom-call(bf16[128,512]{1,0:T(8,128)(2,1)} %bitcast.15, s32[32,128]{1,0:T(8,128)} %bitcast.19, bf16[128,128]{1,0:T(8,128)(2,1)} %constant.10.clone.first_ref, f32[2,64,128]{2,1,0:T(8,128)} %constant.11.clone.twist_ref, bf16[512,128]{1,0:T(8,128)(2,1)} %constant.12.clone.second_ref, ...), custom_call_target="tpu_custom_call" | custom-call | tf_op jit(solution)/shard_map/sky/pallas_call | solution.py:319
  56.7 1.5 %reduce.1 = bf16[128,256]{1,0:T(8,128)(2,1)S(1)} reduce(bf16[128,1,256]{2,0,1:T(8,128)(2,1)} %bitcast.17, bf16[]{:T(256)} %broadcast), dimensions={1}, to_apply=%copy.18.reduce_sub_computation | reduce | bytes 131074 | tf_op jit(solution)/shard_map/all_to_all | solution.py:432
  58.2 19.2 %all_to_all.23 = bf16[128,2,128]{2,1,0:T(2,128)(2,1)S(1)} all-to-all(bf16[128,2,128]{2,1,0:T(2,128)(2,1)S(1)} %reshape.28), channel_id=1, replica_groups=mesh['grp'=2,'ma'=128] {'ma'}, dimensions={0} | all-to-all | bytes 131072 | tf_op jit(solution)/shard_map/all_to_all | solution.py:432
  77.4 0.6 copy.24
  78.1 7.6 %analyse.1 = (f32[8,4,2,2049]{3,2,1,0:T(2,128)}, f32[8,4,2,2049]{3,2,1,0:T(2,128)}) custom-call(s32[1024]{0:T(1024)} %m_ref.3, s32[1,128]{1,0:T(1,128)} %bitcast.21, f32[1,128]{1,0:T(1,128)} %bitcast.23, f32[1,128]{1,0:T(1,128)} %bitcast.24, bf16[128,256]{1,0:T(8,128)(2,1)} %bitcast.16, bf16[8,2048,128]{2,1,0:T(8,128)(2,1)} %get-tuple-element.6.l_ref, ...), custom_call_target="tpu_custom_call" | custom-call | tf_op jit(solution)/shard_map/analyse/pallas_call | solution.py:407
  (3 shorter events, 0.1 us)

commit v3 on v2

v3 whole, which is shorter than its diff:
```python
import functools
import math

import jax
import jax.numpy as jnp
import numpy as np
from jax import lax
from jax.experimental import pallas as pl
from jax.experimental.pallas import tpu as pltpu
from jax.sharding import PartitionSpec as P

F32 = jnp.float32
BF16 = jnp.bfloat16
LANES = 128
FOLD = 64
GRANT = 24 * 2**20
NT = (((1,), (1,)), ((), ()))
NN = (((1,), (0,)), ((), ()))


def dot(a, b, dims=NN):
    return lax.dot_general(a, b, dims, preferred_element_type=F32)


def iota(shape, dim):
    return lax.broadcasted_iota(jnp.int32, shape, dim)


def small_column(m_ref, first, pairs):
    row = iota((pairs, 1), 0)
    column = jnp.zeros((pairs, 1), jnp.int32)
    for p in range(pairs):
        column = jnp.where(row == p, m_ref[first + p], column)
    return column


def layout_rows(small, modes):
    k = iota((small.shape[0], modes), 1)
    upper = k >= modes - small
    degree = jnp.where(upper, k - 1, small + k).astype(F32)
    orders = jnp.where(upper, modes - 1 - small, small).astype(F32)
    last_degree = jnp.full(small.shape, modes - 1, F32)
    last_orders = (modes - 1 - small).astype(F32)
    return (
        (degree, orders, raising(degree, orders)),
        (last_degree, last_orders, raising(last_degree, last_orders)),
    )


def raising(degree, orders):
    square = (
        (degree * degree - orders * orders)
        * (2.0 * degree + 1.0)
        / jnp.maximum(2.0 * degree - 1.0, 1.0)
    )
    return jnp.where(degree > orders, jnp.sqrt(jnp.where(degree > orders, square, 0.0)), 0.0)


def slot_of_cycle(order_ref):
    n = order_ref.shape[1]
    return jnp.where(iota((n, n), 0) == order_ref[...], 1.0, 0.0)


def turn(values):
    rows = values.shape[0]
    real = iota(values.shape, 0) % 2 == 0
    return jnp.where(real, -pltpu.roll(values, rows - 1, 0), pltpu.roll(values, 1, 0))


def synth_kernel(
    axis, m_hbm, order_hbm, colat_hbm, t_hbm, w_hbm, l_hbm, out_ref, lr_ref, ltail_ref,
    m_ref, order_ref, colat_ref, t_ref, w_ref, l_ref, c_ref, s_ref, deg_ref, eps_ref, sems,
):
    pairs, sims = t_ref.shape[0], t_ref.shape[1]
    modes = t_ref.shape[3] - 1
    lines = 2 * sims
    steps = sems.shape[0] - 6
    chunk = modes // steps
    first = lax.axis_index(axis) * pairs
    wide = out_ref.shape[1] * out_ref.shape[2] // pairs

    pieces = [(m_hbm, m_ref), (order_hbm, order_ref), (colat_hbm, colat_ref), (w_hbm, w_ref), (t_hbm, t_ref)]
    for j in range(steps + 1):
        part = pl.ds(j * chunk, chunk if j < steps else 1)
        pieces.append((l_hbm.at[part], l_ref.at[part]))
    copies = [pltpu.make_async_copy(*piece, sems.at[i]) for i, piece in enumerate(pieces)]
    for copy in copies:
        copy.start()
    for copy in copies[:3]:
        copy.wait()

    small = small_column(m_ref, first, pairs)
    (degree, _, eps), (_, _, last_eps) = layout_rows(small, modes)
    deg_ref[...] = degree * (1.0 / modes)
    eps_ref[...] = eps * (1.0 / modes)
    last_eps = last_eps * (1.0 / modes)
    theta = colat_ref[...]
    cos, inv_sin = jnp.cos(theta), 1.0 / jnp.sin(theta)
    cycle_of_slot = slot_of_cycle(order_ref).T.astype(BF16)
    k = iota((1, modes), 1)
    ends = iota((lines, modes), 1) == modes - 1

    copies[3].wait()
    copies[4].wait()
    lasts = []
    for p in range(pairs):
        tbar = t_ref[p].reshape(lines, modes + 1)
        wiener = w_ref[p].reshape(lines, modes + 1).astype(F32)
        main, last = wiener[:, :modes], wiener[:, modes:]
        raised = pltpu.roll(eps_ref[p : p + 1, :] * main, modes - 1, 1)
        raised = jnp.where(ends, last_eps[p : p + 1, :] * last, raised)
        sets = jnp.concatenate(
            [
                jnp.concatenate([tbar[:, :modes].astype(F32), main], axis=0).astype(BF16),
                jnp.concatenate([deg_ref[p : p + 1, :] * main, raised], axis=0).astype(BF16),
            ],
            axis=0,
        )
        upper = jnp.where(k >= modes - m_ref[first + p], 1.0, 0.0)
        upper = jnp.broadcast_to(upper, (4 * lines, modes)).astype(BF16)
        above = sets * upper
        c_ref[p, : 4 * lines, :] = sets - above
        c_ref[p, 4 * lines :, :] = above
        lasts.append(
            jnp.concatenate(
                [tbar[:, modes:].astype(F32), last, ((modes - 1.0) / modes) * last, 0.0 * last], axis=0
            )
            .astype(BF16)
            .astype(F32)
        )

    copies[-1].wait()
    tail_rows = l_ref[modes].astype(F32)
    ltail_ref[...] = tail_rows
    for p in range(pairs):
        s_ref[p, : 4 * lines] = jnp.zeros((4 * lines, s_ref.shape[2]), F32)
        s_ref[p, 4 * lines :] = lasts[p] * tail_rows[p : p + 1, :]
    for j in range(steps):
        copies[5 + j].wait()
        at = slice(j * chunk, (j + 1) * chunk)
        table = jnp.swapaxes(l_ref[at], 0, 1)
        lr_ref[:, at, :] = table
        for p in range(pairs):
            s_ref[p] += dot(c_ref[p, :, at], table[p])

    blocks = []
    for p in range(pairs):
        small = m_ref[first + p]
        for half, order in enumerate((small, modes - 1 - small)):
            at = 4 * lines * half
            s0, s1, s2, s3 = (s_ref[p, at + q * lines : at + (q + 1) * lines, :] for q in range(4))
            weight = jnp.where(order == 0, 1.0, 2.0) * modes ** (-0.5)
            ratio = order.astype(F32) * (1.0 / modes)
            blocks.append(s0 * weight)
            blocks.append((cos * s2 - s3) * inv_sin * weight)
            blocks.append(turn(s1) * ratio * inv_sin * weight)
        row = iota((wide - 6 * lines, s_ref.shape[2]), 0)
        low, high = (small % FOLD).astype(F32), (small // FOLD).astype(F32)
        blocks.append(jnp.where(row == 0, low, jnp.where(row == 1, high, 0.0)))
    fourier = jnp.concatenate(blocks, axis=0).astype(BF16)
    out_ref[...] = dot(cycle_of_slot, fourier, NT).astype(BF16).reshape(out_ref.shape)


def synth(tbar_alm, twf_alm, table, m_slots, cycle_order, colatitude, axis):
    pairs, sims, _, rows = tbar_alm.shape
    modes = rows - 1
    cycles = table.shape[2]
    lines = 2 * sims
    wide = 8 * lines
    steps = 8
    vmem = pl.BlockSpec(memory_space=pltpu.VMEM)
    hbm = pl.BlockSpec(memory_space=pltpu.HBM)
    return pl.pallas_call(
        functools.partial(synth_kernel, axis),
        in_specs=[hbm] * 6,
        out_specs=[vmem] * 3,
        out_shape=[
            pltpu.VMEM((cycles, pairs * wide // LANES, LANES), BF16),
            pltpu.VMEM((pairs, modes, cycles), BF16),
            pltpu.VMEM((pairs, cycles), F32),
        ],
        scratch_shapes=[
            pltpu.SMEM(m_slots.shape, jnp.int32),
            pltpu.VMEM((1, cycles), jnp.int32),
            pltpu.VMEM((1, cycles), F32),
            pltpu.VMEM(tbar_alm.shape, BF16),
            pltpu.VMEM(twf_alm.shape, BF16),
            pltpu.VMEM(table.shape, BF16),
            pltpu.VMEM((pairs, 8 * lines, modes), BF16),
            pltpu.VMEM((pairs, 8 * lines, cycles), F32),
            pltpu.VMEM((pairs, modes), F32),
            pltpu.VMEM((pairs, modes), F32),
            pltpu.SemaphoreType.DMA((steps + 6,)),
        ],
        compiler_params=pltpu.CompilerParams(vmem_limit_bytes=GRANT),
        name="synth",
    )(*(pltpu.with_memory_space_constraint(x, pltpu.HBM) for x in (
        m_slots, cycle_order.reshape(1, -1), colatitude.reshape(1, -1), tbar_alm, twf_alm, table
    )))


def angles(left, right, period):
    return 2.0 * np.pi * (np.outer(left, right) % period) / period


def split(table):
    high = table.astype(np.float32).astype(jnp.bfloat16)
    return high, (table - high.astype(np.float64)).astype(np.float32).astype(jnp.bfloat16)


def sky_tables(modes, pixels):
    m1, j2, m2 = np.arange(FOLD), np.arange(FOLD), np.arange(modes // FOLD)
    j1 = np.arange(pixels // FOLD).reshape(-1, 2).T.reshape(-1)
    th = angles(j2, m2, FOLD).reshape(FOLD, 2, -1)
    c, s = np.cos(th), np.sin(th)
    first = np.stack([np.stack([c, -s], 2), np.stack([s, c], 2)], 0).reshape(2 * FOLD, -1)
    th = angles(j2, m1, pixels)
    twist = np.stack([np.tile(np.cos(th), (1, 2)), np.tile(np.sin(th), (1, 2))])
    th = angles(m1, j1, FOLD)
    two = np.eye(2)
    second = np.concatenate([np.kron(two, np.cos(th)), np.kron(two, -np.sin(th))], 0)
    third = np.concatenate([np.kron(two, np.cos(th.T)), np.kron(two, -np.sin(th.T))], 1)
    th = angles(m2, j2, FOLD).reshape(2, -1, FOLD)
    c, s = np.cos(th), np.sin(th)
    fourth = np.stack([np.concatenate([c, s], 2), np.concatenate([-s, c], 2)], 1)
    fourth = fourth.reshape(2 * modes // FOLD, -1)
    return (
        np.concatenate(split(first), 1), twist.astype(np.float32), np.concatenate(split(second), 0),
        np.concatenate(split(third), 0), np.concatenate(split(fourth), 1),
    )


def sky_kernel(
    pairs, sims, x_ref, mask_ref, first_ref, twist_ref, second_ref, third_ref, fourth_ref, out_ref,
    xt_ref, lhs_ref, hot_ref,
):
    devices = x_ref.shape[0]
    width = x_ref.shape[1] * x_ref.shape[2]
    wide = width // pairs
    lines = 2 * sims
    half_sims = sims // 2
    fold2 = 2 * FOLD
    tall = fourth_ref.shape[0] // 4
    xt_ref[...] = x_ref[...].reshape(devices, width).astype(F32).T
    groups = [(q, a) for q in range(3) for a in range(half_sims)]

    def key(p, half):
        low = xt_ref[p * wide + 6 * lines : p * wide + 6 * lines + 1, :].astype(jnp.int32)
        high = xt_ref[p * wide + 6 * lines + 1 : p * wide + 6 * lines + 2, :].astype(jnp.int32)
        return (FOLD - 1 - low, tall - 1 - high) if half else (low, high)

    sorted_halves, places = [], []
    for half in range(2):
        place = []
        for p in range(pairs):
            low, high = key(p, half)
            place.append(iota((tall, devices), 0) == high)
            for e in range(2):
                at = (e * pairs + p) * devices
                hot_ref[half, :, at : at + devices] = jnp.where(
                    iota((fold2, devices), 0) == low + e * FOLD, 1.0, 0.0
                ).astype(BF16)
                parts = []
                for q, a in groups:
                    for c in range(2):
                        row = p * wide + (half * 3 + q) * lines + (e * half_sims + a) * 2 + c
                        parts.append(jnp.where(place[p], xt_ref[row : row + 1, :], 0.0))
                lhs_ref[:, at : at + devices] = jnp.concatenate(parts, axis=0).astype(BF16)
        places.append(place)
        sorted_halves.append(dot(lhs_ref[...], hot_ref[half], NT).astype(BF16))

    n = 2 * tall
    spread = jnp.concatenate(
        [
            jnp.concatenate([s[g * n : (g + 1) * n] for s in sorted_halves], axis=0)
            for g in range(len(groups))
        ],
        axis=1,
    )
    stage = dot(first_ref[...], jnp.concatenate([spread, spread], axis=0))
    cos, sin = twist_ref[0], twist_ref[1]
    twisted = []
    for g in range(len(groups)):
        re, im = (stage[i * FOLD : (i + 1) * FOLD, g * fold2 : (g + 1) * fold2] for i in range(2))
        twisted.append(jnp.concatenate([re * cos - im * sin, re * sin + im * cos], axis=1))
    twisted = jnp.concatenate(twisted, axis=0).astype(BF16)
    maps = dot(twisted, second_ref[: 2 * fold2]) + dot(twisted, second_ref[2 * fold2 :])

    mask = mask_ref[...].astype(F32).T
    mask = jnp.concatenate([mask[:FOLD], mask[FOLD:]] * 2, axis=1)
    products = []
    for q in range(1, 3):
        for a in range(half_sims):
            one = maps[a * FOLD : (a + 1) * FOLD]
            at = (q * half_sims + a) * FOLD
            products.append(mask * one * maps[at : at + FOLD])
    products = jnp.concatenate(products, axis=0).astype(BF16)
    stage = dot(products, third_ref[:fold2]) + dot(products, third_ref[fold2:])
    twisted = []
    for g in range(2 * half_sims):
        re, im = (stage[g * FOLD : (g + 1) * FOLD, i * fold2 : (i + 1) * fold2] for i in range(2))
        twisted.append(jnp.concatenate([re * cos + im * sin, im * cos - re * sin], axis=0))
    twisted = jnp.concatenate(twisted, axis=1).astype(BF16)
    pixels = mask_ref.shape[0] * mask_ref.shape[1]
    spectra = dot(fourth_ref[...], jnp.concatenate([twisted, twisted], axis=0)) * pixels ** (-0.5)
    spectra = spectra.astype(BF16)

    groups = 2 * half_sims
    add = jnp.where(
        iota((2 * groups, 2 * groups * tall), 1) // tall == iota((2 * groups, 2 * groups * tall), 0), 1.0, 0.0
    ).astype(BF16)
    found = []
    for half in range(2):
        rows = jnp.concatenate(
            [spectra[half * n : (half + 1) * n, g * fold2 : (g + 1) * fold2] for g in range(groups)], axis=0
        )
        for e in range(2):
            for p in range(pairs):
                at = (e * pairs + p) * devices
                values = dot(rows, hot_ref[half, :, at : at + devices])
                keep = jnp.concatenate([places[half][p]] * (2 * groups), axis=0)
                lhs_ref[: values.shape[0], at : at + devices] = jnp.where(keep, values, 0.0).astype(BF16)
        found.append(dot(add, lhs_ref[: 2 * groups * tall, :]))
    blocks = []
    upper = iota((lines, devices), 0) >= lines // 2
    for p in range(pairs):
        for half in range(2):
            a, b = (
                found[half][:, (e * pairs + p) * devices : (e * pairs + p + 1) * devices] for e in range(2)
            )
            blocks.append(jnp.where(upper, pltpu.roll(b, lines // 2, 0), a))
            blocks.append(jnp.where(upper, b, pltpu.roll(a, lines // 2, 0)))
    out_ref[...] = jnp.concatenate(blocks, axis=0).T.astype(BF16).reshape(out_ref.shape)


def sky(received, pixel_mask, pairs, sims, modes):
    devices = received.shape[0]
    pixels = pixel_mask.shape[1]
    tables = sky_tables(modes, pixels)
    vmem = pl.BlockSpec(memory_space=pltpu.VMEM)
    tall = modes // FOLD // 2
    return pl.pallas_call(
        functools.partial(sky_kernel, pairs, sims),
        in_specs=[vmem] * 7,
        out_specs=vmem,
        out_shape=jax.ShapeDtypeStruct((devices, pairs * 8 * sims // LANES, LANES), BF16),
        scratch_shapes=[
            pltpu.VMEM((received.shape[1] * LANES, devices), F32),
            pltpu.VMEM((3 * sims * tall, 2 * pairs * devices), BF16),
            pltpu.VMEM((2, 2 * FOLD, 2 * pairs * devices), BF16),
        ],
        compiler_params=pltpu.CompilerParams(vmem_limit_bytes=GRANT),
        name="sky",
    )(received, pixel_mask.reshape(-1, 2 * FOLD), *(jnp.asarray(t) for t in tables))


def analyse_kernel(
    axis, m_ref, order_ref, colat_ref, weight_ref, r_ref, l_ref, tail_ref, grad_hbm, curl_hbm,
    w_ref, deg_ref, eps_ref, ord_ref, grad_ref, curl_ref, sems,
):
    pairs, modes, cycles = l_ref.shape
    lines = w_ref.shape[1] // 8
    sims = lines // 2
    first = lax.axis_index(axis) * pairs
    factor = (modes / cycles) ** 0.5

    def scale_of(degree):
        return factor / jnp.sqrt(jnp.maximum(degree * (degree + 1.0), 1.0))

    small = small_column(m_ref, first, pairs)
    (degree, orders, eps), (last_degree, last_orders, last_eps) = layout_rows(small, modes)
    scale = scale_of(degree)
    deg_ref[...] = degree * scale
    eps_ref[...] = eps * scale
    ord_ref[...] = orders * scale
    scale = scale_of(last_degree)
    last_degree, last_orders, last_eps = last_degree * scale, last_orders * scale, last_eps * scale

    rows = r_ref[...].reshape(cycles, r_ref.shape[1] * r_ref.shape[2])
    spectra = dot(rows.astype(F32).T.astype(BF16), slot_of_cycle(order_ref).astype(BF16), NT)
    theta, weight = colat_ref[...], weight_ref[...]
    with_cos = weight * jnp.cos(theta) / jnp.sin(theta)
    with_sin = weight / jnp.sin(theta)
    for i in range(pairs):
        for half in range(2):
            parts = []
            for q in range(2):
                at = ((i * 2 + half) * 2 + q) * lines
                values = spectra[at : at + lines]
                parts += [values * with_cos, values * with_sin]
            w_ref[i, half * 4 * lines : (half + 1) * 4 * lines] = jnp.concatenate(parts, axis=0).astype(BF16)

    k = iota((lines, modes), 1)
    starts = k == 0

    def previous(values):
        return jnp.where(starts, 0.0, pltpu.roll(values, 1, 1))

    copies = []
    for p in range(pairs):
        weighted = w_ref[p]
        sums = dot(weighted, l_ref[p], NT)
        upper = k >= modes - m_ref[first + p]
        a0, a1, a2, a3 = (
            jnp.where(upper, sums[(4 + q) * lines : (5 + q) * lines], sums[q * lines : (q + 1) * lines])
            for q in range(4)
        )
        level, raised, azimuth = (ref[p : p + 1, :] for ref in (deg_ref, eps_ref, ord_ref))
        grad = level * a0 - raised * previous(a1) - azimuth * turn(a3)
        curl = level * a2 - raised * previous(a3) + azimuth * turn(a1)
        last = jnp.sum(weighted[4 * lines :].astype(F32) * tail_ref[p : p + 1, :], axis=1, keepdims=True)
        level, raised, azimuth = (v[p : p + 1, :] for v in (last_degree, last_eps, last_orders))
        b0, b1, b2, b3 = (last[q * lines : (q + 1) * lines] for q in range(4))
        last_grad = level * b0 - raised * a1[:, modes - 1 :] - azimuth * turn(b3)
        last_curl = level * b2 - raised * a3[:, modes - 1 :] + azimuth * turn(b1)
        for ref, hbm, main, last in ((grad_ref, grad_hbm, grad, last_grad), (curl_ref, curl_hbm, curl, last_curl)):
            ref[p, :, :, :modes] = main.reshape(sims, 2, modes)
            ref[p, :, :, modes:] = last.reshape(sims, 2, 1)
            copies.append(pltpu.make_async_copy(ref.at[p], hbm.at[p], sems.at[len(copies)]))
            copies[-1].start()
    for copy in copies:
        copy.wait()


def analyse(returned, table, tail, m_slots, cycle_order, colatitude, cycle_weight, sims, axis):
    pairs, modes, cycles = table.shape
    vmem = pl.BlockSpec(memory_space=pltpu.VMEM)
    hbm = pl.BlockSpec(memory_space=pltpu.HBM)
    shape = (pairs, sims, 2, modes + 1)
    out = jax.ShapeDtypeStruct(shape, F32)
    return pl.pallas_call(
        functools.partial(analyse_kernel, axis),
        in_specs=[pl.BlockSpec(memory_space=pltpu.SMEM)] + [vmem] * 6,
        out_specs=[hbm, hbm],
        out_shape=[out, out],
        scratch_shapes=[
            pltpu.VMEM((pairs, 16 * sims, cycles), BF16),
            pltpu.VMEM((pairs, modes), F32),
            pltpu.VMEM((pairs, modes), F32),
            pltpu.VMEM((pairs, modes), F32),
            pltpu.VMEM(shape, F32),
            pltpu.VMEM(shape, F32),
            pltpu.SemaphoreType.DMA((2 * pairs,)),
        ],
        compiler_params=pltpu.CompilerParams(vmem_limit_bytes=GRANT),
        name="analyse",
    )(m_slots, cycle_order.reshape(1, -1), colatitude.reshape(1, -1), cycle_weight.reshape(1, -1), returned, table, tail)


def exchange(values, axis):
    return lax.all_to_all(values, axis, 0, 0, tiled=True)


def shards(axis, tbar_alm, twf_alm, legendre, m_slots, cycle_order, colatitude, cycle_weight, pixel_mask):
    pairs, sims, _, rows = tbar_alm.shape
    by_row = jnp.transpose(legendre, (1, 0, 2))
    outgoing, table, tail = synth(tbar_alm, twf_alm, by_row, m_slots, cycle_order, colatitude, axis)
    received = exchange(outgoing, axis)
    spectra = sky(received, pixel_mask, pairs, sims, rows - 1)
    returned = exchange(spectra, axis)
    return analyse(returned, table, tail, m_slots, cycle_order, colatitude, cycle_weight, sims, axis)


def solution(mesh):
    coefficients = P("ma", "grp", None, None)
    return jax.shard_map(
        functools.partial(shards, "ma"),
        mesh=mesh,
        in_specs=(coefficients, coefficients, P("ma", None, None), P(), P(), P(), P(), P("ma", None)),
        out_specs=(coefficients, coefficients),
        check_vma=False,
    )
```

time: 86.3 us -> 71.2 us (0.83)
  Pallas kernels: 21.5 us -> 11.4 us
  other arithmetic: 3.02 us -> 0 us
  local copies, waits for them, and re-layouts: 2.03 us -> 0.06 us
    pallas_call x2, Pallas kernels: 16.9 us -> 8.6 us  [the longest x1 5.28 us: synth(): pl.pallas_call(functools.partial(synth_kernel, axis), in_specs=[hbm] * 6,...]
    all_to_all x2 -> x0, other arithmetic: 3.02 us -> none  [the longest x1 1.55 us: shards(): received = lax.all_to_all(outgoing, axis, 0, 0, tiled=True)]
    pallas_call x1, Pallas kernels: 4.56 us -> 2.82 us  [sky(): pl.pallas_call(functools.partial(sky_kernel, pairs, sims), in_specs=[vmem...]
    unnamed x6 -> x20, local copies, waits for them, and re-layouts: 1.51 us -> 0.06 us
where the time goes in v3:
time: 71.2 us; the launch traced here: 71 us
  blocking collectives  58.6 us (82%)
  Pallas kernels  11.4 us (16%)
  between operations  0.93 us (1%)
    all_to_all x2, blocking collectives, exchange(): return lax.all_to_all(values, axis, 0, 0, tiled=True)  58.6 us
    pallas_call x1, Pallas kernels, synth(): pl.pallas_call(functools.partial(synth_kernel, axis), in_specs=[hbm] * 6,...  5.28 us
    pallas_call x1, Pallas kernels, analyse(): pl.pallas_call(functools.partial(analyse_kernel, axis), in_specs=[pl.Bloc...  3.33 us
    pallas_call x1, Pallas kernels, sky(): pl.pallas_call(functools.partial(sky_kernel, pairs, sims), in_specs=[vmem...  2.82 us

profile of v3, /device:TPU:513, one launch (start us, length us, event | category | flops | bytes accessed | tf_op | source)
XLA Modules:
  0.0 71.0 jit_solution(16738064272426115601)
XLA Ops:
  0.6 0.0 copy-start.3
  0.6 0.0 copy-start
  0.7 0.0 copy-start.1
  0.7 0.0 copy-start.2
  0.7 0.0 copy-start.4
  0.7 0.0 copy-start.6
  0.7 0.0 copy-start.8
  0.7 0.0 copy-start.7
  0.7 0.0 copy-start.5
  0.7 0.0 copy-start.9
  0.7 5.3 %synth.1 = (bf16[128,4,128]{2,1,0:T(4,128)(2,1)S(1)}, bf16[8,2048,128]{2,1,0:T(8,128)(2,1)S(1)}, f32[8,128]{1,0:T(8,128)S(1)}) custom-call(s32[1024]{0:T(1024)} %m_ref.1, s32[1,128]{1,0:T(1,128)} %bitcast.6, f32[1,128]{1,0:T(1,128)} %bitcast.8, bf16[8,4,2,2049]{3,2,1,0:T(2,128)(2,1)} %t_hbm.1, bf16[8,4,2,2049]{3,2,1,0:T(2,128)(2,1)} %w_hbm.1, ...), custom_call_target="tpu_custom_call" | custom-call | tf_op jit(solution)/shard_map/synth/pallas_call | solution.py:173
  6.0 39.3 %all_to_all.10.x_ref = bf16[128,4,128]{2,1,0:T(4,128)(2,1)S(1)} all-to-all(bf16[128,4,128]{2,1,0:T(4,128)(2,1)S(1)} %get-tuple-element.5), channel_id=1, replica_groups=mesh['grp'=2,'ma'=128] {'ma'}, dimensions={0} | all-to-all | bytes 262144 | tf_op jit(solution)/shard_map/all_to_all | solution.py:451
  45.3 0.0 copy-done.3
  45.3 0.0 copy-done
  45.3 0.0 copy-done.1
  45.3 0.0 copy-done.2
  45.3 0.0 copy-done.4
  45.3 0.0 copy-done.5
  45.3 2.8 %sky.1 = bf16[128,2,128]{2,1,0:T(2,128)(2,1)S(1)} custom-call(bf16[128,4,128]{2,1,0:T(4,128)(2,1)S(1)} %all_to_all.10.x_ref, s32[32,128]{1,0:T(8,128)S(1)} %bitcast.5, bf16[128,128]{1,0:T(8,128)(2,1)S(1)} %copy-done.4, f32[2,64,128]{2,1,0:T(8,128)S(1)} %copy-done.2, bf16[512,128]{1,0:T(8,128)(2,1)S(1)} %copy-done.1, bf16[256,256]{1,0:T(8,128)(2,1)S(1)} %copy-done, ...), custom_call_target="tpu_custom_call" | custom-call | tf_op jit(solution)/shard_map/sky/pallas_call | solution.py:342
  48.2 19.3 %all_to_all.11.r_ref = bf16[128,2,128]{2,1,0:T(2,128)(2,1)S(1)} all-to-all(bf16[128,2,128]{2,1,0:T(2,128)(2,1)S(1)} %sky.1), channel_id=1, replica_groups=mesh['grp'=2,'ma'=128] {'ma'}, dimensions={0} | all-to-all | bytes 131072 | tf_op jit(solution)/shard_map/all_to_all | solution.py:451
  67.5 0.0 copy-done.6
  67.5 0.0 copy-done.8
  67.5 0.0 copy-done.7
  67.5 0.0 copy-done.9
  67.5 3.3 %analyse.1 = (f32[8,4,2,2049]{3,2,1,0:T(2,128)}, f32[8,4,2,2049]{3,2,1,0:T(2,128)}) custom-call(s32[1024]{0:T(1024)S(1)} %copy-done.6, s32[1,128]{1,0:T(1,128)S(1)} %bitcast.7, f32[1,128]{1,0:T(1,128)S(1)} %bitcast.9, f32[1,128]{1,0:T(1,128)S(1)} %bitcast.10, bf16[128,2,128]{2,1,0:T(2,128)(2,1)S(1)} %all_to_all.11.r_ref, ...), custom_call_target="tpu_custom_call" | custom-call | tf_op jit(solution)/shard_map/analyse/pallas_call | solution.py:431
Async XLA Ops:
  0.6 44.7 %copy-start.3 = (bf16[64,256]{1,0:T(8,128)(2,1)S(1)}, bf16[64,256]{1,0:T(8,128)(2,1)}, u32[]{:S(2)}) copy-start(bf16[64,256]{1,0:T(8,128)(2,1)} %constant.14.clone.fourth_ref) | copy-start | bytes 98308
  0.6 44.6 %copy-start = (bf16[256,256]{1,0:T(8,128)(2,1)S(1)}, bf16[256,256]{1,0:T(8,128)(2,1)}, u32[]{:S(2)}) copy-start(bf16[256,256]{1,0:T(8,128)(2,1)} %constant.13.clone.third_ref) | copy-start | bytes 393220
  0.7 44.6 %copy-start.1 = (bf16[512,128]{1,0:T(8,128)(2,1)S(1)}, bf16[512,128]{1,0:T(8,128)(2,1)}, u32[]{:S(2)}) copy-start(bf16[512,128]{1,0:T(8,128)(2,1)} %constant.12.clone.second_ref) | copy-start | bytes 393220
  0.7 44.6 %copy-start.2 = (f32[2,64,128]{2,1,0:T(8,128)S(1)}, f32[2,64,128]{2,1,0:T(8,128)}, u32[]{:S(2)}) copy-start(f32[2,64,128]{2,1,0:T(8,128)} %constant.11.clone.twist_ref) | copy-start | bytes 196612
  0.7 44.6 %copy-start.4 = (bf16[128,128]{1,0:T(8,128)(2,1)S(1)}, bf16[128,128]{1,0:T(8,128)(2,1)}, u32[]{:S(2)}) copy-start(bf16[128,128]{1,0:T(8,128)(2,1)} %constant.10.clone.first_ref) | copy-start | bytes 98308
  0.7 66.8 %copy-start.6 = (s32[1024]{0:T(1024)S(1)}, s32[1024]{0:T(1024)}, u32[]{:S(2)}) copy-start(s32[1024]{0:T(1024)} %m_ref.1) | copy-start | bytes 12292
  0.7 66.8 %copy-start.8 = (f32[128]{0:T(128)S(1)}, f32[128]{0:T(128)}, u32[]{:S(2)}) copy-start(f32[128]{0:T(128)} %param.18) | copy-start | bytes 1540
  0.7 66.8 %copy-start.7 = (s32[128]{0:T(128)S(1)}, s32[128]{0:T(128)}, u32[]{:S(2)}) copy-start(s32[128]{0:T(128)} %param.17) | copy-start | bytes 1540
  0.7 44.6 %copy-start.5 = (s32[1,4096]{1,0:T(1,128)S(1)}, s32[1,4096]{1,0:T(1,128)}, u32[]{:S(2)}) copy-start(s32[1,4096]{1,0:T(1,128)} %param.20) | copy-start | bytes 49156
  0.7 66.8 %copy-start.9 = (f32[128]{0:T(128)S(1)}, f32[128]{0:T(128)}, u32[]{:S(2)}) copy-start(f32[128]{0:T(128)} %param.19) | copy-start | bytes 1540

commit v4 on v3

--- a/solution.py
+++ b/solution.py
@@ -7,6 +7,7 @@
 from jax import lax
 from jax.experimental import pallas as pl
 from jax.experimental.pallas import tpu as pltpu
+from jax.sharding import Mesh
 from jax.sharding import PartitionSpec as P
 
 F32 = jnp.float32
@@ -14,6 +15,7 @@
 LANES = 128
 FOLD = 64
 GRANT = 24 * 2**20
+CHIP, CORE = "chip", "core"
 NT = (((1,), (1,)), ((), ()))
 NN = (((1,), (0,)), ((), ()))
 
@@ -58,7 +60,17 @@
 
 def slot_of_cycle(order_ref):
     n = order_ref.shape[1]
-    return jnp.where(iota((n, n), 0) == order_ref[...], 1.0, 0.0)
+    core = lax.axis_index(CORE)
+    place = iota((n, n), 1)
+    near = place < n // 2
+    slot = 2 * (place % (n // 2)) + jnp.where(near, core, 1 - core)
+    pick = jnp.where(iota((n, n), 0) == slot, 1.0, 0.0).astype(BF16)
+    order = jnp.broadcast_to(order_ref[...].astype(F32), (8, n)).astype(BF16)
+    return jnp.where(iota((n, n), 0).astype(F32) == dot(order, pick)[:1], 1.0, 0.0)
+
+
+def first_pair(pairs):
+    return (lax.axis_index(CHIP) * lax.axis_size(CORE) + lax.axis_index(CORE)) * pairs
 
 
 def turn(values):
@@ -68,21 +80,21 @@
 
 
 def synth_kernel(
-    axis, m_hbm, order_hbm, colat_hbm, t_hbm, w_hbm, l_hbm, out_ref, lr_ref, ltail_ref,
-    m_ref, order_ref, colat_ref, t_ref, w_ref, l_ref, c_ref, s_ref, deg_ref, eps_ref, sems,
+    m_hbm, order_hbm, colat_hbm, t_hbm, w_hbm, l_hbm, near_ref, far_ref, lr_ref, ltail_ref,
+    m_ref, order_ref, colat_ref, t_ref, w_ref, last_ref, c_ref, s_ref, deg_ref, eps_ref, up_ref, end_ref, lasts_ref, sems, *l_refs,
 ):
     pairs, sims = t_ref.shape[0], t_ref.shape[1]
     modes = t_ref.shape[3] - 1
     lines = 2 * sims
-    steps = sems.shape[0] - 6
+    steps = len(l_refs)
     chunk = modes // steps
-    first = lax.axis_index(axis) * pairs
-    wide = out_ref.shape[1] * out_ref.shape[2] // pairs
+    first = first_pair(pairs)
+    wide = near_ref.shape[1] * near_ref.shape[2] // pairs
+    cycles = last_ref.shape[2]
 
     pieces = [(m_hbm, m_ref), (order_hbm, order_ref), (colat_hbm, colat_ref), (w_hbm, w_ref), (t_hbm, t_ref)]
-    for j in range(steps + 1):
-        part = pl.ds(j * chunk, chunk if j < steps else 1)
-        pieces.append((l_hbm.at[part], l_ref.at[part]))
+    pieces.append((l_hbm.at[pl.ds(modes, 1)], last_ref))
+    pieces += [(l_hbm.at[pl.ds(j * chunk, chunk)], l_refs[j]) for j in range(steps)]
     copies = [pltpu.make_async_copy(*piece, sems.at[i]) for i, piece in enumerate(pieces)]
     for copy in copies:
         copy.start()
@@ -97,58 +109,55 @@
     theta = colat_ref[...]
     cos, inv_sin = jnp.cos(theta), 1.0 / jnp.sin(theta)
     cycle_of_slot = slot_of_cycle(order_ref).T.astype(BF16)
-    k = iota((1, modes), 1)
+    up_ref[...] = jnp.where(iota((pairs, modes), 1) >= modes - small, 1.0, 0.0)
     ends = iota((lines, modes), 1) == modes - 1
 
     copies[3].wait()
     copies[4].wait()
-    lasts = []
-    for p in range(pairs):
+    def coefficients(p, _):
         tbar = t_ref[p].reshape(lines, modes + 1)
-        wiener = w_ref[p].reshape(lines, modes + 1).astype(F32)
-        main, last = wiener[:, :modes], wiener[:, modes:]
-        raised = pltpu.roll(eps_ref[p : p + 1, :] * main, modes - 1, 1)
-        raised = jnp.where(ends, last_eps[p : p + 1, :] * last, raised)
-        sets = jnp.concatenate(
-            [
-                jnp.concatenate([tbar[:, :modes].astype(F32), main], axis=0).astype(BF16),
-                jnp.concatenate([deg_ref[p : p + 1, :] * main, raised], axis=0).astype(BF16),
-            ],
-            axis=0,
+        wiener = w_ref[p].reshape(lines, modes + 1)
+        main, last = wiener[:, :modes].astype(F32), wiener[:, modes:].astype(F32)
+        raised = pltpu.roll(eps_ref[pl.ds(p, 1), :] * main, modes - 1, 1)
+        raised = jnp.where(ends, end_ref[pl.ds(p, 1), :][:, :1] * last, raised)
+        raised = jnp.concatenate([deg_ref[pl.ds(p, 1), :] * main, raised], axis=0).astype(BF16)
+        upper = jnp.broadcast_to(up_ref[pl.ds(p, 1), :], (2 * lines, modes)).astype(BF16)
+        for i, sets in enumerate((jnp.concatenate([tbar[:, :modes], wiener[:, :modes]], axis=0), raised)):
+            c_ref[p, 2 * i * lines : 2 * (i + 1) * lines, :] = sets
+            c_ref[p, 2 * (i + 2) * lines : 2 * (i + 3) * lines, :] = sets * upper
+        lasts = jnp.concatenate(
+            [tbar[:, modes:].astype(F32), last, ((modes - 1.0) / modes) * last, 0.0 * last], axis=0
         )
-        upper = jnp.where(k >= modes - m_ref[first + p], 1.0, 0.0)
-        upper = jnp.broadcast_to(upper, (4 * lines, modes)).astype(BF16)
-        above = sets * upper
-        c_ref[p, : 4 * lines, :] = sets - above
-        c_ref[p, 4 * lines :, :] = above
-        lasts.append(
-            jnp.concatenate(
-                [tbar[:, modes:].astype(F32), last, ((modes - 1.0) / modes) * last, 0.0 * last], axis=0
-            )
-            .astype(BF16)
-            .astype(F32)
-        )
-
-    copies[-1].wait()
-    tail_rows = l_ref[modes].astype(F32)
+        lasts_ref[p] = jnp.broadcast_to(lasts.astype(BF16).astype(F32), lasts_ref.shape[1:])
+        return 0
+
+    end_ref[...] = jnp.broadcast_to(last_eps, end_ref.shape)
+    lax.fori_loop(0, pairs, coefficients, 0)
+
+    copies[5].wait()
+    tail_rows = last_ref[0].astype(F32)
     ltail_ref[...] = tail_rows
-    for p in range(pairs):
-        s_ref[p, : 4 * lines] = jnp.zeros((4 * lines, s_ref.shape[2]), F32)
-        s_ref[p, 4 * lines :] = lasts[p] * tail_rows[p : p + 1, :]
-    for j in range(steps):
-        copies[5 + j].wait()
-        at = slice(j * chunk, (j + 1) * chunk)
-        table = jnp.swapaxes(l_ref[at], 0, 1)
-        lr_ref[:, at, :] = table
-        for p in range(pairs):
-            s_ref[p] += dot(c_ref[p, :, at], table[p])
+    for j in range(steps + 1):
+        if j < steps:
+            copies[6 + j].wait()
+            lr_ref[:, j * chunk : (j + 1) * chunk, :] = jnp.swapaxes(l_refs[j][...], 0, 1)
+        if j == 0:
+            continue
+        at = slice((j - 1) * chunk, j * chunk)
+        for p in range(0, pairs, 2):
+            both = jnp.concatenate([c_ref[p, :, at], c_ref[p + 1, :, at]], axis=0)
+            sums = dot(both, jnp.concatenate([lr_ref[p, at, :], lr_ref[p + 1, at, :]], axis=1))
+            for i in range(2):
+                part = sums[i * 8 * lines : (i + 1) * 8 * lines, i * cycles : (i + 1) * cycles]
+                s_ref[p + i] = part if j == 1 else s_ref[p + i] + part
 
     blocks = []
     for p in range(pairs):
         small = m_ref[first + p]
         for half, order in enumerate((small, modes - 1 - small)):
-            at = 4 * lines * half
-            s0, s1, s2, s3 = (s_ref[p, at + q * lines : at + (q + 1) * lines, :] for q in range(4))
+            above = s_ref[p, 4 * lines :, :]
+            sums = above + lasts_ref[p] * tail_rows[p : p + 1, :] if half else s_ref[p, : 4 * lines, :] - above
+            s0, s1, s2, s3 = (sums[q * lines : (q + 1) * lines] for q in range(4))
             weight = jnp.where(order == 0, 1.0, 2.0) * modes ** (-0.5)
             ratio = order.astype(F32) * (1.0 / modes)
             blocks.append(s0 * weight)
@@ -158,24 +167,27 @@
         low, high = (small % FOLD).astype(F32), (small // FOLD).astype(F32)
         blocks.append(jnp.where(row == 0, low, jnp.where(row == 1, high, 0.0)))
     fourier = jnp.concatenate(blocks, axis=0).astype(BF16)
-    out_ref[...] = dot(cycle_of_slot, fourier, NT).astype(BF16).reshape(out_ref.shape)
-
-
-def synth(tbar_alm, twf_alm, table, m_slots, cycle_order, colatitude, axis):
+    out = dot(cycle_of_slot, fourier, NT).astype(BF16)
+    near_ref[...] = out[: cycles // 2].reshape(near_ref.shape)
+    far_ref[...] = out[cycles // 2 :].reshape(far_ref.shape)
+
+
+def synth(tbar_alm, twf_alm, table, m_slots, cycle_order, colatitude):
     pairs, sims, _, rows = tbar_alm.shape
     modes = rows - 1
     cycles = table.shape[2]
     lines = 2 * sims
     wide = 8 * lines
-    steps = 8
+    steps = 4
     vmem = pl.BlockSpec(memory_space=pltpu.VMEM)
     hbm = pl.BlockSpec(memory_space=pltpu.HBM)
     return pl.pallas_call(
-        functools.partial(synth_kernel, axis),
+        synth_kernel,
         in_specs=[hbm] * 6,
-        out_specs=[vmem] * 3,
+        out_specs=[vmem] * 4,
         out_shape=[
-            pltpu.VMEM((cycles, pairs * wide // LANES, LANES), BF16),
+            pltpu.VMEM((cycles // 2, pairs * wide // LANES, LANES), BF16),
+            pltpu.VMEM((cycles // 2, pairs * wide // LANES, LANES), BF16),
             pltpu.VMEM((pairs, modes, cycles), BF16),
             pltpu.VMEM((pairs, cycles), F32),
         ],
@@ -185,13 +197,17 @@
             pltpu.VMEM((1, cycles), F32),
             pltpu.VMEM(tbar_alm.shape, BF16),
             pltpu.VMEM(twf_alm.shape, BF16),
-            pltpu.VMEM(table.shape, BF16),
+            pltpu.VMEM((1, pairs, cycles), BF16),
             pltpu.VMEM((pairs, 8 * lines, modes), BF16),
             pltpu.VMEM((pairs, 8 * lines, cycles), F32),
             pltpu.VMEM((pairs, modes), F32),
             pltpu.VMEM((pairs, modes), F32),
+            pltpu.VMEM((pairs, modes), F32),
+            pltpu.VMEM((pairs, LANES), F32),
+            pltpu.VMEM((pairs, 4 * lines, cycles), F32),
             pltpu.SemaphoreType.DMA((steps + 6,)),
-        ],
+        ]
+        + [pltpu.VMEM((modes // steps, pairs, cycles), BF16)] * steps,
         compiler_params=pltpu.CompilerParams(vmem_limit_bytes=GRANT),
         name="synth",
     )(*(pltpu.with_memory_space_constraint(x, pltpu.HBM) for x in (
@@ -230,18 +246,24 @@
     )
 
 
+def near_then_far(ref):
+    chips, parts, lanes = ref.shape
+    halves = (ref[:, : parts // 2], ref[:, parts // 2 :])
+    return jnp.concatenate([h.reshape(chips, parts // 2 * lanes) for h in halves], axis=0)
+
+
 def sky_kernel(
-    pairs, sims, x_ref, mask_ref, first_ref, twist_ref, second_ref, third_ref, fourth_ref, out_ref,
+    pairs, sims, x_ref, mask_ref, first_ref, twist_ref, second_ref, third_ref, fourth_ref, near_ref, far_ref,
     xt_ref, lhs_ref, hot_ref,
 ):
-    devices = x_ref.shape[0]
-    width = x_ref.shape[1] * x_ref.shape[2]
+    devices = 2 * x_ref.shape[0]
+    width = x_ref.shape[1] * x_ref.shape[2] // 2
     wide = width // pairs
     lines = 2 * sims
     half_sims = sims // 2
     fold2 = 2 * FOLD
     tall = fourth_ref.shape[0] // 4
-    xt_ref[...] = x_ref[...].reshape(devices, width).astype(F32).T
+    xt_ref[...] = near_then_far(x_ref).astype(F32).T
     groups = [(q, a) for q in range(3) for a in range(half_sims)]
 
     def key(p, half):
@@ -330,11 +352,13 @@
             )
             blocks.append(jnp.where(upper, pltpu.roll(b, lines // 2, 0), a))
             blocks.append(jnp.where(upper, b, pltpu.roll(a, lines // 2, 0)))
-    out_ref[...] = jnp.concatenate(blocks, axis=0).T.astype(BF16).reshape(out_ref.shape)
+    out = jnp.concatenate(blocks, axis=0).T.astype(BF16)
+    near_ref[...] = out[: devices // 2].reshape(near_ref.shape)
+    far_ref[...] = out[devices // 2 :].reshape(far_ref.shape)
 
 
 def sky(received, pixel_mask, pairs, sims, modes):
-    devices = received.shape[0]
+    devices = 2 * received.shape[0]
     pixels = pixel_mask.shape[1]
     tables = sky_tables(modes, pixels)
     vmem = pl.BlockSpec(memory_space=pltpu.VMEM)
@@ -342,10 +366,10 @@
     return pl.pallas_call(
         functools.partial(sky_kernel, pairs, sims),
         in_specs=[vmem] * 7,
-        out_specs=vmem,
-        out_shape=jax.ShapeDtypeStruct((devices, pairs * 8 * sims // LANES, LANES), BF16),
+        out_specs=[vmem] * 2,
+        out_shape=[pltpu.VMEM((devices // 2, pairs * 8 * sims // LANES, LANES), BF16)] * 2,
         scratch_shapes=[
-            pltpu.VMEM((received.shape[1] * LANES, devices), F32),
+            pltpu.VMEM((received.shape[1] // 2 * LANES, devices), F32),
             pltpu.VMEM((3 * sims * tall, 2 * pairs * devices), BF16),
             pltpu.VMEM((2, 2 * FOLD, 2 * pairs * devices), BF16),
         ],
@@ -355,13 +379,13 @@
 
 
 def analyse_kernel(
-    axis, m_ref, order_ref, colat_ref, weight_ref, r_ref, l_ref, tail_ref, grad_hbm, curl_hbm,
+    m_ref, order_ref, colat_ref, weight_ref, r_ref, l_ref, tail_ref, grad_hbm, curl_hbm,
     w_ref, deg_ref, eps_ref, ord_ref, grad_ref, curl_ref, sems,
 ):
     pairs, modes, cycles = l_ref.shape
-    lines = w_ref.shape[1] // 8
+    lines = w_ref.shape[1] // 16
     sims = lines // 2
-    first = lax.axis_index(axis) * pairs
+    first = first_pair(pairs)
     factor = (modes / cycles) ** 0.5
 
     def scale_of(degree):
@@ -376,11 +400,11 @@
     scale = scale_of(last_degree)
     last_degree, last_orders, last_eps = last_degree * scale, last_orders * scale, last_eps * scale
 
-    rows = r_ref[...].reshape(cycles, r_ref.shape[1] * r_ref.shape[2])
-    spectra = dot(rows.astype(F32).T.astype(BF16), slot_of_cycle(order_ref).astype(BF16), NT)
+    spectra = dot(near_then_far(r_ref).astype(F32).T.astype(BF16), slot_of_cycle(order_ref).astype(BF16), NT)
     theta, weight = colat_ref[...], weight_ref[...]
     with_cos = weight * jnp.cos(theta) / jnp.sin(theta)
     with_sin = weight / jnp.sin(theta)
+    blank = jnp.zeros((4 * lines, cycles), F32)
     for i in range(pairs):
         for half in range(2):
             parts = []
@@ -388,7 +412,11 @@
                 at = ((i * 2 + half) * 2 + q) * lines
                 values = spectra[at : at + lines]
                 parts += [values * with_cos, values * with_sin]
-            w_ref[i, half * 4 * lines : (half + 1) * 4 * lines] = jnp.concatenate(parts, axis=0).astype(BF16)
+            parts = jnp.concatenate(parts, axis=0)
+            at = ((i % 2) * 2 + half) * 4 * lines
+            w_ref[i // 2, at : at + 4 * lines] = jnp.concatenate(
+                [blank, parts] if i % 2 else [parts, blank], axis=1
+            ).astype(BF16)
 
     k = iota((lines, modes), 1)
     starts = k == 0
@@ -398,8 +426,12 @@
 
     copies = []
     for p in range(pairs):
-        weighted = w_ref[p]
-        sums = dot(weighted, l_ref[p], NT)
+        odd = p % 2
+        weighted = w_ref[p // 2, odd * 8 * lines : (odd + 1) * 8 * lines, odd * cycles : (odd + 1) * cycles]
+        if not odd:
+            tables = jnp.concatenate([l_ref[p], l_ref[p + 1]], axis=1)
+            both = dot(w_ref[p // 2], tables, NT)
+        sums = both[odd * 8 * lines : (odd + 1) * 8 * lines]
         upper = k >= modes - m_ref[first + p]
         a0, a1, a2, a3 = (
             jnp.where(upper, sums[(4 + q) * lines : (5 + q) * lines], sums[q * lines : (q + 1) * lines])
@@ -422,19 +454,19 @@
         copy.wait()
 
 
-def analyse(returned, table, tail, m_slots, cycle_order, colatitude, cycle_weight, sims, axis):
+def analyse(returned, table, tail, m_slots, cycle_order, colatitude, cycle_weight, sims):
     pairs, modes, cycles = table.shape
     vmem = pl.BlockSpec(memory_space=pltpu.VMEM)
     hbm = pl.BlockSpec(memory_space=pltpu.HBM)
     shape = (pairs, sims, 2, modes + 1)
     out = jax.ShapeDtypeStruct(shape, F32)
     return pl.pallas_call(
-        functools.partial(analyse_kernel, axis),
+        analyse_kernel,
         in_specs=[pl.BlockSpec(memory_space=pltpu.SMEM)] + [vmem] * 6,
         out_specs=[hbm, hbm],
         out_shape=[out, out],
         scratch_shapes=[
-            pltpu.VMEM((pairs, 16 * sims, cycles), BF16),
+            pltpu.VMEM((pairs // 2, 32 * sims, 2 * cycles), BF16),
             pltpu.VMEM((pairs, modes), F32),
             pltpu.VMEM((pairs, modes), F32),
             pltpu.VMEM((pairs, modes), F32),
@@ -447,26 +479,45 @@
     )(m_slots, cycle_order.reshape(1, -1), colatitude.reshape(1, -1), cycle_weight.reshape(1, -1), returned, table, tail)
 
 
-def exchange(values, axis):
-    return lax.all_to_all(values, axis, 0, 0, tiled=True)
-
-
-def shards(axis, tbar_alm, twf_alm, legendre, m_slots, cycle_order, colatitude, cycle_weight, pixel_mask):
+def merge_kernel(near_ref, far_ref, out_ref):
+    parts = near_ref.shape[1]
+    out_ref[:, :parts] = near_ref[...]
+    out_ref[:, parts:] = far_ref[...]
+
+
+def exchange(near, far):
+    vmem = pl.BlockSpec(memory_space=pltpu.VMEM)
+    swapped = lax.ppermute(far, CORE, [(0, 1), (1, 0)])
+    chips, parts, lanes = near.shape
+    both = pl.pallas_call(
+        merge_kernel,
+        in_specs=[vmem] * 2,
+        out_specs=vmem,
+        out_shape=pltpu.VMEM((chips, 2 * parts, lanes), near.dtype),
+        compiler_params=pltpu.CompilerParams(vmem_limit_bytes=GRANT),
+        name="merge",
+    )(near, swapped)
+    return lax.all_to_all(both, CHIP, 0, 0, tiled=True)
+
+
+def shards(tbar_alm, twf_alm, legendre, m_slots, cycle_order, colatitude, cycle_weight, pixel_mask):
     pairs, sims, _, rows = tbar_alm.shape
     by_row = jnp.transpose(legendre, (1, 0, 2))
-    outgoing, table, tail = synth(tbar_alm, twf_alm, by_row, m_slots, cycle_order, colatitude, axis)
-    received = exchange(outgoing, axis)
-    spectra = sky(received, pixel_mask, pairs, sims, rows - 1)
-    returned = exchange(spectra, axis)
-    return analyse(returned, table, tail, m_slots, cycle_order, colatitude, cycle_weight, sims, axis)
+    near, far, table, tail = synth(tbar_alm, twf_alm, by_row, m_slots, cycle_order, colatitude)
+    near, far = sky(exchange(near, far), pixel_mask, pairs, sims, rows - 1)
+    returned = exchange(near, far)
+    return analyse(returned, table, tail, m_slots, cycle_order, colatitude, cycle_weight, sims)
 
 
 def solution(mesh):
-    coefficients = P("ma", "grp", None, None)
+    devices = mesh.devices.reshape(mesh.shape["grp"], -1, 2)
+    finer = Mesh(devices, ("grp", CHIP, CORE))
+    ma = (CHIP, CORE)
+    coefficients = P(ma, "grp", None, None)
     return jax.shard_map(
-        functools.partial(shards, "ma"),
-        mesh=mesh,
-        in_specs=(coefficients, coefficients, P("ma", None, None), P(), P(), P(), P(), P("ma", None)),
+        shards,
+        mesh=finer,
+        in_specs=(coefficients, coefficients, P(ma, None, None), P(), P(), P(), P(), P(ma, None)),
         out_specs=(coefficients, coefficients),
         check_vma=False,
     )

time: 71.2 us -> 67.8 us (0.952)
  blocking collectives: 58.6 us -> 31.4 us
  starting transfers between devices: 0 us -> 22.8 us
  waiting for transfers between devices: 0 us -> 1.76 us
    all_to_all x2, blocking collectives: 58.6 us -> 31.4 us  [exchange(): return lax.all_to_all(both, CHIP, 0, 0, tiled=True)]
    ppermute x0 -> x2, starting transfers between devices: none -> 22.8 us  [exchange(): swapped = lax.ppermute(far, CORE, [(0, 1), (1, 0)])]
    ppermute x0 -> x2, waiting for transfers between devices: none -> 1.76 us  [exchange(): swapped = lax.ppermute(far, CORE, [(0, 1), (1, 0)])]
    pallas_call x2 -> x4, Pallas kernels: 8.6 us -> 8.03 us  [the longest x1 4.51 us: synth(): pl.pallas_call(synth_kernel, in_specs=[hbm] * 6, out_specs=[vmem] * 4, ou...]
  transfers between devices with their start and end apart: 0 -> 2, of which waited for: 0 -> 2; matrix products, arithmetic and copies ran while one was open for 0% -> 0% of each run, Pallas kernels for 0% -> 0%
where the time goes in v4:
time: 67.8 us; the launch traced here: 67.7 us
  blocking collectives  31.4 us (46%)
  starting transfers between devices  22.8 us (34%)
  Pallas kernels  10.9 us (16%)
  waiting for transfers between devices  1.76 us (3%)
  between operations  0.78 us (1%)
    all_to_all x2, blocking collectives, exchange(): return lax.all_to_all(both, CHIP, 0, 0, tiled=True)  31.4 us
    ppermute x2, starting transfers between devices, exchange(): swapped = lax.ppermute(far, CORE, [(0, 1), (1, 0)])  22.8 us
    pallas_call x1, Pallas kernels, synth(): pl.pallas_call(synth_kernel, in_specs=[hbm] * 6, out_specs=[vmem] * 4, ou...  4.51 us
    pallas_call x1, Pallas kernels, analyse(): pl.pallas_call(analyse_kernel, in_specs=[pl.BlockSpec(memory_space=pltpu....  3.38 us
    pallas_call x1, Pallas kernels, sky(): pl.pallas_call(functools.partial(sky_kernel, pairs, sims), in_specs=[vmem...  2.83 us
    ppermute x2, waiting for transfers between devices, exchange(): swapped = lax.ppermute(far, CORE, [(0, 1), (1, 0)])  1.76 us
  transfers between devices with their start and end apart: 2, of which 2 were waited for; matrix products, arithmetic and copies ran while one was open for 0% of the time, Pallas kernels for 0%

profile of v4, /device:TPU:513, one launch (start us, length us, event | category | flops | bytes accessed | tf_op | source)
XLA Modules:
  0.0 67.7 jit_solution(17744669719082539270)
XLA Ops:
  0.6 0.0 copy-start.3
  0.6 0.0 copy-start
  0.7 0.0 copy-start.1
  0.7 0.0 copy-start.2
  0.7 0.0 copy-start.4
  0.7 0.0 copy-start.6
  0.7 0.0 copy-start.8
  0.7 0.0 copy-start.7
  0.7 0.0 copy-start.5
  0.7 0.0 copy-start.9
  0.7 4.5 %synth.1 = (bf16[64,4,128]{2,1,0:T(4,128)(2,1)S(1)}, bf16[64,4,128]{2,1,0:T(4,128)(2,1)S(1)}, bf16[8,2048,128]{2,1,0:T(8,128)(2,1)S(1)}, f32[8,128]{1,0:T(8,128)S(1)}) custom-call(s32[1024]{0:T(1024)} %m_ref.1, s32[1,128]{1,0:T(1,128)} %bitcast.6, f32[1,128]{1,0:T(1,128)} %bitcast.8, bf16[8,4,2,2049]{3,2,1,0:T(2,128)(2,1)} %t_hbm.1, ...), custom_call_target="tpu_custom_call" | custom-call | tf_op jit(solution)/shard_map/synth/pallas_call | solution.py:184
  5.3 20.5 %collective-permute-start = (bf16[64,4,128]{2,1,0:T(4,128)(2,1)S(1)}, bf16[64,4,128]{2,1,0:T(4,128)(2,1)S(1)}, u32[]{:S(2)}, u32[]{:S(2)}) collective-permute-start(bf16[64,4,128]{2,1,0:T(4,128)(2,1)S(1)} %get-tuple-element.9), channel_id=1, source_target_pairs={{0,1},{1,0},{2,3},{3,2},{4,5},{5,4},{6,7},{7,6},{8,9},{9,8},{10,11... | collective-permute-start | bytes 196616 | tf_op jit(solution)/shard_map/ppermute | solution.py:490
  25.8 0.9 %collective-permute-done.far_ref = bf16[64,4,128]{2,1,0:T(4,128)(2,1)S(1)} collective-permute-done((bf16[64,4,128]{2,1,0:T(4,128)(2,1)S(1)}, bf16[64,4,128]{2,1,0:T(4,128)(2,1)S(1)}, u32[]{:S(2)}, u32[]{:S(2)}) %collective-permute-start) | collective-permute-done | bytes 65568 | tf_op jit(solution)/shard_map/ppermute | solution.py:490
  26.7 0.1 merge.2
  26.8 15.9 %all_to_all.10.x_ref = bf16[64,8,128]{2,1,0:T(8,128)(2,1)S(1)} all-to-all(bf16[64,8,128]{2,1,0:T(8,128)(2,1)S(1)} %merge.2), channel_id=1, replica_groups=mesh['grp'=2,'chip'=64,'core'=2] {'chip'}, dimensions={0} | all-to-all | bytes 262144 | tf_op jit(solution)/shard_map/all_to_all | solution.py:500
  42.7 0.0 copy-done.3
  42.7 0.0 copy-done
  42.7 0.0 copy-done.1
  42.7 0.0 copy-done.2
  42.7 0.0 copy-done.4
  42.7 0.0 copy-done.5
  42.7 2.8 %sky.1 = (bf16[64,2,128]{2,1,0:T(2,128)(2,1)S(1)}, bf16[64,2,128]{2,1,0:T(2,128)(2,1)S(1)}) custom-call(bf16[64,8,128]{2,1,0:T(8,128)(2,1)S(1)} %all_to_all.10.x_ref, s32[32,128]{1,0:T(8,128)S(1)} %bitcast.5, bf16[128,128]{1,0:T(8,128)(2,1)S(1)} %copy-done.4, f32[2,64,128]{2,1,0:T(8,128)S(1)} %copy-done.2, bf16[512,128]{1,0:T(8,128)(2,1)S(1)} %copy-done.1, ...), custom_call_target="tpu_custom_call" | custom-call | tf_op jit(solution)/shard_map/sky/pallas_call | solution.py:366
  45.6 2.2 %collective-permute-start.1 = (bf16[64,2,128]{2,1,0:T(2,128)(2,1)S(1)}, bf16[64,2,128]{2,1,0:T(2,128)(2,1)S(1)}, u32[]{:S(2)}, u32[]{:S(2)}) collective-permute-start(bf16[64,2,128]{2,1,0:T(2,128)(2,1)S(1)} %get-tuple-element.11), channel_id=1, source_target_pairs={{0,1},{1,0},{2,3},{3,2},{4,5},{5,4},{6,7},{7,6},{8,9},{9,8},{10,11... | collective-permute-start | bytes 98312 | tf_op jit(solution)/shard_map/ppermute | solution.py:490
  47.8 0.9 %collective-permute-done.1.far_ref = bf16[64,2,128]{2,1,0:T(2,128)(2,1)S(1)} collective-permute-done((bf16[64,2,128]{2,1,0:T(2,128)(2,1)S(1)}, bf16[64,2,128]{2,1,0:T(2,128)(2,1)S(1)}, u32[]{:S(2)}, u32[]{:S(2)}) %collective-permute-start.1) | collective-permute-done | bytes 32800 | tf_op jit(solution)/shard_map/ppermute | solution.py:490
  48.6 0.1 merge.3
  48.7 15.6 %all_to_all.11.r_ref = bf16[64,4,128]{2,1,0:T(4,128)(2,1)S(1)} all-to-all(bf16[64,4,128]{2,1,0:T(4,128)(2,1)S(1)} %merge.3), channel_id=1, replica_groups=mesh['grp'=2,'chip'=64,'core'=2] {'chip'}, dimensions={0} | all-to-all | bytes 131072 | tf_op jit(solution)/shard_map/all_to_all | solution.py:500
  64.3 0.0 copy-done.6
  64.3 0.0 copy-done.8
  64.3 0.0 copy-done.7
  64.3 0.0 copy-done.9
  64.3 3.4 %analyse.1 = (f32[8,4,2,2049]{3,2,1,0:T(2,128)}, f32[8,4,2,2049]{3,2,1,0:T(2,128)}) custom-call(s32[1024]{0:T(1024)S(1)} %copy-done.6, s32[1,128]{1,0:T(1,128)S(1)} %bitcast.7, f32[1,128]{1,0:T(1,128)S(1)} %bitcast.9, f32[1,128]{1,0:T(1,128)S(1)} %bitcast.10, bf16[64,4,128]{2,1,0:T(4,128)(2,1)S(1)} %all_to_all.11.r_ref, ...), custom_call_target="tpu_custom_call" | custom-call | tf_op jit(solution)/shard_map/analyse/pallas_call | solution.py:463
Async XLA Ops:
  0.6 42.0 %copy-start.3 = (bf16[64,256]{1,0:T(8,128)(2,1)S(1)}, bf16[64,256]{1,0:T(8,128)(2,1)}, u32[]{:S(2)}) copy-start(bf16[64,256]{1,0:T(8,128)(2,1)} %constant.14.clone.fourth_ref) | copy-start | bytes 98308
  0.6 42.0 %copy-start = (bf16[256,256]{1,0:T(8,128)(2,1)S(1)}, bf16[256,256]{1,0:T(8,128)(2,1)}, u32[]{:S(2)}) copy-start(bf16[256,256]{1,0:T(8,128)(2,1)} %constant.13.clone.third_ref) | copy-start | bytes 393220
  0.7 42.0 %copy-start.1 = (bf16[512,128]{1,0:T(8,128)(2,1)S(1)}, bf16[512,128]{1,0:T(8,128)(2,1)}, u32[]{:S(2)}) copy-start(bf16[512,128]{1,0:T(8,128)(2,1)} %constant.12.clone.second_ref) | copy-start | bytes 393220
  0.7 42.0 %copy-start.2 = (f32[2,64,128]{2,1,0:T(8,128)S(1)}, f32[2,64,128]{2,1,0:T(8,128)}, u32[]{:S(2)}) copy-start(f32[2,64,128]{2,1,0:T(8,128)} %constant.11.clone.twist_ref) | copy-start | bytes 196612
  0.7 42.0 %copy-start.4 = (bf16[128,128]{1,0:T(8,128)(2,1)S(1)}, bf16[128,128]{1,0:T(8,128)(2,1)}, u32[]{:S(2)}) copy-start(bf16[128,128]{1,0:T(8,128)(2,1)} %constant.10.clone.first_ref) | copy-start | bytes 98308
  0.7 63.6 %copy-start.6 = (s32[1024]{0:T(1024)S(1)}, s32[1024]{0:T(1024)}, u32[]{:S(2)}) copy-start(s32[1024]{0:T(1024)} %m_ref.1) | copy-start | bytes 12292
  0.7 63.6 %copy-start.8 = (f32[128]{0:T(128)S(1)}, f32[128]{0:T(128)}, u32[]{:S(2)}) copy-start(f32[128]{0:T(128)} %param.18) | copy-start | bytes 1540
  0.7 63.6 %copy-start.7 = (s32[128]{0:T(128)S(1)}, s32[128]{0:T(128)}, u32[]{:S(2)}) copy-start(s32[128]{0:T(128)} %param.17) | copy-start | bytes 1540
  0.7 42.0 %copy-start.5 = (s32[1,4096]{1,0:T(1,128)S(1)}, s32[1,4096]{1,0:T(1,128)}, u32[]{:S(2)}) copy-start(s32[1,4096]{1,0:T(1,128)} %param.20) | copy-start | bytes 49156
  0.7 63.5 %copy-start.9 = (f32[128]{0:T(128)S(1)}, f32[128]{0:T(128)}, u32[]{:S(2)}) copy-start(f32[128]{0:T(128)} %param.19) | copy-start | bytes 1540
  5.3 21.4 %collective-permute-start = (bf16[64,4,128]{2,1,0:T(4,128)(2,1)S(1)}, bf16[64,4,128]{2,1,0:T(4,128)(2,1)S(1)}, u32[]{:S(2)}, u32[]{:S(2)}) collective-permute-start(bf16[64,4,128]{2,1,0:T(4,128)(2,1)S(1)} %get-tuple-element.9), channel_id=1, source_target_pairs={{0,1},{1,0},{2,3},{3,2},{4,5},{5,4},{6,7},{7,6},{8,9},{9,8},{10,11... | collective-permute-start | bytes 196616 | tf_op jit(solution)/shard_map/ppermute | solution.py:490
  45.6 3.1 %collective-permute-start.1 = (bf16[64,2,128]{2,1,0:T(2,128)(2,1)S(1)}, bf16[64,2,128]{2,1,0:T(2,128)(2,1)S(1)}, u32[]{:S(2)}, u32[]{:S(2)}) collective-permute-start(bf16[64,2,128]{2,1,0:T(2,128)(2,1)S(1)} %get-tuple-element.11), channel_id=1, source_target_pairs={{0,1},{1,0},{2,3},{3,2},{4,5},{5,4},{6,7},{7,6},{8,9},{9,8},{10,11... | collective-permute-start | bytes 98312 | tf_op jit(solution)/shard_map/ppermute | solution.py:490

commit v5 on v4

v5 whole, which is shorter than its diff:
```python
import functools
import math

import jax
import jax.numpy as jnp
import numpy as np
from jax import lax
from jax.experimental import pallas as pl
from jax.experimental.pallas import tpu as pltpu
from jax.sharding import Mesh
from jax.sharding import PartitionSpec as P

F32 = jnp.float32
BF16 = jnp.bfloat16
LANES = 128
GRANT = 24 * 2**20
CHIP, CORE = "chip", "core"
NT = (((1,), (1,)), ((), ()))
NN = (((1,), (0,)), ((), ()))


def dot(a, b, dims=NN):
    return lax.dot_general(a, b, dims, preferred_element_type=F32)


def iota(shape, dim):
    return lax.broadcasted_iota(jnp.int32, shape, dim)


def small_column(m_ref, first, pairs):
    row = iota((pairs, 1), 0)
    column = jnp.zeros((pairs, 1), jnp.int32)
    for p in range(pairs):
        column = jnp.where(row == p, m_ref[first + p], column)
    return column


def layout_rows(small, modes):
    k = iota((small.shape[0], modes), 1)
    upper = k >= modes - small
    degree = jnp.where(upper, k - 1, small + k).astype(F32)
    orders = jnp.where(upper, modes - 1 - small, small).astype(F32)
    last_degree = jnp.full(small.shape, modes - 1, F32)
    last_orders = (modes - 1 - small).astype(F32)
    return (
        (degree, orders, raising(degree, orders)),
        (last_degree, last_orders, raising(last_degree, last_orders)),
    )


def raising(degree, orders):
    square = (
        (degree * degree - orders * orders)
        * (2.0 * degree + 1.0)
        / jnp.maximum(2.0 * degree - 1.0, 1.0)
    )
    return jnp.where(degree > orders, jnp.sqrt(jnp.where(degree > orders, square, 0.0)), 0.0)


def slot_of_cycle(order_ref):
    n = order_ref.shape[1]
    core = lax.axis_index(CORE)
    place = iota((n, n), 1)
    near = place < n // 2
    slot = 2 * (place % (n // 2)) + jnp.where(near, core, 1 - core)
    pick = jnp.where(iota((n, n), 0) == slot, 1.0, 0.0).astype(BF16)
    order = jnp.broadcast_to(order_ref[...].astype(F32), (8, n)).astype(BF16)
    return jnp.where(iota((n, n), 0).astype(F32) == dot(order, pick)[:1], 1.0, 0.0)


def first_pair(pairs):
    return (lax.axis_index(CHIP) * lax.axis_size(CORE) + lax.axis_index(CORE)) * pairs


def turn(values):
    rows = values.shape[0]
    real = iota(values.shape, 0) % 2 == 0
    return jnp.where(real, -pltpu.roll(values, rows - 1, 0), pltpu.roll(values, 1, 0))


def synth_kernel(
    m_hbm, order_hbm, colat_hbm, t_hbm, w_hbm, l_hbm, near_ref, far_ref, lr_ref, ltail_ref, small_ref,
    m_ref, order_ref, colat_ref, t_ref, w_ref, last_ref, c_ref, s_ref, deg_ref, eps_ref, up_ref, end_ref, lasts_ref, sems, *l_refs,
):
    pairs, sims = t_ref.shape[0], t_ref.shape[1]
    modes = t_ref.shape[3] - 1
    lines = 2 * sims
    steps = len(l_refs)
    chunk = modes // steps
    first = first_pair(pairs)
    wide = near_ref.shape[1] * near_ref.shape[2] // pairs
    cycles = last_ref.shape[2]

    pieces = [(m_hbm, m_ref), (order_hbm, order_ref), (colat_hbm, colat_ref), (w_hbm, w_ref), (t_hbm, t_ref)]
    pieces.append((l_hbm.at[pl.ds(modes, 1)], last_ref))
    pieces += [(l_hbm.at[pl.ds(j * chunk, chunk)], l_refs[j]) for j in range(steps)]
    copies = [pltpu.make_async_copy(*piece, sems.at[i]) for i, piece in enumerate(pieces)]
    for copy in copies:
        copy.start()
    for copy in copies[:3]:
        copy.wait()

    small = small_column(m_ref, first, pairs)
    (degree, _, eps), (_, _, last_eps) = layout_rows(small, modes)
    small_ref[...] = jnp.broadcast_to(small.astype(F32), small_ref.shape)
    deg_ref[...] = degree * (1.0 / modes)
    eps_ref[...] = eps * (1.0 / modes)
    last_eps = last_eps * (1.0 / modes)
    theta = colat_ref[...]
    cos, inv_sin = jnp.cos(theta), 1.0 / jnp.sin(theta)
    cycle_of_slot = slot_of_cycle(order_ref).T.astype(BF16)
    up_ref[...] = jnp.where(iota((pairs, modes), 1) >= modes - small, 1.0, 0.0)
    ends = iota((lines, modes), 1) == modes - 1

    copies[3].wait()
    copies[4].wait()
    def coefficients(p, _):
        tbar = t_ref[p].reshape(lines, modes + 1)
        wiener = w_ref[p].reshape(lines, modes + 1)
        main, last = wiener[:, :modes].astype(F32), wiener[:, modes:].astype(F32)
        raised = pltpu.roll(eps_ref[pl.ds(p, 1), :] * main, modes - 1, 1)
        raised = jnp.where(ends, end_ref[pl.ds(p, 1), :][:, :1] * last, raised)
        raised = jnp.concatenate([deg_ref[pl.ds(p, 1), :] * main, raised], axis=0).astype(BF16)
        upper = jnp.broadcast_to(up_ref[pl.ds(p, 1), :], (2 * lines, modes)).astype(BF16)
        for i, sets in enumerate((jnp.concatenate([tbar[:, :modes], wiener[:, :modes]], axis=0), raised)):
            c_ref[p, 2 * i * lines : 2 * (i + 1) * lines, :] = sets
            c_ref[p, 2 * (i + 2) * lines : 2 * (i + 3) * lines, :] = sets * upper
        lasts = jnp.concatenate(
            [tbar[:, modes:].astype(F32), last, ((modes - 1.0) / modes) * last, 0.0 * last], axis=0
        )
        lasts_ref[p] = jnp.broadcast_to(lasts.astype(BF16).astype(F32), lasts_ref.shape[1:])
        return 0

    end_ref[...] = jnp.broadcast_to(last_eps, end_ref.shape)
    lax.fori_loop(0, pairs, coefficients, 0, unroll=2)

    copies[5].wait()
    tail_rows = last_ref[0].astype(F32)
    ltail_ref[...] = tail_rows
    for j in range(steps + 1):
        if j < steps:
            copies[6 + j].wait()
            lr_ref[:, j * chunk : (j + 1) * chunk, :] = jnp.swapaxes(l_refs[j][...], 0, 1)
        if j == 0:
            continue
        at = slice((j - 1) * chunk, j * chunk)
        for p in range(0, pairs, 2):
            both = jnp.concatenate([c_ref[p, :, at], c_ref[p + 1, :, at]], axis=0)
            sums = dot(both, jnp.concatenate([lr_ref[p, at, :], lr_ref[p + 1, at, :]], axis=1))
            for i in range(2):
                part = sums[i * 8 * lines : (i + 1) * 8 * lines, i * cycles : (i + 1) * cycles]
                s_ref[p + i] = part if j == 1 else s_ref[p + i] + part

    blocks = []
    for p in range(pairs):
        small = m_ref[first + p]
        for half, order in enumerate((small, modes - 1 - small)):
            above = s_ref[p, 4 * lines :, :]
            sums = above + lasts_ref[p] * tail_rows[p : p + 1, :] if half else s_ref[p, : 4 * lines, :] - above
            s0, s1, s2, s3 = (sums[q * lines : (q + 1) * lines] for q in range(4))
            weight = jnp.where(order == 0, 1.0, 2.0) * modes ** (-0.5)
            ratio = order.astype(F32) * (1.0 / modes)
            blocks.append(s0 * weight)
            blocks.append((cos * s2 - s3) * inv_sin * weight)
            blocks.append(turn(s1) * ratio * inv_sin * weight)
        row = iota((wide - 6 * lines, s_ref.shape[2]), 0)
        low, high = (small % LANES).astype(F32), (small // LANES).astype(F32)
        blocks.append(jnp.where(row == 0, low, jnp.where(row == 1, high, 0.0)))
    fourier = jnp.concatenate(blocks, axis=0).astype(BF16)
    out = dot(cycle_of_slot, fourier, NT).astype(BF16)
    near_ref[...] = out[: cycles // 2].reshape(near_ref.shape)
    far_ref[...] = out[cycles // 2 :].reshape(far_ref.shape)


def synth(tbar_alm, twf_alm, table, m_slots, cycle_order, colatitude):
    pairs, sims, _, rows = tbar_alm.shape
    modes = rows - 1
    cycles = table.shape[2]
    lines = 2 * sims
    wide = 8 * lines
    steps = 4
    vmem = pl.BlockSpec(memory_space=pltpu.VMEM)
    hbm = pl.BlockSpec(memory_space=pltpu.HBM)
    return pl.pallas_call(
        synth_kernel,
        in_specs=[hbm] * 6,
        out_specs=[vmem] * 5,
        out_shape=[
            pltpu.VMEM((cycles // 2, pairs * wide // LANES, LANES), BF16),
            pltpu.VMEM((cycles // 2, pairs * wide // LANES, LANES), BF16),
            pltpu.VMEM((pairs, modes, cycles), BF16),
            pltpu.VMEM((pairs, cycles), F32),
            pltpu.VMEM((pairs, LANES), F32),
        ],
        scratch_shapes=[
            pltpu.SMEM(m_slots.shape, jnp.int32),
            pltpu.VMEM((1, cycles), jnp.int32),
            pltpu.VMEM((1, cycles), F32),
            pltpu.VMEM(tbar_alm.shape, BF16),
            pltpu.VMEM(twf_alm.shape, BF16),
            pltpu.VMEM((1, pairs, cycles), BF16),
            pltpu.VMEM((pairs, 8 * lines, modes), BF16),
            pltpu.VMEM((pairs, 8 * lines, cycles), F32),
            pltpu.VMEM((pairs, modes), F32),
            pltpu.VMEM((pairs, modes), F32),
            pltpu.VMEM((pairs, modes), F32),
            pltpu.VMEM((pairs, LANES), F32),
            pltpu.VMEM((pairs, 4 * lines, cycles), F32),
            pltpu.SemaphoreType.DMA((steps + 6,)),
        ]
        + [pltpu.VMEM((modes // steps, pairs, cycles), BF16)] * steps,
        compiler_params=pltpu.CompilerParams(vmem_limit_bytes=GRANT),
        name="synth",
    )(*(pltpu.with_memory_space_constraint(x, pltpu.HBM) for x in (
        m_slots, cycle_order.reshape(1, -1), colatitude.reshape(1, -1), tbar_alm, twf_alm, table
    )))


def angles(left, right, period):
    return 2.0 * np.pi * (np.outer(left, right) % period) / period


def split(table):
    high = table.astype(np.float32).astype(jnp.bfloat16)
    return high, (table - high.astype(np.float64)).astype(np.float32).astype(jnp.bfloat16)


def sky_tables(modes, pixels):
    small = pixels // LANES
    m1, j2, m2 = np.arange(LANES), np.arange(small), np.arange(modes // LANES)
    j1 = np.arange(LANES).reshape(-1, LANES // small).T.reshape(-1)
    th = angles(j2, m2, small).reshape(small, 2, -1)
    c, s = np.cos(th), np.sin(th)
    first = np.stack([np.stack([c, -s], 2), np.stack([s, c], 2)], 0).reshape(2 * small, -1)
    th = angles(j2, m1, pixels)
    twist = np.stack([np.cos(th), np.sin(th)])
    th = angles(m1, j1, LANES)
    second = np.concatenate([np.cos(th), -np.sin(th)], 0)
    third = np.concatenate([np.cos(th.T), -np.sin(th.T)], 1)
    th = angles(m2, j2, small).reshape(2, -1, small)
    c, s = np.cos(th), np.sin(th)
    fourth = np.stack([np.concatenate([c, s], 2), np.concatenate([-s, c], 2)], 1)
    fourth = fourth.reshape(2 * modes // LANES, -1)
    return (
        np.concatenate(split(first), 1), twist.astype(np.float32), np.concatenate(split(second), 0),
        np.concatenate(split(third), 0), np.concatenate(split(fourth), 1),
    )


def near_then_far(ref):
    chips, parts, lanes = ref.shape
    halves = (ref[:, : parts // 2], ref[:, parts // 2 :])
    return jnp.concatenate([h.reshape(chips, parts // 2 * lanes) for h in halves], axis=0)


def sky_kernel(
    pairs, sims, x_ref, mask_ref, first_ref, twist_ref, second_ref, third_ref, fourth_ref, near_ref, far_ref,
    xt_ref, lhs_ref, hot_ref,
):
    devices = 2 * x_ref.shape[0]
    wide = x_ref.shape[1] * x_ref.shape[2] // 2 // pairs
    lines = 2 * sims
    small = twist_ref.shape[1]
    pixels = small * LANES
    tall = fourth_ref.shape[0] // 4
    xt_ref[...] = near_then_far(x_ref).astype(F32).T

    n = 2 * tall
    groups = 3 * sims
    sorted_halves, places = [], []
    for half in range(2):
        place = []
        for p in range(pairs):
            at = p * wide + 6 * lines
            low, high = (xt_ref[at + i : at + i + 1, :].astype(jnp.int32) for i in range(2))
            if half:
                low, high = LANES - 1 - low, tall - 1 - high
            place.append(iota((tall, devices), 0) == high)
            tile = slice(p * devices, (p + 1) * devices)
            hot_ref[half, :, tile] = jnp.where(iota((LANES, devices), 0) == low, 1.0, 0.0).astype(BF16)
            parts = []
            for row in range(3 * lines):
                at = p * wide + half * 3 * lines + row
                parts.append(jnp.where(place[p], xt_ref[at : at + 1, :], 0.0))
            lhs_ref[:, tile] = jnp.concatenate(parts, axis=0).astype(BF16)
        places.append(place)
        sorted_halves.append(dot(lhs_ref[...], hot_ref[half], NT).astype(BF16))

    spread = jnp.concatenate(
        [
            jnp.concatenate([s[g * n : (g + 1) * n] for s in sorted_halves], axis=0)
            for g in range(groups)
        ],
        axis=1,
    )
    stage = dot(first_ref[...], jnp.concatenate([spread, spread], axis=0))
    cos, sin = twist_ref[0], twist_ref[1]
    twisted = []
    for g in range(groups):
        re, im = (stage[i * small : (i + 1) * small, g * LANES : (g + 1) * LANES] for i in range(2))
        twisted.append(jnp.concatenate([re * cos - im * sin, re * sin + im * cos], axis=1))
    twisted = jnp.concatenate(twisted, axis=0).astype(BF16)
    maps = dot(twisted, second_ref[: 2 * LANES]) + dot(twisted, second_ref[2 * LANES :])

    mask = mask_ref[...].astype(F32).T
    mask = jnp.concatenate([mask[i * small : (i + 1) * small] for i in range(LANES // small)], axis=1)
    products = []
    for q in range(1, 3):
        for s in range(sims):
            at = (q * sims + s) * small
            products.append(mask * maps[s * small : (s + 1) * small] * maps[at : at + small])
    products = jnp.concatenate(products, axis=0).astype(BF16)
    stage = dot(products, third_ref[:LANES]) + dot(products, third_ref[LANES:])
    groups = 2 * sims
    twisted = []
    for g in range(groups):
        re, im = (stage[g * small : (g + 1) * small, i * LANES : (i + 1) * LANES] for i in range(2))
        twisted.append(jnp.concatenate([re * cos + im * sin, im * cos - re * sin], axis=0))
    twisted = jnp.concatenate(twisted, axis=1).astype(BF16)
    spectra = dot(fourth_ref[...], jnp.concatenate([twisted, twisted], axis=0)) * pixels ** (-0.5)
    spectra = spectra.astype(BF16)

    rows, columns = 2 * groups, 2 * groups * tall
    add = jnp.where(iota((rows, columns), 1) // tall == iota((rows, columns), 0), 1.0, 0.0).astype(BF16)
    found = []
    for half in range(2):
        stacked = jnp.concatenate(
            [spectra[half * n : (half + 1) * n, g * LANES : (g + 1) * LANES] for g in range(groups)], axis=0
        )
        values = dot(stacked, hot_ref[half])
        for p in range(pairs):
            tile = slice(p * devices, (p + 1) * devices)
            keep = jnp.concatenate([places[half][p]] * rows, axis=0)
            lhs_ref[:columns, tile] = jnp.where(keep, values[:, tile], 0.0).astype(BF16)
        found.append(dot(add, lhs_ref[:columns, :]))
    blocks = [found[half][:, p * devices : (p + 1) * devices] for p in range(pairs) for half in range(2)]
    out = jnp.concatenate(blocks, axis=0).T.astype(BF16)
    near_ref[...] = out[: devices // 2].reshape(near_ref.shape)
    far_ref[...] = out[devices // 2 :].reshape(far_ref.shape)


def sky(received, pixel_mask, pairs, sims, modes):
    devices = 2 * received.shape[0]
    pixels = pixel_mask.shape[1]
    tables = sky_tables(modes, pixels)
    vmem = pl.BlockSpec(memory_space=pltpu.VMEM)
    tall = modes // LANES // 2
    return pl.pallas_call(
        functools.partial(sky_kernel, pairs, sims),
        in_specs=[vmem] * 7,
        out_specs=[vmem] * 2,
        out_shape=[pltpu.VMEM((devices // 2, pairs * 8 * sims // LANES, LANES), BF16)] * 2,
        scratch_shapes=[
            pltpu.VMEM((received.shape[1] // 2 * LANES, devices), F32),
            pltpu.VMEM((6 * sims * tall, pairs * devices), BF16),
            pltpu.VMEM((2, LANES, pairs * devices), BF16),
        ],
        compiler_params=pltpu.CompilerParams(vmem_limit_bytes=GRANT),
        name="sky",
    )(received, pixel_mask.reshape(-1, LANES), *(jnp.asarray(t) for t in tables))


def rows_kernel(
    small_ref, order_ref, colat_ref, weight_ref, table_ref, _, row_ref, end_ref, hot_ref, with_ref, flip_ref
):
    pairs, modes, cycles = row_ref.shape[1], row_ref.shape[3], end_ref.shape[2]
    small = small_ref[:, :1].astype(jnp.int32)
    main, last = layout_rows(small, modes)
    for i, ref in enumerate((row_ref, end_ref)):
        degree, orders, eps = (main, last)[i]
        scale = (modes / cycles) ** 0.5 / jnp.sqrt(jnp.maximum(degree * (degree + 1.0), 1.0))
        for j, values in enumerate((degree * scale, eps * scale, orders * scale)):
            if i:
                ref[j] = jnp.broadcast_to(values, ref.shape[1:])
            else:
                for p in range(pairs):
                    ref[j, p] = jnp.broadcast_to(values[p : p + 1], ref.shape[2:])
    late = flip_ref.shape[0]
    for p in range(late):
        flip_ref[p] = table_ref[pairs - late + p].T
    hot_ref[...] = slot_of_cycle(order_ref).astype(BF16)
    theta, weight = colat_ref[...], weight_ref[...]
    with_ref[0] = jnp.broadcast_to(weight * jnp.cos(theta) / jnp.sin(theta), with_ref.shape[1:])
    with_ref[1] = jnp.broadcast_to(weight / jnp.sin(theta), with_ref.shape[1:])


def layout(small, cycle_order, colatitude, cycle_weight, table, late, after, lines, modes):
    pairs = small.shape[0]
    cycles = cycle_order.shape[0]
    vmem = pl.BlockSpec(memory_space=pltpu.VMEM)
    return pl.pallas_call(
        rows_kernel,
        in_specs=[vmem] * 6,
        out_specs=[vmem] * 5,
        out_shape=[
            pltpu.VMEM((3, pairs, lines, modes), F32), pltpu.VMEM((3, pairs, cycles), F32),
            pltpu.VMEM((cycles, cycles), BF16), pltpu.VMEM((2, lines, cycles), F32),
            pltpu.VMEM((late, cycles, modes), BF16),
        ],
        compiler_params=pltpu.CompilerParams(vmem_limit_bytes=GRANT),
        cost_estimate=pl.CostEstimate(flops=10**9, bytes_accessed=10**6, transcendentals=10**5),
        name="layout",
    )(small, cycle_order.reshape(1, -1), colatitude.reshape(1, -1), cycle_weight.reshape(1, -1), table, after)


def flip_kernel(table_ref, _, out_ref):
    for p in range(out_ref.shape[0]):
        out_ref[p] = table_ref[p].T


def flip(table, pairs, after):
    _, modes, cycles = table.shape
    vmem = pl.BlockSpec(memory_space=pltpu.VMEM)
    return pl.pallas_call(
        flip_kernel,
        in_specs=[vmem] * 2,
        out_specs=vmem,
        out_shape=pltpu.VMEM((pairs, cycles, modes), BF16),
        compiler_params=pltpu.CompilerParams(vmem_limit_bytes=GRANT),
        cost_estimate=pl.CostEstimate(flops=10**9, bytes_accessed=10**6, transcendentals=0),
        name="flip",
    )(table, after)


def analyse_kernel(
    small_ref, r_ref, l_ref, l2_ref, tail_ref, row_ref, end_ref, hot_ref, with_ref, grad_hbm, curl_hbm,
    w_ref, grad_ref, curl_ref, sems,
):
    pairs, lines, modes = row_ref.shape[1:]
    cycles = l_ref.shape[1]
    sims = lines // 2
    high = 6 * lines

    spectra = dot(near_then_far(r_ref).astype(F32).T.astype(BF16), hot_ref[...], NT)
    with_cos, with_sin = with_ref[0], with_ref[1]
    blank = jnp.zeros((high, cycles), F32)
    for i in range(pairs):
        for half in range(2):
            at = (i * 2 + half) * 2 * lines
            parts, turned = [], []
            for values in (spectra[at : at + lines], spectra[at + lines : at + 2 * lines]):
                parts += [values * with_cos, values * with_sin]
                turned.append(turn(parts[-1]))
            parts = jnp.concatenate(parts + turned, axis=0)
            at = ((i % 2) * 2 + half) * high
            w_ref[i // 2, at : at + high] = jnp.concatenate(
                [blank, parts] if i % 2 else [parts, blank], axis=1
            ).astype(BF16)

    k = iota((lines, modes), 1)
    starts = k == 0

    def previous(values):
        return jnp.where(starts, 0.0, pltpu.roll(values, 1, 1))

    copies = []
    for p in range(pairs):
        odd = p % 2
        if not odd:
            ref, at = (l_ref, p) if p < l_ref.shape[0] else (l2_ref, p - l_ref.shape[0])
            tables = jnp.concatenate([ref[at], ref[at + 1]], axis=0)
            both = dot(w_ref[p // 2], tables)
        sums = both[odd * 2 * high : (odd + 1) * 2 * high]
        upper = k >= modes - small_ref[p : p + 1, :1].astype(jnp.int32)
        a0, a1, a2, a3, t1, t3 = (
            jnp.where(upper, sums[high + q * lines : high + (q + 1) * lines], sums[q * lines : (q + 1) * lines])
            for q in range(6)
        )
        level, raised, azimuth = (row_ref[i, p] for i in range(3))
        grad = level * a0 - raised * previous(a1) - azimuth * t3
        curl = level * a2 - raised * previous(a3) + azimuth * t1
        weighted = w_ref[p // 2, (2 * odd + 1) * high : (2 * odd + 2) * high, odd * cycles : (odd + 1) * cycles]
        last = jnp.sum(weighted.astype(F32) * tail_ref[p : p + 1, :], axis=1, keepdims=True)
        level, raised, azimuth = (end_ref[i, p : p + 1, :1] for i in range(3))
        b0, b1, b2, b3, u1, u3 = (last[q * lines : (q + 1) * lines] for q in range(6))
        last_grad = level * b0 - raised * a1[:, modes - 1 :] - azimuth * u3
        last_curl = level * b2 - raised * a3[:, modes - 1 :] + azimuth * u1
        for ref, hbm, main, last in ((grad_ref, grad_hbm, grad, last_grad), (curl_ref, curl_hbm, curl, last_curl)):
            ref[p, :, :, :modes] = main.reshape(sims, 2, modes)
            ref[p, :, :, modes:] = last.reshape(sims, 2, 1)
            copies.append(pltpu.make_async_copy(ref.at[p], hbm.at[p], sems.at[len(copies)]))
            copies[-1].start()
    for copy in copies:
        copy.wait()


def analyse(returned, tables, tail, small, rows, ends, hot, weights):
    _, pairs, lines, modes = rows.shape
    cycles = hot.shape[0]
    vmem = pl.BlockSpec(memory_space=pltpu.VMEM)
    hbm = pl.BlockSpec(memory_space=pltpu.HBM)
    shape = (pairs, lines // 2, 2, modes + 1)
    out = jax.ShapeDtypeStruct(shape, F32)
    return pl.pallas_call(
        analyse_kernel,
        in_specs=[vmem] * 9,
        out_specs=[hbm, hbm],
        out_shape=[out, out],
        scratch_shapes=[
            pltpu.VMEM((pairs // 2, 24 * lines, 2 * cycles), BF16),
            pltpu.VMEM(shape, F32),
            pltpu.VMEM(shape, F32),
            pltpu.SemaphoreType.DMA((2 * pairs,)),
        ],
        compiler_params=pltpu.CompilerParams(vmem_limit_bytes=GRANT),
        name="analyse",
    )(small, returned, *tables, tail, rows, ends, hot, weights)


def merge_kernel(near_ref, far_ref, *refs):
    out_ref = refs[-1]
    parts = near_ref.shape[1]
    out_ref[:, :parts] = near_ref[...]
    out_ref[:, parts:] = far_ref[...]


def exchange(near, far, *beside):
    vmem = pl.BlockSpec(memory_space=pltpu.VMEM)
    swapped = lax.ppermute(far, CORE, [(0, 1), (1, 0)])
    chips, parts, lanes = near.shape
    both = pl.pallas_call(
        merge_kernel,
        in_specs=[vmem] * (2 + len(beside)),
        out_specs=vmem,
        out_shape=pltpu.VMEM((chips, 2 * parts, lanes), near.dtype),
        compiler_params=pltpu.CompilerParams(vmem_limit_bytes=GRANT),
        name="merge",
    )(near, swapped, *beside)
    return lax.all_to_all(both, CHIP, 0, 0, tiled=True)


def shards(tbar_alm, twf_alm, legendre, m_slots, cycle_order, colatitude, cycle_weight, pixel_mask):
    pairs, sims, _, rows = tbar_alm.shape
    by_row = jnp.transpose(legendre, (1, 0, 2))
    near, far, table, tail, small = synth(tbar_alm, twf_alm, by_row, m_slots, cycle_order, colatitude)
    early = pairs // 4 * 3
    flipped = flip(table, early, near)
    near, far = sky(exchange(near, far, flipped), pixel_mask, pairs, sims, rows - 1)
    factors, ends, hot, weights, others = layout(
        small, cycle_order, colatitude, cycle_weight, table, pairs - early, near, 2 * sims, rows - 1
    )
    returned = exchange(near, far, ends)
    return analyse(returned, (flipped, others), tail, small, factors, ends, hot, weights)


def solution(mesh):
    devices = mesh.devices.reshape(mesh.shape["grp"], -1, 2)
    finer = Mesh(devices, ("grp", CHIP, CORE))
    ma = (CHIP, CORE)
    coefficients = P(ma, "grp", None, None)
    return jax.shard_map(
        shards,
        mesh=finer,
        in_specs=(coefficients, coefficients, P(ma, None, None), P(), P(), P(), P(), P(ma, None)),
        out_specs=(coefficients, coefficients),
        check_vma=False,
    )
```

time: 67.8 us -> 65.6 us (0.968)
  waiting for transfers between devices: 1.76 us -> 0.32 us
  Pallas kernels: 10.9 us -> 10.1 us
    ppermute x2, waiting for transfers between devices: 1.76 us -> 0.32 us  [exchange(): swapped = lax.ppermute(far, CORE, [(0, 1), (1, 0)])]
    pallas_call x1, Pallas kernels: 2.83 us -> 2.09 us  [sky(): pl.pallas_call(functools.partial(sky_kernel, pairs, sims), in_specs=[vmem...]
    pallas_call x4 -> x6, Pallas kernels: 8.03 us -> 7.97 us  [the longest x1 4.12 us: synth(): pl.pallas_call(synth_kernel, in_specs=[hbm] * 6, out_specs=[vmem] * 5, ou...]
  transfers between devices with their start and end apart: 2 -> 2, of which waited for: 2 -> 1; matrix products, arithmetic and copies ran while one was open for 0% -> 0% of each run, Pallas kernels for 0% -> 2%
where the time goes in v5:
time: 65.6 us; the launch traced here: 65.4 us
  blocking collectives  31.5 us (48%)
  starting transfers between devices  22.7 us (35%)
  Pallas kernels  10.1 us (15%)
  between operations  0.75 us (1%)
    all_to_all x2, blocking collectives, exchange(): return lax.all_to_all(both, CHIP, 0, 0, tiled=True)  31.5 us
    ppermute x2, starting transfers between devices, exchange(): swapped = lax.ppermute(far, CORE, [(0, 1), (1, 0)])  22.7 us
    pallas_call x1, Pallas kernels, synth(): pl.pallas_call(synth_kernel, in_specs=[hbm] * 6, out_specs=[vmem] * 5, ou...  4.12 us
    pallas_call x1, Pallas kernels, analyse(): pl.pallas_call(analyse_kernel, in_specs=[vmem] * 9, out_specs=[hbm, hbm],...  2.3 us
    pallas_call x1, Pallas kernels, sky(): pl.pallas_call(functools.partial(sky_kernel, pairs, sims), in_specs=[vmem...  2.09 us
  transfers between devices with their start and end apart: 2, of which 1 were waited for; matrix products, arithmetic and copies ran while one was open for 0% of the time, Pallas kernels for 2%

profile of v5, /device:TPU:513, one launch (start us, length us, event | category | flops | bytes accessed | tf_op | source)
XLA Modules:
  0.0 65.4 jit_solution(14739044984961434488)
XLA Ops:
  0.6 4.1 %synth.1 = (bf16[64,4,128]{2,1,0:T(4,128)(2,1)S(1)}, bf16[64,4,128]{2,1,0:T(4,128)(2,1)S(1)}, bf16[8,2048,128]{2,1,0:T(8,128)(2,1)S(1)}, f32[8,128]{1,0:T(8,128)S(1)}, f32[8,128]{1,0:T(8,128)S(1)}) custom-call(s32[1024]{0:T(1024)} %m_hbm.1, s32[1,128]{1,0:T(1,128)} %bitcast.6, f32[1,128]{1,0:T(1,128)} %bitcast.8, bf16[8,4,2,2049]{3,2,1,0:T(2,128)(2,1)} %t_hbm.1, ...), custom_call_target="tpu_custom_call" | custom-call | tf_op jit(solution)/shard_map/synth/pallas_call | solution.py:184
  4.8 20.5 %collective-permute-start = (bf16[64,4,128]{2,1,0:T(4,128)(2,1)S(1)}, bf16[64,4,128]{2,1,0:T(4,128)(2,1)S(1)}, u32[]{:S(2)}, u32[]{:S(2)}) collective-permute-start(bf16[64,4,128]{2,1,0:T(4,128)(2,1)S(1)} %get-tuple-element.16), channel_id=1, source_target_pairs={{0,1},{1,0},{2,3},{3,2},{4,5},{5,4},{6,7},{7,6},{8,9},{9,8},{10,11... | collective-permute-start | bytes 196616 | tf_op jit(solution)/shard_map/ppermute | solution.py:519
  25.3 0.0 copy-start
  25.3 0.0 copy-start.1
  25.3 0.0 copy-start.2
  25.3 0.0 copy-start.3
  25.3 0.0 copy-start.4
  25.3 0.0 copy-start.5
  25.3 0.0 copy-start.6
  25.3 0.0 copy-start.7
  25.4 0.0 copy-start.8
  25.4 0.9 %flip.1.refs_0_.l_ref = bf16[6,128,2048]{2,1,0:T(8,128)(2,1)S(1)} custom-call(bf16[8,2048,128]{2,1,0:T(8,128)(2,1)S(1)} %get-tuple-element.17.table_ref, bf16[64,4,128]{2,1,0:T(4,128)(2,1)S(1)} %get-tuple-element.15._.near_ref), custom_call_target="tpu_custom_call" | custom-call | flops 1000000000 | bytes 1000000 | tf_op jit(solution)/shard_map/flip/pallas_call | solution.py:414
  26.2 0.0 collective-permute-done.far_ref
  26.2 0.1 merge.2
  26.3 15.9 %all_to_all.10.x_ref = bf16[64,8,128]{2,1,0:T(8,128)(2,1)S(1)} all-to-all(bf16[64,8,128]{2,1,0:T(8,128)(2,1)S(1)} %merge.2), channel_id=1, replica_groups=mesh['grp'=2,'chip'=64,'core'=2] {'chip'}, dimensions={0} | all-to-all | bytes 262144 | tf_op jit(solution)/shard_map/all_to_all | solution.py:529
  42.3 0.0 copy-done
  42.3 0.0 copy-done.1
  42.3 0.0 copy-done.2
  42.3 0.0 copy-done.3
  42.3 0.0 copy-done.4
  42.3 0.0 copy-done.5
  42.3 2.1 %sky.1 = (bf16[64,2,128]{2,1,0:T(2,128)(2,1)S(1)}, bf16[64,2,128]{2,1,0:T(2,128)(2,1)S(1)}) custom-call(bf16[64,8,128]{2,1,0:T(8,128)(2,1)S(1)} %all_to_all.10.x_ref, s32[32,128]{1,0:T(8,128)S(1)} %bitcast.5, bf16[64,64]{1,0:T(8,128)(2,1)S(1)} %copy-done.4, f32[2,32,128]{2,1,0:T(8,128)S(1)} %copy-done.2, bf16[512,128]{1,0:T(8,128)(2,1)S(1)} %copy-done.1, ...), custom_call_target="tpu_custom_call" | custom-call | tf_op jit(solution)/shard_map/sky/pallas_call | solution.py:348
  44.4 2.2 %collective-permute-start.1 = (bf16[64,2,128]{2,1,0:T(2,128)(2,1)S(1)}, bf16[64,2,128]{2,1,0:T(2,128)(2,1)S(1)}, u32[]{:S(2)}, u32[]{:S(2)}) collective-permute-start(bf16[64,2,128]{2,1,0:T(2,128)(2,1)S(1)} %get-tuple-element.19), channel_id=1, source_target_pairs={{0,1},{1,0},{2,3},{3,2},{4,5},{5,4},{6,7},{7,6},{8,9},{9,8},{10,11... | collective-permute-start | bytes 98312 | tf_op jit(solution)/shard_map/ppermute | solution.py:519
  46.6 0.0 copy-done.6
  46.6 0.0 copy-done.7
  46.6 0.0 copy-done.8
  46.6 0.5 layout.1
  47.1 0.3 collective-permute-done.1.far_ref
  47.5 0.1 merge.3
  47.5 15.6 %all_to_all.11.r_ref = bf16[64,4,128]{2,1,0:T(4,128)(2,1)S(1)} all-to-all(bf16[64,4,128]{2,1,0:T(4,128)(2,1)S(1)} %merge.3), channel_id=1, replica_groups=mesh['grp'=2,'chip'=64,'core'=2] {'chip'}, dimensions={0} | all-to-all | bytes 131072 | tf_op jit(solution)/shard_map/all_to_all | solution.py:529
  63.1 2.3 %analyse.1 = (f32[8,4,2,2049]{3,2,1,0:T(2,128)}, f32[8,4,2,2049]{3,2,1,0:T(2,128)}) custom-call(f32[8,128]{1,0:T(8,128)S(1)} %get-tuple-element.14.small_ref, bf16[64,4,128]{2,1,0:T(4,128)(2,1)S(1)} %all_to_all.11.r_ref, bf16[6,128,2048]{2,1,0:T(8,128)(2,1)S(1)} %flip.1.refs_0_.l_ref, bf16[2,128,2048]{2,1,0:T(8,128)(2,1)S(1)} %get-tuple-element.21.l2_ref, ...), custom_call_target="tpu_custom_call" | custom-call | tf_op jit(solution)/shard_map/analyse/pallas_call | solution.py:494
Async XLA Ops:
  4.8 21.5 %collective-permute-start = (bf16[64,4,128]{2,1,0:T(4,128)(2,1)S(1)}, bf16[64,4,128]{2,1,0:T(4,128)(2,1)S(1)}, u32[]{:S(2)}, u32[]{:S(2)}) collective-permute-start(bf16[64,4,128]{2,1,0:T(4,128)(2,1)S(1)} %get-tuple-element.16), channel_id=1, source_target_pairs={{0,1},{1,0},{2,3},{3,2},{4,5},{5,4},{6,7},{7,6},{8,9},{9,8},{10,11... | collective-permute-start | bytes 196616 | tf_op jit(solution)/shard_map/ppermute | solution.py:519
  25.3 17.0 %copy-start = (bf16[256,256]{1,0:T(8,128)(2,1)S(1)}, bf16[256,256]{1,0:T(8,128)(2,1)}, u32[]{:S(2)}) copy-start(bf16[256,256]{1,0:T(8,128)(2,1)} %constant.13.clone.third_ref) | copy-start | bytes 393220
  25.3 17.0 %copy-start.1 = (bf16[512,128]{1,0:T(8,128)(2,1)S(1)}, bf16[512,128]{1,0:T(8,128)(2,1)}, u32[]{:S(2)}) copy-start(bf16[512,128]{1,0:T(8,128)(2,1)} %constant.12.clone.second_ref) | copy-start | bytes 393220
  25.3 17.0 %copy-start.2 = (f32[2,32,128]{2,1,0:T(8,128)S(1)}, f32[2,32,128]{2,1,0:T(8,128)}, u32[]{:S(2)}) copy-start(f32[2,32,128]{2,1,0:T(8,128)} %constant.11.clone.twist_ref) | copy-start | bytes 98308
  25.3 17.0 %copy-start.3 = (s32[1,4096]{1,0:T(1,128)S(1)}, s32[1,4096]{1,0:T(1,128)}, u32[]{:S(2)}) copy-start(s32[1,4096]{1,0:T(1,128)} %param.20) | copy-start | bytes 49156
  25.3 17.0 %copy-start.4 = (bf16[64,64]{1,0:T(8,128)(2,1)S(1)}, bf16[64,64]{1,0:T(8,128)(2,1)}, u32[]{:S(2)}) copy-start(bf16[64,64]{1,0:T(8,128)(2,1)} %constant.10.clone.first_ref) | copy-start | bytes 24580
  25.3 17.0 %copy-start.5 = (bf16[32,128]{1,0:T(8,128)(2,1)S(1)}, bf16[32,128]{1,0:T(8,128)(2,1)}, u32[]{:S(2)}) copy-start(bf16[32,128]{1,0:T(8,128)(2,1)} %constant.14.clone.fourth_ref) | copy-start | bytes 24580
  25.3 21.3 %copy-start.6 = (s32[128]{0:T(128)S(1)}, s32[128]{0:T(128)}, u32[]{:S(2)}) copy-start(s32[128]{0:T(128)} %param.17) | copy-start | bytes 1540
  25.3 21.3 %copy-start.7 = (f32[128]{0:T(128)S(1)}, f32[128]{0:T(128)}, u32[]{:S(2)}) copy-start(f32[128]{0:T(128)} %param.18) | copy-start | bytes 1540
  25.4 21.2 %copy-start.8 = (f32[128]{0:T(128)S(1)}, f32[128]{0:T(128)}, u32[]{:S(2)}) copy-start(f32[128]{0:T(128)} %param.19) | copy-start | bytes 1540
  44.4 3.1 %collective-permute-start.1 = (bf16[64,2,128]{2,1,0:T(2,128)(2,1)S(1)}, bf16[64,2,128]{2,1,0:T(2,128)(2,1)S(1)}, u32[]{:S(2)}, u32[]{:S(2)}) collective-permute-start(bf16[64,2,128]{2,1,0:T(2,128)(2,1)S(1)} %get-tuple-element.19), channel_id=1, source_target_pairs={{0,1},{1,0},{2,3},{3,2},{4,5},{5,4},{6,7},{7,6},{8,9},{9,8},{10,11... | collective-permute-start | bytes 98312 | tf_op jit(solution)/shard_map/ppermute | solution.py:519

commit v6 on v5

--- a/solution.py
+++ b/solution.py
@@ -14,6 +14,7 @@
 BF16 = jnp.bfloat16
 LANES = 128
 GRANT = 24 * 2**20
+STRIDE = 9
 CHIP, CORE = "chip", "core"
 NT = (((1,), (1,)), ((), ()))
 NN = (((1,), (0,)), ((), ()))
@@ -25,6 +26,10 @@
 
 def iota(shape, dim):
     return lax.broadcasted_iota(jnp.int32, shape, dim)
+
+
+def across(tiles):
+    return jnp.concatenate(list(tiles), axis=1)
 
 
 def small_column(m_ref, first, pairs):
@@ -80,7 +85,7 @@
 
 def synth_kernel(
     m_hbm, order_hbm, colat_hbm, t_hbm, w_hbm, l_hbm, near_ref, far_ref, lr_ref, ltail_ref, small_ref,
-    m_ref, order_ref, colat_ref, t_ref, w_ref, last_ref, c_ref, s_ref, deg_ref, eps_ref, up_ref, end_ref, lasts_ref, sems, *l_refs,
+    m_ref, order_ref, colat_ref, t_ref, w_ref, last_ref, c_ref, s_ref, deg_ref, eps_ref, up_ref, end_ref, lasts_ref, f_ref, sems, *l_refs,
 ):
     pairs, sims = t_ref.shape[0], t_ref.shape[1]
     modes = t_ref.shape[3] - 1
@@ -123,8 +128,11 @@
         raised = jnp.concatenate([deg_ref[pl.ds(p, 1), :] * main, raised], axis=0).astype(BF16)
         upper = jnp.broadcast_to(up_ref[pl.ds(p, 1), :], (2 * lines, modes)).astype(BF16)
         for i, sets in enumerate((jnp.concatenate([tbar[:, :modes], wiener[:, :modes]], axis=0), raised)):
-            c_ref[p, 2 * i * lines : 2 * (i + 1) * lines, :] = sets
-            c_ref[p, 2 * (i + 2) * lines : 2 * (i + 3) * lines, :] = sets * upper
+            above = sets * upper
+            for t in range(modes // LANES):
+                tile = slice(t * LANES, (t + 1) * LANES)
+                c_ref[p, t, 2 * i * lines : 2 * (i + 1) * lines] = sets[:, tile]
+                c_ref[p, t, 2 * (i + 2) * lines : 2 * (i + 3) * lines] = above[:, tile]
         lasts = jnp.concatenate(
             [tbar[:, modes:].astype(F32), last, ((modes - 1.0) / modes) * last, 0.0 * last], axis=0
         )
@@ -137,19 +145,22 @@
     copies[5].wait()
     tail_rows = last_ref[0].astype(F32)
     ltail_ref[...] = tail_rows
-    for j in range(steps + 1):
-        if j < steps:
-            copies[6 + j].wait()
-            lr_ref[:, j * chunk : (j + 1) * chunk, :] = jnp.swapaxes(l_refs[j][...], 0, 1)
-        if j == 0:
-            continue
-        at = slice((j - 1) * chunk, j * chunk)
+    for j in range(steps):
+        copies[6 + j].wait()
+        at = slice(j * chunk, (j + 1) * chunk)
+        for row in range(chunk):
+            f_ref[row * STRIDE : row * STRIDE + pairs, :] = l_refs[j][row].astype(F32)
         for p in range(0, pairs, 2):
-            both = jnp.concatenate([c_ref[p, :, at], c_ref[p + 1, :, at]], axis=0)
-            sums = dot(both, jnp.concatenate([lr_ref[p, at, :], lr_ref[p + 1, at, :]], axis=1))
+            tables = [f_ref[pl.ds(p + i, chunk, stride=STRIDE), :].astype(BF16) for i in range(2)]
+            both = across(
+                jnp.concatenate([c_ref[p, t], c_ref[p + 1, t]], axis=0)
+                for t in range(j * chunk // LANES, (j + 1) * chunk // LANES)
+            )
+            sums = dot(both, jnp.concatenate(tables, axis=1))
             for i in range(2):
+                lr_ref[p + i, at, :] = tables[i]
                 part = sums[i * 8 * lines : (i + 1) * 8 * lines, i * cycles : (i + 1) * cycles]
-                s_ref[p + i] = part if j == 1 else s_ref[p + i] + part
+                s_ref[p + i] = part if j == 0 else s_ref[p + i] + part
 
     blocks = []
     for p in range(pairs):
@@ -199,13 +210,14 @@
             pltpu.VMEM(tbar_alm.shape, BF16),
             pltpu.VMEM(twf_alm.shape, BF16),
             pltpu.VMEM((1, pairs, cycles), BF16),
-            pltpu.VMEM((pairs, 8 * lines, modes), BF16),
+            pltpu.VMEM((pairs, modes // LANES, 8 * lines, LANES), BF16),
             pltpu.VMEM((pairs, 8 * lines, cycles), F32),
             pltpu.VMEM((pairs, modes), F32),
             pltpu.VMEM((pairs, modes), F32),
             pltpu.VMEM((pairs, modes), F32),
             pltpu.VMEM((pairs, LANES), F32),
             pltpu.VMEM((pairs, 4 * lines, cycles), F32),
+            pltpu.VMEM((modes // steps * STRIDE, cycles), F32),
             pltpu.SemaphoreType.DMA((steps + 6,)),
         ]
         + [pltpu.VMEM((modes // steps, pairs, cycles), BF16)] * steps,
@@ -276,15 +288,15 @@
             if half:
                 low, high = LANES - 1 - low, tall - 1 - high
             place.append(iota((tall, devices), 0) == high)
-            tile = slice(p * devices, (p + 1) * devices)
-            hot_ref[half, :, tile] = jnp.where(iota((LANES, devices), 0) == low, 1.0, 0.0).astype(BF16)
+            hot_ref[half, p] = jnp.where(iota((LANES, devices), 0) == low, 1.0, 0.0).astype(BF16)
             parts = []
             for row in range(3 * lines):
                 at = p * wide + half * 3 * lines + row
                 parts.append(jnp.where(place[p], xt_ref[at : at + 1, :], 0.0))
-            lhs_ref[:, tile] = jnp.concatenate(parts, axis=0).astype(BF16)
+            lhs_ref[p] = jnp.concatenate(parts, axis=0).astype(BF16)
         places.append(place)
-        sorted_halves.append(dot(lhs_ref[...], hot_ref[half], NT).astype(BF16))
+        left, right = (across(ref[p] for p in range(pairs)) for ref in (lhs_ref, hot_ref.at[half]))
+        sorted_halves.append(dot(left, right, NT).astype(BF16))
 
     spread = jnp.concatenate(
         [
@@ -327,12 +339,12 @@
         stacked = jnp.concatenate(
             [spectra[half * n : (half + 1) * n, g * LANES : (g + 1) * LANES] for g in range(groups)], axis=0
         )
-        values = dot(stacked, hot_ref[half])
+        values = dot(stacked, across(hot_ref[half, p] for p in range(pairs)))
         for p in range(pairs):
             tile = slice(p * devices, (p + 1) * devices)
             keep = jnp.concatenate([places[half][p]] * rows, axis=0)
-            lhs_ref[:columns, tile] = jnp.where(keep, values[:, tile], 0.0).astype(BF16)
-        found.append(dot(add, lhs_ref[:columns, :]))
+            lhs_ref[p, :columns] = jnp.where(keep, values[:, tile], 0.0).astype(BF16)
+        found.append(dot(add, across(lhs_ref[p, :columns] for p in range(pairs))))
     blocks = [found[half][:, p * devices : (p + 1) * devices] for p in range(pairs) for half in range(2)]
     out = jnp.concatenate(blocks, axis=0).T.astype(BF16)
     near_ref[...] = out[: devices // 2].reshape(near_ref.shape)
@@ -352,8 +364,8 @@
         out_shape=[pltpu.VMEM((devices // 2, pairs * 8 * sims // LANES, LANES), BF16)] * 2,
         scratch_shapes=[
             pltpu.VMEM((received.shape[1] // 2 * LANES, devices), F32),
-            pltpu.VMEM((6 * sims * tall, pairs * devices), BF16),
-            pltpu.VMEM((2, LANES, pairs * devices), BF16),
+            pltpu.VMEM((pairs, 6 * sims * tall, devices), BF16),
+            pltpu.VMEM((2, pairs, LANES, devices), BF16),
         ],
         compiler_params=pltpu.CompilerParams(vmem_limit_bytes=GRANT),
         name="sky",
@@ -377,7 +389,8 @@
                     ref[j, p] = jnp.broadcast_to(values[p : p + 1], ref.shape[2:])
     late = flip_ref.shape[0]
     for p in range(late):
-        flip_ref[p] = table_ref[pairs - late + p].T
+        for t in range(modes // LANES):
+            flip_ref[p, t] = table_ref[pairs - late + p, t * LANES : (t + 1) * LANES].T
     hot_ref[...] = slot_of_cycle(order_ref).astype(BF16)
     theta, weight = colat_ref[...], weight_ref[...]
     with_ref[0] = jnp.broadcast_to(weight * jnp.cos(theta) / jnp.sin(theta), with_ref.shape[1:])
@@ -395,7 +408,7 @@
         out_shape=[
             pltpu.VMEM((3, pairs, lines, modes), F32), pltpu.VMEM((3, pairs, cycles), F32),
             pltpu.VMEM((cycles, cycles), BF16), pltpu.VMEM((2, lines, cycles), F32),
-            pltpu.VMEM((late, cycles, modes), BF16),
+            pltpu.VMEM((late, modes // LANES, cycles, LANES), BF16),
         ],
         compiler_params=pltpu.CompilerParams(vmem_limit_bytes=GRANT),
         cost_estimate=pl.CostEstimate(flops=10**9, bytes_accessed=10**6, transcendentals=10**5),
@@ -405,7 +418,8 @@
 
 def flip_kernel(table_ref, _, out_ref):
     for p in range(out_ref.shape[0]):
-        out_ref[p] = table_ref[p].T
+        for t in range(out_ref.shape[1]):
+            out_ref[p, t] = table_ref[p, t * LANES : (t + 1) * LANES].T
 
 
 def flip(table, pairs, after):
@@ -415,7 +429,7 @@
         flip_kernel,
         in_specs=[vmem] * 2,
         out_specs=vmem,
-        out_shape=pltpu.VMEM((pairs, cycles, modes), BF16),
+        out_shape=pltpu.VMEM((pairs, modes // LANES, cycles, LANES), BF16),
         compiler_params=pltpu.CompilerParams(vmem_limit_bytes=GRANT),
         cost_estimate=pl.CostEstimate(flops=10**9, bytes_accessed=10**6, transcendentals=0),
         name="flip",
@@ -427,13 +441,12 @@
     w_ref, grad_ref, curl_ref, sems,
 ):
     pairs, lines, modes = row_ref.shape[1:]
-    cycles = l_ref.shape[1]
+    cycles = l_ref.shape[2]
     sims = lines // 2
     high = 6 * lines
 
     spectra = dot(near_then_far(r_ref).astype(F32).T.astype(BF16), hot_ref[...], NT)
     with_cos, with_sin = with_ref[0], with_ref[1]
-    blank = jnp.zeros((high, cycles), F32)
     for i in range(pairs):
         for half in range(2):
             at = (i * 2 + half) * 2 * lines
@@ -442,10 +455,7 @@
                 parts += [values * with_cos, values * with_sin]
                 turned.append(turn(parts[-1]))
             parts = jnp.concatenate(parts + turned, axis=0)
-            at = ((i % 2) * 2 + half) * high
-            w_ref[i // 2, at : at + high] = jnp.concatenate(
-                [blank, parts] if i % 2 else [parts, blank], axis=1
-            ).astype(BF16)
+            w_ref[i, half * high : (half + 1) * high] = parts.astype(BF16)
 
     k = iota((lines, modes), 1)
     starts = k == 0
@@ -458,8 +468,12 @@
         odd = p % 2
         if not odd:
             ref, at = (l_ref, p) if p < l_ref.shape[0] else (l2_ref, p - l_ref.shape[0])
-            tables = jnp.concatenate([ref[at], ref[at + 1]], axis=0)
-            both = dot(w_ref[p // 2], tables)
+            tables = across(
+                jnp.concatenate([ref[at, t], ref[at + 1, t]], axis=0) for t in range(ref.shape[1])
+            )
+            blank = jnp.zeros((2 * high, cycles), BF16)
+            left = [jnp.concatenate([w_ref[p], blank], axis=0), jnp.concatenate([blank, w_ref[p + 1]], axis=0)]
+            both = dot(across(left), tables)
         sums = both[odd * 2 * high : (odd + 1) * 2 * high]
         upper = k >= modes - small_ref[p : p + 1, :1].astype(jnp.int32)
         a0, a1, a2, a3, t1, t3 = (
@@ -469,8 +483,7 @@
         level, raised, azimuth = (row_ref[i, p] for i in range(3))
         grad = level * a0 - raised * previous(a1) - azimuth * t3
         curl = level * a2 - raised * previous(a3) + azimuth * t1
-        weighted = w_ref[p // 2, (2 * odd + 1) * high : (2 * odd + 2) * high, odd * cycles : (odd + 1) * cycles]
-        last = jnp.sum(weighted.astype(F32) * tail_ref[p : p + 1, :], axis=1, keepdims=True)
+        last = jnp.sum(w_ref[p, high:].astype(F32) * tail_ref[p : p + 1, :], axis=1, keepdims=True)
         level, raised, azimuth = (end_ref[i, p : p + 1, :1] for i in range(3))
         b0, b1, b2, b3, u1, u3 = (last[q * lines : (q + 1) * lines] for q in range(6))
         last_grad = level * b0 - raised * a1[:, modes - 1 :] - azimuth * u3
@@ -497,7 +510,7 @@
         out_specs=[hbm, hbm],
         out_shape=[out, out],
         scratch_shapes=[
-            pltpu.VMEM((pairs // 2, 24 * lines, 2 * cycles), BF16),
+            pltpu.VMEM((pairs, 12 * lines, cycles), BF16),
             pltpu.VMEM(shape, F32),
             pltpu.VMEM(shape, F32),
             pltpu.SemaphoreType.DMA((2 * pairs,)),

time: 65.6 us -> 64.8 us (0.988)
  Pallas kernels: 10.1 us -> 9.32 us
where the time goes in v6:
time: 64.8 us; the launch traced here: 64.6 us
  blocking collectives  31.5 us (49%)
  starting transfers between devices  22.7 us (35%)
  Pallas kernels  9.32 us (14%)
  between operations  0.76 us (1%)
    all_to_all x2, blocking collectives, exchange(): return lax.all_to_all(both, CHIP, 0, 0, tiled=True)  31.5 us
    ppermute x2, starting transfers between devices, exchange(): swapped = lax.ppermute(far, CORE, [(0, 1), (1, 0)])  22.7 us
    pallas_call x1, Pallas kernels, synth(): pl.pallas_call(synth_kernel, in_specs=[hbm] * 6, out_specs=[vmem] * 5, ou...  3.54 us
    pallas_call x1, Pallas kernels, analyse(): pl.pallas_call(analyse_kernel, in_specs=[vmem] * 9, out_specs=[hbm, hbm],...  2.26 us
    pallas_call x1, Pallas kernels, sky(): pl.pallas_call(functools.partial(sky_kernel, pairs, sims), in_specs=[vmem...  1.96 us
  transfers between devices with their start and end apart: 2, of which 1 were waited for; matrix products, arithmetic and copies ran while one was open for 0% of the time, Pallas kernels for 2%

profile of v6, /device:TPU:513, one launch (start us, length us, event | category | flops | bytes accessed | tf_op | source)
XLA Modules:
  0.0 64.6 jit_solution(8363022044315053391)
XLA Ops:
  0.6 3.5 %synth.1 = (bf16[64,4,128]{2,1,0:T(4,128)(2,1)S(1)}, bf16[64,4,128]{2,1,0:T(4,128)(2,1)S(1)}, bf16[8,2048,128]{2,1,0:T(8,128)(2,1)S(1)}, f32[8,128]{1,0:T(8,128)S(1)}, f32[8,128]{1,0:T(8,128)S(1)}) custom-call(s32[1024]{0:T(1024)} %m_hbm.1, s32[1,128]{1,0:T(1,128)} %bitcast.6, f32[1,128]{1,0:T(1,128)} %bitcast.8, bf16[8,4,2,2049]{3,2,1,0:T(2,128)(2,1)} %t_hbm.1, ...), custom_call_target="tpu_custom_call" | custom-call | tf_op jit(solution)/shard_map/synth/pallas_call | solution.py:195
  4.2 20.5 %collective-permute-start = (bf16[64,4,128]{2,1,0:T(4,128)(2,1)S(1)}, bf16[64,4,128]{2,1,0:T(4,128)(2,1)S(1)}, u32[]{:S(2)}, u32[]{:S(2)}) collective-permute-start(bf16[64,4,128]{2,1,0:T(4,128)(2,1)S(1)} %get-tuple-element.16), channel_id=1, source_target_pairs={{0,1},{1,0},{2,3},{3,2},{4,5},{5,4},{6,7},{7,6},{8,9},{9,8},{10,11... | collective-permute-start | bytes 196616 | tf_op jit(solution)/shard_map/ppermute | solution.py:532
  24.7 0.0 copy-start
  24.7 0.0 copy-start.1
  24.7 0.0 copy-start.2
  24.7 0.0 copy-start.3
  24.7 0.0 copy-start.4
  24.7 0.0 copy-start.5
  24.7 0.0 copy-start.6
  24.8 0.0 copy-start.7
  24.8 0.0 copy-start.8
  24.8 0.9 %flip.1.refs_0_.l_ref = bf16[6,16,128,128]{3,2,1,0:T(8,128)(2,1)S(1)} custom-call(bf16[8,2048,128]{2,1,0:T(8,128)(2,1)S(1)} %get-tuple-element.17.table_ref, bf16[64,4,128]{2,1,0:T(4,128)(2,1)S(1)} %get-tuple-element.15._.near_ref), custom_call_target="tpu_custom_call" | custom-call | flops 1000000000 | bytes 1000000 | tf_op jit(solution)/shard_map/flip/pallas_call | solution.py:428
  25.6 0.0 collective-permute-done.far_ref
  25.7 0.1 merge.2
  25.7 15.9 %all_to_all.10.x_ref = bf16[64,8,128]{2,1,0:T(8,128)(2,1)S(1)} all-to-all(bf16[64,8,128]{2,1,0:T(8,128)(2,1)S(1)} %merge.2), channel_id=1, replica_groups=mesh['grp'=2,'chip'=64,'core'=2] {'chip'}, dimensions={0} | all-to-all | bytes 262144 | tf_op jit(solution)/shard_map/all_to_all | solution.py:542
  41.7 0.0 copy-done
  41.7 0.0 copy-done.1
  41.7 0.0 copy-done.2
  41.7 0.0 copy-done.3
  41.7 0.0 copy-done.4
  41.7 0.0 copy-done.5
  41.7 2.0 %sky.1 = (bf16[64,2,128]{2,1,0:T(2,128)(2,1)S(1)}, bf16[64,2,128]{2,1,0:T(2,128)(2,1)S(1)}) custom-call(bf16[64,8,128]{2,1,0:T(8,128)(2,1)S(1)} %all_to_all.10.x_ref, s32[32,128]{1,0:T(8,128)S(1)} %bitcast.5, bf16[64,64]{1,0:T(8,128)(2,1)S(1)} %copy-done.4, f32[2,32,128]{2,1,0:T(8,128)S(1)} %copy-done.2, bf16[512,128]{1,0:T(8,128)(2,1)S(1)} %copy-done.1, ...), custom_call_target="tpu_custom_call" | custom-call | tf_op jit(solution)/shard_map/sky/pallas_call | solution.py:360
  43.7 2.2 %collective-permute-start.1 = (bf16[64,2,128]{2,1,0:T(2,128)(2,1)S(1)}, bf16[64,2,128]{2,1,0:T(2,128)(2,1)S(1)}, u32[]{:S(2)}, u32[]{:S(2)}) collective-permute-start(bf16[64,2,128]{2,1,0:T(2,128)(2,1)S(1)} %get-tuple-element.19), channel_id=1, source_target_pairs={{0,1},{1,0},{2,3},{3,2},{4,5},{5,4},{6,7},{7,6},{8,9},{9,8},{10,11... | collective-permute-start | bytes 98312 | tf_op jit(solution)/shard_map/ppermute | solution.py:532
  45.9 0.0 copy-done.6
  45.9 0.0 copy-done.7
  45.9 0.0 copy-done.8
  45.9 0.6 layout.1
  46.4 0.3 collective-permute-done.1.far_ref
  46.7 0.1 merge.3
  46.8 15.6 %all_to_all.11.r_ref = bf16[64,4,128]{2,1,0:T(4,128)(2,1)S(1)} all-to-all(bf16[64,4,128]{2,1,0:T(4,128)(2,1)S(1)} %merge.3), channel_id=1, replica_groups=mesh['grp'=2,'chip'=64,'core'=2] {'chip'}, dimensions={0} | all-to-all | bytes 131072 | tf_op jit(solution)/shard_map/all_to_all | solution.py:542
  62.4 2.3 %analyse.1 = (f32[8,4,2,2049]{3,2,1,0:T(2,128)}, f32[8,4,2,2049]{3,2,1,0:T(2,128)}) custom-call(f32[8,128]{1,0:T(8,128)S(1)} %get-tuple-element.14.small_ref, bf16[64,4,128]{2,1,0:T(4,128)(2,1)S(1)} %all_to_all.11.r_ref, bf16[6,16,128,128]{3,2,1,0:T(8,128)(2,1)S(1)} %flip.1.refs_0_.l_ref, bf16[2,16,128,128]{3,2,1,0:T(8,128)(2,1)S(1)} %get-tuple-element.21.l2_ref, ...), custom_call_target="tpu_custom_call" | custom-call | tf_op jit(solution)/shard_map/analyse/pallas_call | solution.py:507
Async XLA Ops:
  4.2 21.5 %collective-permute-start = (bf16[64,4,128]{2,1,0:T(4,128)(2,1)S(1)}, bf16[64,4,128]{2,1,0:T(4,128)(2,1)S(1)}, u32[]{:S(2)}, u32[]{:S(2)}) collective-permute-start(bf16[64,4,128]{2,1,0:T(4,128)(2,1)S(1)} %get-tuple-element.16), channel_id=1, source_target_pairs={{0,1},{1,0},{2,3},{3,2},{4,5},{5,4},{6,7},{7,6},{8,9},{9,8},{10,11... | collective-permute-start | bytes 196616 | tf_op jit(solution)/shard_map/ppermute | solution.py:532
  24.7 17.0 %copy-start = (bf16[256,256]{1,0:T(8,128)(2,1)S(1)}, bf16[256,256]{1,0:T(8,128)(2,1)}, u32[]{:S(2)}) copy-start(bf16[256,256]{1,0:T(8,128)(2,1)} %constant.13.clone.third_ref) | copy-start | bytes 393220
  24.7 17.0 %copy-start.1 = (bf16[512,128]{1,0:T(8,128)(2,1)S(1)}, bf16[512,128]{1,0:T(8,128)(2,1)}, u32[]{:S(2)}) copy-start(bf16[512,128]{1,0:T(8,128)(2,1)} %constant.12.clone.second_ref) | copy-start | bytes 393220
  24.7 17.0 %copy-start.2 = (f32[2,32,128]{2,1,0:T(8,128)S(1)}, f32[2,32,128]{2,1,0:T(8,128)}, u32[]{:S(2)}) copy-start(f32[2,32,128]{2,1,0:T(8,128)} %constant.11.clone.twist_ref) | copy-start | bytes 98308
  24.7 17.0 %copy-start.3 = (s32[1,4096]{1,0:T(1,128)S(1)}, s32[1,4096]{1,0:T(1,128)}, u32[]{:S(2)}) copy-start(s32[1,4096]{1,0:T(1,128)} %param.20) | copy-start | bytes 49156
  24.7 17.0 %copy-start.4 = (bf16[64,64]{1,0:T(8,128)(2,1)S(1)}, bf16[64,64]{1,0:T(8,128)(2,1)}, u32[]{:S(2)}) copy-start(bf16[64,64]{1,0:T(8,128)(2,1)} %constant.10.clone.first_ref) | copy-start | bytes 24580
  24.7 17.0 %copy-start.5 = (bf16[32,128]{1,0:T(8,128)(2,1)S(1)}, bf16[32,128]{1,0:T(8,128)(2,1)}, u32[]{:S(2)}) copy-start(bf16[32,128]{1,0:T(8,128)(2,1)} %constant.14.clone.fourth_ref) | copy-start | bytes 24580
  24.7 21.1 %copy-start.6 = (s32[128]{0:T(128)S(1)}, s32[128]{0:T(128)}, u32[]{:S(2)}) copy-start(s32[128]{0:T(128)} %param.17) | copy-start | bytes 1540
  24.8 21.1 %copy-start.7 = (f32[128]{0:T(128)S(1)}, f32[128]{0:T(128)}, u32[]{:S(2)}) copy-start(f32[128]{0:T(128)} %param.18) | copy-start | bytes 1540
  24.8 21.1 %copy-start.8 = (f32[128]{0:T(128)S(1)}, f32[128]{0:T(128)}, u32[]{:S(2)}) copy-start(f32[128]{0:T(128)} %param.19) | copy-start | bytes 1540
  43.7 3.0 %collective-permute-start.1 = (bf16[64,2,128]{2,1,0:T(2,128)(2,1)S(1)}, bf16[64,2,128]{2,1,0:T(2,128)(2,1)S(1)}, u32[]{:S(2)}, u32[]{:S(2)}) collective-permute-start(bf16[64,2,128]{2,1,0:T(2,128)(2,1)S(1)} %get-tuple-element.19), channel_id=1, source_target_pairs={{0,1},{1,0},{2,3},{3,2},{4,5},{5,4},{6,7},{7,6},{8,9},{9,8},{10,11... | collective-permute-start | bytes 98312 | tf_op jit(solution)/shard_map/ppermute | solution.py:532

commit v7 on v6

--- a/solution.py
+++ b/solution.py
@@ -15,6 +15,7 @@
 LANES = 128
 GRANT = 24 * 2**20
 STRIDE = 9
+CUTS = 4
 CHIP, CORE = "chip", "core"
 NT = (((1,), (1,)), ((), ()))
 NN = (((1,), (0,)), ((), ()))
@@ -75,6 +76,12 @@
 
 def first_pair(pairs):
     return (lax.axis_index(CHIP) * lax.axis_size(CORE) + lax.axis_index(CORE)) * pairs
+
+
+def swap_rows(values):
+    rows = values.shape[0]
+    real = iota(values.shape, 0) % 2 == 0
+    return jnp.where(real, pltpu.roll(values, rows - 1, 0), pltpu.roll(values, 1, 0))
 
 
 def turn(values):
@@ -386,7 +393,8 @@
                 ref[j] = jnp.broadcast_to(values, ref.shape[1:])
             else:
                 for p in range(pairs):
-                    ref[j, p] = jnp.broadcast_to(values[p : p + 1], ref.shape[2:])
+                    row = jnp.broadcast_to(values[p : p + 1], ref.shape[2:])
+                    ref[j, p] = jnp.where(iota(row.shape, 0) % 2 == 0, -row, row) if j == 2 else row
     late = flip_ref.shape[0]
     for p in range(late):
         for t in range(modes // LANES):
@@ -443,55 +451,52 @@
     pairs, lines, modes = row_ref.shape[1:]
     cycles = l_ref.shape[2]
     sims = lines // 2
-    high = 6 * lines
+    high = 4 * lines
 
     spectra = dot(near_then_far(r_ref).astype(F32).T.astype(BF16), hot_ref[...], NT)
     with_cos, with_sin = with_ref[0], with_ref[1]
     for i in range(pairs):
         for half in range(2):
             at = (i * 2 + half) * 2 * lines
-            parts, turned = [], []
+            parts = []
             for values in (spectra[at : at + lines], spectra[at + lines : at + 2 * lines]):
                 parts += [values * with_cos, values * with_sin]
-                turned.append(turn(parts[-1]))
-            parts = jnp.concatenate(parts + turned, axis=0)
+            parts = jnp.concatenate(parts, axis=0)
             w_ref[i, half * high : (half + 1) * high] = parts.astype(BF16)
 
-    k = iota((lines, modes), 1)
-    starts = k == 0
-
-    def previous(values):
-        return jnp.where(starts, 0.0, pltpu.roll(values, 1, 1))
-
+    chunk = modes // CUTS
+    k = iota((lines, chunk), 1)
     copies = []
     for p in range(pairs):
-        odd = p % 2
-        if not odd:
-            ref, at = (l_ref, p) if p < l_ref.shape[0] else (l2_ref, p - l_ref.shape[0])
-            tables = across(
-                jnp.concatenate([ref[at, t], ref[at + 1, t]], axis=0) for t in range(ref.shape[1])
+        ref, at = (l_ref, p) if p < l_ref.shape[0] else (l2_ref, p - l_ref.shape[0])
+        before = [jnp.zeros((lines, LANES), F32)] * 2
+        bound = modes - small_ref[p : p + 1, :1].astype(jnp.int32)
+        for cut in range(CUTS):
+            columns = slice(cut * chunk, (cut + 1) * chunk)
+            sums = dot(w_ref[p], across(ref[at, t] for t in range(cut * chunk // LANES, (cut + 1) * chunk // LANES)))
+            upper = k >= bound - cut * chunk
+            a0, a1, a2, a3 = (
+                jnp.where(upper, sums[high + q * lines : high + (q + 1) * lines], sums[q * lines : (q + 1) * lines])
+                for q in range(4)
             )
-            blank = jnp.zeros((2 * high, cycles), BF16)
-            left = [jnp.concatenate([w_ref[p], blank], axis=0), jnp.concatenate([blank, w_ref[p + 1]], axis=0)]
-            both = dot(across(left), tables)
-        sums = both[odd * 2 * high : (odd + 1) * 2 * high]
-        upper = k >= modes - small_ref[p : p + 1, :1].astype(jnp.int32)
-        a0, a1, a2, a3, t1, t3 = (
-            jnp.where(upper, sums[high + q * lines : high + (q + 1) * lines], sums[q * lines : (q + 1) * lines])
-            for q in range(6)
-        )
-        level, raised, azimuth = (row_ref[i, p] for i in range(3))
-        grad = level * a0 - raised * previous(a1) - azimuth * t3
-        curl = level * a2 - raised * previous(a3) + azimuth * t1
+            level, raised, azimuth = (row_ref[i, p, :, columns] for i in range(3))
+            shifted = [
+                pltpu.roll(across((tile, values)), 1, 1)[:, LANES:] for tile, values in zip(before, (a1, a3))
+            ]
+            before = [a1[:, chunk - LANES :], a3[:, chunk - LANES :]]
+            grad = level * a0 - raised * shifted[0] - azimuth * swap_rows(a3)
+            curl = level * a2 - raised * shifted[1] + azimuth * swap_rows(a1)
+            grad_ref[p, :, :, columns] = grad.reshape(sims, 2, chunk)
+            curl_ref[p, :, :, columns] = curl.reshape(sims, 2, chunk)
         last = jnp.sum(w_ref[p, high:].astype(F32) * tail_ref[p : p + 1, :], axis=1, keepdims=True)
         level, raised, azimuth = (end_ref[i, p : p + 1, :1] for i in range(3))
-        b0, b1, b2, b3, u1, u3 = (last[q * lines : (q + 1) * lines] for q in range(6))
-        last_grad = level * b0 - raised * a1[:, modes - 1 :] - azimuth * u3
-        last_curl = level * b2 - raised * a3[:, modes - 1 :] + azimuth * u1
-        for ref, hbm, main, last in ((grad_ref, grad_hbm, grad, last_grad), (curl_ref, curl_hbm, curl, last_curl)):
-            ref[p, :, :, :modes] = main.reshape(sims, 2, modes)
-            ref[p, :, :, modes:] = last.reshape(sims, 2, 1)
-            copies.append(pltpu.make_async_copy(ref.at[p], hbm.at[p], sems.at[len(copies)]))
+        b0, b1, b2, b3 = (last[q * lines : (q + 1) * lines] for q in range(4))
+        a1, a3 = (values[:, LANES - 1 :] for values in before)
+        last_grad = level * b0 - raised * a1 - azimuth * turn(b3)
+        last_curl = level * b2 - raised * a3 + azimuth * turn(b1)
+        for out, hbm, last in ((grad_ref, grad_hbm, last_grad), (curl_ref, curl_hbm, last_curl)):
+            out[p, :, :, modes:] = last.reshape(sims, 2, 1)
+            copies.append(pltpu.make_async_copy(out.at[p], hbm.at[p], sems.at[len(copies)]))
             copies[-1].start()
     for copy in copies:
         copy.wait()
@@ -510,7 +515,7 @@
         out_specs=[hbm, hbm],
         out_shape=[out, out],
         scratch_shapes=[
-            pltpu.VMEM((pairs, 12 * lines, cycles), BF16),
+            pltpu.VMEM((pairs, 8 * lines, cycles), BF16),
             pltpu.VMEM(shape, F32),
             pltpu.VMEM(shape, F32),
             pltpu.SemaphoreType.DMA((2 * pairs,)),

time: 64.8 us -> 64.6 us (level)
  no operation moved by 1% of the time
where the time goes in v7:
time: 64.6 us; the launch traced here: 64.4 us
  blocking collectives  31.5 us (49%)
  starting transfers between devices  22.7 us (35%)
  Pallas kernels  9.08 us (14%)
  between operations  0.76 us (1%)
    all_to_all x2, blocking collectives, exchange(): return lax.all_to_all(both, CHIP, 0, 0, tiled=True)  31.5 us
    ppermute x2, starting transfers between devices, exchange(): swapped = lax.ppermute(far, CORE, [(0, 1), (1, 0)])  22.7 us
    pallas_call x1, Pallas kernels, synth(): pl.pallas_call(synth_kernel, in_specs=[hbm] * 6, out_specs=[vmem] * 5, ou...  3.54 us
    pallas_call x1, Pallas kernels, analyse(): pl.pallas_call(analyse_kernel, in_specs=[vmem] * 9, out_specs=[hbm, hbm],...  2.04 us
    pallas_call x1, Pallas kernels, sky(): pl.pallas_call(functools.partial(sky_kernel, pairs, sims), in_specs=[vmem...  1.96 us
  transfers between devices with their start and end apart: 2, of which 1 were waited for; matrix products, arithmetic and copies ran while one was open for 0% of the time, Pallas kernels for 2%

profile of v7, /device:TPU:513, one launch (start us, length us, event | category | flops | bytes accessed | tf_op | source)
XLA Modules:
  0.0 64.4 jit_solution(1564811645949444067)
XLA Ops:
  0.6 3.5 %synth.1 = (bf16[64,4,128]{2,1,0:T(4,128)(2,1)S(1)}, bf16[64,4,128]{2,1,0:T(4,128)(2,1)S(1)}, bf16[8,2048,128]{2,1,0:T(8,128)(2,1)S(1)}, f32[8,128]{1,0:T(8,128)S(1)}, f32[8,128]{1,0:T(8,128)S(1)}) custom-call(s32[1024]{0:T(1024)} %m_hbm.1, s32[1,128]{1,0:T(1,128)} %bitcast.6, f32[1,128]{1,0:T(1,128)} %bitcast.8, bf16[8,4,2,2049]{3,2,1,0:T(2,128)(2,1)} %t_hbm.1, ...), custom_call_target="tpu_custom_call" | custom-call | tf_op jit(solution)/shard_map/synth/pallas_call | solution.py:202
  4.2 20.5 %collective-permute-start = (bf16[64,4,128]{2,1,0:T(4,128)(2,1)S(1)}, bf16[64,4,128]{2,1,0:T(4,128)(2,1)S(1)}, u32[]{:S(2)}, u32[]{:S(2)}) collective-permute-start(bf16[64,4,128]{2,1,0:T(4,128)(2,1)S(1)} %get-tuple-element.16), channel_id=1, source_target_pairs={{0,1},{1,0},{2,3},{3,2},{4,5},{5,4},{6,7},{7,6},{8,9},{9,8},{10,11... | collective-permute-start | bytes 196616 | tf_op jit(solution)/shard_map/ppermute | solution.py:537
  24.7 0.0 copy-start
  24.7 0.0 copy-start.1
  24.7 0.0 copy-start.2
  24.7 0.0 copy-start.3
  24.7 0.0 copy-start.4
  24.7 0.0 copy-start.5
  24.7 0.0 copy-start.6
  24.8 0.0 copy-start.7
  24.8 0.0 copy-start.8
  24.8 0.9 %flip.1.refs_0_.l_ref = bf16[6,16,128,128]{3,2,1,0:T(8,128)(2,1)S(1)} custom-call(bf16[8,2048,128]{2,1,0:T(8,128)(2,1)S(1)} %get-tuple-element.17.table_ref, bf16[64,4,128]{2,1,0:T(4,128)(2,1)S(1)} %get-tuple-element.15._.near_ref), custom_call_target="tpu_custom_call" | custom-call | flops 1000000000 | bytes 1000000 | tf_op jit(solution)/shard_map/flip/pallas_call | solution.py:436
  25.6 0.0 collective-permute-done.far_ref
  25.7 0.1 merge.2
  25.7 15.9 %all_to_all.10.x_ref = bf16[64,8,128]{2,1,0:T(8,128)(2,1)S(1)} all-to-all(bf16[64,8,128]{2,1,0:T(8,128)(2,1)S(1)} %merge.2), channel_id=1, replica_groups=mesh['grp'=2,'chip'=64,'core'=2] {'chip'}, dimensions={0} | all-to-all | bytes 262144 | tf_op jit(solution)/shard_map/all_to_all | solution.py:547
  41.7 0.0 copy-done
  41.7 0.0 copy-done.1
  41.7 0.0 copy-done.2
  41.7 0.0 copy-done.3
  41.7 0.0 copy-done.4
  41.7 0.0 copy-done.5
  41.7 2.0 %sky.1 = (bf16[64,2,128]{2,1,0:T(2,128)(2,1)S(1)}, bf16[64,2,128]{2,1,0:T(2,128)(2,1)S(1)}) custom-call(bf16[64,8,128]{2,1,0:T(8,128)(2,1)S(1)} %all_to_all.10.x_ref, s32[32,128]{1,0:T(8,128)S(1)} %bitcast.5, bf16[64,64]{1,0:T(8,128)(2,1)S(1)} %copy-done.4, f32[2,32,128]{2,1,0:T(8,128)S(1)} %copy-done.2, bf16[512,128]{1,0:T(8,128)(2,1)S(1)} %copy-done.1, ...), custom_call_target="tpu_custom_call" | custom-call | tf_op jit(solution)/shard_map/sky/pallas_call | solution.py:367
  43.7 2.2 %collective-permute-start.1 = (bf16[64,2,128]{2,1,0:T(2,128)(2,1)S(1)}, bf16[64,2,128]{2,1,0:T(2,128)(2,1)S(1)}, u32[]{:S(2)}, u32[]{:S(2)}) collective-permute-start(bf16[64,2,128]{2,1,0:T(2,128)(2,1)S(1)} %get-tuple-element.19), channel_id=1, source_target_pairs={{0,1},{1,0},{2,3},{3,2},{4,5},{5,4},{6,7},{7,6},{8,9},{9,8},{10,11... | collective-permute-start | bytes 98312 | tf_op jit(solution)/shard_map/ppermute | solution.py:537
  45.9 0.0 copy-done.6
  45.9 0.0 copy-done.7
  45.9 0.0 copy-done.8
  45.9 0.5 layout.1
  46.4 0.3 collective-permute-done.1.far_ref
  46.7 0.1 merge.3
  46.8 15.6 %all_to_all.11.r_ref = bf16[64,4,128]{2,1,0:T(4,128)(2,1)S(1)} all-to-all(bf16[64,4,128]{2,1,0:T(4,128)(2,1)S(1)} %merge.3), channel_id=1, replica_groups=mesh['grp'=2,'chip'=64,'core'=2] {'chip'}, dimensions={0} | all-to-all | bytes 131072 | tf_op jit(solution)/shard_map/all_to_all | solution.py:547
  62.4 2.0 %analyse.1 = (f32[8,4,2,2049]{3,2,1,0:T(2,128)}, f32[8,4,2,2049]{3,2,1,0:T(2,128)}) custom-call(f32[8,128]{1,0:T(8,128)S(1)} %get-tuple-element.14.small_ref, bf16[64,4,128]{2,1,0:T(4,128)(2,1)S(1)} %all_to_all.11.r_ref, bf16[6,16,128,128]{3,2,1,0:T(8,128)(2,1)S(1)} %flip.1.refs_0_.l_ref, bf16[2,16,128,128]{3,2,1,0:T(8,128)(2,1)S(1)} %get-tuple-element.21.l2_ref, ...), custom_call_target="tpu_custom_call" | custom-call | tf_op jit(solution)/shard_map/analyse/pallas_call | solution.py:512
Async XLA Ops:
  4.2 21.5 %collective-permute-start = (bf16[64,4,128]{2,1,0:T(4,128)(2,1)S(1)}, bf16[64,4,128]{2,1,0:T(4,128)(2,1)S(1)}, u32[]{:S(2)}, u32[]{:S(2)}) collective-permute-start(bf16[64,4,128]{2,1,0:T(4,128)(2,1)S(1)} %get-tuple-element.16), channel_id=1, source_target_pairs={{0,1},{1,0},{2,3},{3,2},{4,5},{5,4},{6,7},{7,6},{8,9},{9,8},{10,11... | collective-permute-start | bytes 196616 | tf_op jit(solution)/shard_map/ppermute | solution.py:537
  24.7 17.0 %copy-start = (bf16[256,256]{1,0:T(8,128)(2,1)S(1)}, bf16[256,256]{1,0:T(8,128)(2,1)}, u32[]{:S(2)}) copy-start(bf16[256,256]{1,0:T(8,128)(2,1)} %constant.13.clone.third_ref) | copy-start | bytes 393220
  24.7 17.0 %copy-start.1 = (bf16[512,128]{1,0:T(8,128)(2,1)S(1)}, bf16[512,128]{1,0:T(8,128)(2,1)}, u32[]{:S(2)}) copy-start(bf16[512,128]{1,0:T(8,128)(2,1)} %constant.12.clone.second_ref) | copy-start | bytes 393220
  24.7 17.0 %copy-start.2 = (f32[2,32,128]{2,1,0:T(8,128)S(1)}, f32[2,32,128]{2,1,0:T(8,128)}, u32[]{:S(2)}) copy-start(f32[2,32,128]{2,1,0:T(8,128)} %constant.11.clone.twist_ref) | copy-start | bytes 98308
  24.7 17.0 %copy-start.3 = (s32[1,4096]{1,0:T(1,128)S(1)}, s32[1,4096]{1,0:T(1,128)}, u32[]{:S(2)}) copy-start(s32[1,4096]{1,0:T(1,128)} %param.20) | copy-start | bytes 49156
  24.7 17.0 %copy-start.4 = (bf16[64,64]{1,0:T(8,128)(2,1)S(1)}, bf16[64,64]{1,0:T(8,128)(2,1)}, u32[]{:S(2)}) copy-start(bf16[64,64]{1,0:T(8,128)(2,1)} %constant.10.clone.first_ref) | copy-start | bytes 24580
  24.7 17.0 %copy-start.5 = (bf16[32,128]{1,0:T(8,128)(2,1)S(1)}, bf16[32,128]{1,0:T(8,128)(2,1)}, u32[]{:S(2)}) copy-start(bf16[32,128]{1,0:T(8,128)(2,1)} %constant.14.clone.fourth_ref) | copy-start | bytes 24580
  24.7 21.1 %copy-start.6 = (s32[128]{0:T(128)S(1)}, s32[128]{0:T(128)}, u32[]{:S(2)}) copy-start(s32[128]{0:T(128)} %param.17) | copy-start | bytes 1540
  24.8 21.1 %copy-start.7 = (f32[128]{0:T(128)S(1)}, f32[128]{0:T(128)}, u32[]{:S(2)}) copy-start(f32[128]{0:T(128)} %param.18) | copy-start | bytes 1540
  24.8 21.1 %copy-start.8 = (f32[128]{0:T(128)S(1)}, f32[128]{0:T(128)}, u32[]{:S(2)}) copy-start(f32[128]{0:T(128)} %param.19) | copy-start | bytes 1540
  43.7 3.0 %collective-permute-start.1 = (bf16[64,2,128]{2,1,0:T(2,128)(2,1)S(1)}, bf16[64,2,128]{2,1,0:T(2,128)(2,1)S(1)}, u32[]{:S(2)}, u32[]{:S(2)}) collective-permute-start(bf16[64,2,128]{2,1,0:T(2,128)(2,1)S(1)} %get-tuple-element.19), channel_id=1, source_target_pairs={{0,1},{1,0},{2,3},{3,2},{4,5},{5,4},{6,7},{7,6},{8,9},{9,8},{10,11... | collective-permute-start | bytes 98312 | tf_op jit(solution)/shard_map/ppermute | solution.py:537

commit v8 on v7

--- a/solution.py
+++ b/solution.py
@@ -261,7 +261,7 @@
     fourth = np.stack([np.concatenate([c, s], 2), np.concatenate([-s, c], 2)], 1)
     fourth = fourth.reshape(2 * modes // LANES, -1)
     return (
-        np.concatenate(split(first), 1), twist.astype(np.float32), np.concatenate(split(second), 0),
+        np.concatenate(split(first), 1), twist.astype(np.float32), split(second)[0],
         np.concatenate(split(third), 0), np.concatenate(split(fourth), 1),
     )
 
@@ -319,7 +319,7 @@
         re, im = (stage[i * small : (i + 1) * small, g * LANES : (g + 1) * LANES] for i in range(2))
         twisted.append(jnp.concatenate([re * cos - im * sin, re * sin + im * cos], axis=1))
     twisted = jnp.concatenate(twisted, axis=0).astype(BF16)
-    maps = dot(twisted, second_ref[: 2 * LANES]) + dot(twisted, second_ref[2 * LANES :])
+    maps = dot(twisted, second_ref[...])
 
     mask = mask_ref[...].astype(F32).T
     mask = jnp.concatenate([mask[i * small : (i + 1) * small] for i in range(LANES // small)], axis=1)
@@ -329,7 +329,7 @@
             at = (q * sims + s) * small
             products.append(mask * maps[s * small : (s + 1) * small] * maps[at : at + small])
     products = jnp.concatenate(products, axis=0).astype(BF16)
-    stage = dot(products, third_ref[:LANES]) + dot(products, third_ref[LANES:])
+    stage = dot(across((products, products)), third_ref[...])
     groups = 2 * sims
     twisted = []
     for g in range(groups):

time: 64.6 us -> 64.4 us (level)
  no operation moved by 1% of the time
where the time goes in v8:
time: 64.4 us; the launch traced here: 64.3 us
  blocking collectives  31.5 us (49%)
  starting transfers between devices  22.7 us (35%)
  Pallas kernels  8.93 us (14%)
  between operations  0.76 us (1%)
    all_to_all x2, blocking collectives, exchange(): return lax.all_to_all(both, CHIP, 0, 0, tiled=True)  31.5 us
    ppermute x2, starting transfers between devices, exchange(): swapped = lax.ppermute(far, CORE, [(0, 1), (1, 0)])  22.7 us
    pallas_call x1, Pallas kernels, synth(): pl.pallas_call(synth_kernel, in_specs=[hbm] * 6, out_specs=[vmem] * 5, ou...  3.54 us
    pallas_call x1, Pallas kernels, analyse(): pl.pallas_call(analyse_kernel, in_specs=[vmem] * 9, out_specs=[hbm, hbm],...  2.05 us
    pallas_call x1, Pallas kernels, sky(): pl.pallas_call(functools.partial(sky_kernel, pairs, sims), in_specs=[vmem...  1.8 us
  transfers between devices with their start and end apart: 2, of which 1 were waited for; matrix products, arithmetic and copies ran while one was open for 0% of the time, Pallas kernels for 2%

profile of v8, /device:TPU:513, one launch (start us, length us, event | category | flops | bytes accessed | tf_op | source)
XLA Modules:
  0.0 64.3 jit_solution(9219611779057811195)
XLA Ops:
  0.6 3.5 %synth.1 = (bf16[64,4,128]{2,1,0:T(4,128)(2,1)S(1)}, bf16[64,4,128]{2,1,0:T(4,128)(2,1)S(1)}, bf16[8,2048,128]{2,1,0:T(8,128)(2,1)S(1)}, f32[8,128]{1,0:T(8,128)S(1)}, f32[8,128]{1,0:T(8,128)S(1)}) custom-call(s32[1024]{0:T(1024)} %m_hbm.1, s32[1,128]{1,0:T(1,128)} %bitcast.6, f32[1,128]{1,0:T(1,128)} %bitcast.8, bf16[8,4,2,2049]{3,2,1,0:T(2,128)(2,1)} %t_hbm.1, ...), custom_call_target="tpu_custom_call" | custom-call | tf_op jit(solution)/shard_map/synth/pallas_call | solution.py:202
  4.2 20.5 %collective-permute-start = (bf16[64,4,128]{2,1,0:T(4,128)(2,1)S(1)}, bf16[64,4,128]{2,1,0:T(4,128)(2,1)S(1)}, u32[]{:S(2)}, u32[]{:S(2)}) collective-permute-start(bf16[64,4,128]{2,1,0:T(4,128)(2,1)S(1)} %get-tuple-element.16), channel_id=1, source_target_pairs={{0,1},{1,0},{2,3},{3,2},{4,5},{5,4},{6,7},{7,6},{8,9},{9,8},{10,11... | collective-permute-start | bytes 196616 | tf_op jit(solution)/shard_map/ppermute | solution.py:537
  24.7 0.0 copy-start
  24.7 0.0 copy-start.1
  24.7 0.0 copy-start.2
  24.7 0.0 copy-start.3
  24.7 0.0 copy-start.4
  24.7 0.0 copy-start.5
  24.7 0.0 copy-start.6
  24.8 0.0 copy-start.7
  24.8 0.0 copy-start.8
  24.8 0.9 %flip.1.refs_0_.l_ref = bf16[6,16,128,128]{3,2,1,0:T(8,128)(2,1)S(1)} custom-call(bf16[8,2048,128]{2,1,0:T(8,128)(2,1)S(1)} %get-tuple-element.17.table_ref, bf16[64,4,128]{2,1,0:T(4,128)(2,1)S(1)} %get-tuple-element.15._.near_ref), custom_call_target="tpu_custom_call" | custom-call | flops 1000000000 | bytes 1000000 | tf_op jit(solution)/shard_map/flip/pallas_call | solution.py:436
  25.6 0.0 collective-permute-done.far_ref
  25.7 0.1 merge.2
  25.7 15.9 %all_to_all.10.x_ref = bf16[64,8,128]{2,1,0:T(8,128)(2,1)S(1)} all-to-all(bf16[64,8,128]{2,1,0:T(8,128)(2,1)S(1)} %merge.2), channel_id=1, replica_groups=mesh['grp'=2,'chip'=64,'core'=2] {'chip'}, dimensions={0} | all-to-all | bytes 262144 | tf_op jit(solution)/shard_map/all_to_all | solution.py:547
  41.7 0.0 copy-done
  41.7 0.0 copy-done.1
  41.7 0.0 copy-done.2
  41.7 0.0 copy-done.3
  41.7 0.0 copy-done.4
  41.7 0.0 copy-done.5
  41.7 1.8 %sky.1 = (bf16[64,2,128]{2,1,0:T(2,128)(2,1)S(1)}, bf16[64,2,128]{2,1,0:T(2,128)(2,1)S(1)}) custom-call(bf16[64,8,128]{2,1,0:T(8,128)(2,1)S(1)} %all_to_all.10.x_ref, s32[32,128]{1,0:T(8,128)S(1)} %bitcast.5, bf16[64,64]{1,0:T(8,128)(2,1)S(1)} %copy-done.4, f32[2,32,128]{2,1,0:T(8,128)S(1)} %copy-done.2, bf16[256,128]{1,0:T(8,128)(2,1)S(1)} %copy-done.1, ...), custom_call_target="tpu_custom_call" | custom-call | tf_op jit(solution)/shard_map/sky/pallas_call | solution.py:367
  43.5 2.2 %collective-permute-start.1 = (bf16[64,2,128]{2,1,0:T(2,128)(2,1)S(1)}, bf16[64,2,128]{2,1,0:T(2,128)(2,1)S(1)}, u32[]{:S(2)}, u32[]{:S(2)}) collective-permute-start(bf16[64,2,128]{2,1,0:T(2,128)(2,1)S(1)} %get-tuple-element.19), channel_id=1, source_target_pairs={{0,1},{1,0},{2,3},{3,2},{4,5},{5,4},{6,7},{7,6},{8,9},{9,8},{10,11... | collective-permute-start | bytes 98312 | tf_op jit(solution)/shard_map/ppermute | solution.py:537
  45.7 0.0 copy-done.6
  45.7 0.0 copy-done.7
  45.7 0.0 copy-done.8
  45.7 0.5 layout.1
  46.3 0.3 collective-permute-done.1.far_ref
  46.6 0.1 merge.3
  46.7 15.6 %all_to_all.11.r_ref = bf16[64,4,128]{2,1,0:T(4,128)(2,1)S(1)} all-to-all(bf16[64,4,128]{2,1,0:T(4,128)(2,1)S(1)} %merge.3), channel_id=1, replica_groups=mesh['grp'=2,'chip'=64,'core'=2] {'chip'}, dimensions={0} | all-to-all | bytes 131072 | tf_op jit(solution)/shard_map/all_to_all | solution.py:547
  62.2 2.0 %analyse.1 = (f32[8,4,2,2049]{3,2,1,0:T(2,128)}, f32[8,4,2,2049]{3,2,1,0:T(2,128)}) custom-call(f32[8,128]{1,0:T(8,128)S(1)} %get-tuple-element.14.small_ref, bf16[64,4,128]{2,1,0:T(4,128)(2,1)S(1)} %all_to_all.11.r_ref, bf16[6,16,128,128]{3,2,1,0:T(8,128)(2,1)S(1)} %flip.1.refs_0_.l_ref, bf16[2,16,128,128]{3,2,1,0:T(8,128)(2,1)S(1)} %get-tuple-element.21.l2_ref, ...), custom_call_target="tpu_custom_call" | custom-call | tf_op jit(solution)/shard_map/analyse/pallas_call | solution.py:512
Async XLA Ops:
  4.2 21.5 %collective-permute-start = (bf16[64,4,128]{2,1,0:T(4,128)(2,1)S(1)}, bf16[64,4,128]{2,1,0:T(4,128)(2,1)S(1)}, u32[]{:S(2)}, u32[]{:S(2)}) collective-permute-start(bf16[64,4,128]{2,1,0:T(4,128)(2,1)S(1)} %get-tuple-element.16), channel_id=1, source_target_pairs={{0,1},{1,0},{2,3},{3,2},{4,5},{5,4},{6,7},{7,6},{8,9},{9,8},{10,11... | collective-permute-start | bytes 196616 | tf_op jit(solution)/shard_map/ppermute | solution.py:537
  24.7 17.0 %copy-start = (bf16[256,256]{1,0:T(8,128)(2,1)S(1)}, bf16[256,256]{1,0:T(8,128)(2,1)}, u32[]{:S(2)}) copy-start(bf16[256,256]{1,0:T(8,128)(2,1)} %constant.13.clone.third_ref) | copy-start | bytes 393220
  24.7 17.0 %copy-start.1 = (bf16[256,128]{1,0:T(8,128)(2,1)S(1)}, bf16[256,128]{1,0:T(8,128)(2,1)}, u32[]{:S(2)}) copy-start(bf16[256,128]{1,0:T(8,128)(2,1)} %constant.12.clone.second_ref) | copy-start | bytes 196612
  24.7 17.0 %copy-start.2 = (f32[2,32,128]{2,1,0:T(8,128)S(1)}, f32[2,32,128]{2,1,0:T(8,128)}, u32[]{:S(2)}) copy-start(f32[2,32,128]{2,1,0:T(8,128)} %constant.11.clone.twist_ref) | copy-start | bytes 98308
  24.7 17.0 %copy-start.3 = (s32[1,4096]{1,0:T(1,128)S(1)}, s32[1,4096]{1,0:T(1,128)}, u32[]{:S(2)}) copy-start(s32[1,4096]{1,0:T(1,128)} %param.20) | copy-start | bytes 49156
  24.7 17.0 %copy-start.4 = (bf16[64,64]{1,0:T(8,128)(2,1)S(1)}, bf16[64,64]{1,0:T(8,128)(2,1)}, u32[]{:S(2)}) copy-start(bf16[64,64]{1,0:T(8,128)(2,1)} %constant.10.clone.first_ref) | copy-start | bytes 24580
  24.7 17.0 %copy-start.5 = (bf16[32,128]{1,0:T(8,128)(2,1)S(1)}, bf16[32,128]{1,0:T(8,128)(2,1)}, u32[]{:S(2)}) copy-start(bf16[32,128]{1,0:T(8,128)(2,1)} %constant.14.clone.fourth_ref) | copy-start | bytes 24580
  24.7 21.0 %copy-start.6 = (s32[128]{0:T(128)S(1)}, s32[128]{0:T(128)}, u32[]{:S(2)}) copy-start(s32[128]{0:T(128)} %param.17) | copy-start | bytes 1540
  24.8 21.0 %copy-start.7 = (f32[128]{0:T(128)S(1)}, f32[128]{0:T(128)}, u32[]{:S(2)}) copy-start(f32[128]{0:T(128)} %param.18) | copy-start | bytes 1540
  24.8 21.0 %copy-start.8 = (f32[128]{0:T(128)S(1)}, f32[128]{0:T(128)}, u32[]{:S(2)}) copy-start(f32[128]{0:T(128)} %param.19) | copy-start | bytes 1540
  43.5 3.0 %collective-permute-start.1 = (bf16[64,2,128]{2,1,0:T(2,128)(2,1)S(1)}, bf16[64,2,128]{2,1,0:T(2,128)(2,1)S(1)}, u32[]{:S(2)}, u32[]{:S(2)}) collective-permute-start(bf16[64,2,128]{2,1,0:T(2,128)(2,1)S(1)} %get-tuple-element.19), channel_id=1, source_target_pairs={{0,1},{1,0},{2,3},{3,2},{4,5},{5,4},{6,7},{7,6},{8,9},{9,8},{10,11... | collective-permute-start | bytes 98312 | tf_op jit(solution)/shard_map/ppermute | solution.py:537
